TPU v7x, 8 devices: a whole 2x2x1 slice. The times are simulated.
8 devices in a mesh: data: 1 (over z), ys: 2 (over y), xs: 4 (over x, core).
Axes of the slice: x: 2, y: 2, z: 1, core: 2. Of those that a mesh axis runs over, the one named last changes fastest.
Arguments:
- field: float32 [48, 64, 64, 40, 20], P('data', 'xs', 'ys')
- spec_real: float32 [2, 16, 16, 8, 20, 20], replicated
- spec_imag: float32 [2, 16, 16, 8, 20, 20], replicated
- mix_weight: float32 [2, 20, 20], replicated
- bias: float32 [2, 20], replicated
Outputs:
- output: float32 [48, 64, 64, 40, 20], P('data', 'xs', 'ys')
All inputs are finite; a program needn't handle non-finite values.
Results may differ from a plain program's by a relative error of at most 0.001.
Values are sent between devices in bfloat16 or wider.
A program may use at most 1 GiB of HBM per device.

v0:
```python
import math
import jax
import jax.numpy as jnp
from jax import lax
from jax.sharding import PartitionSpec as P

EXACT_DOT = lax.Precision.HIGHEST


def kept_freqs(count, size):
    slots = jnp.arange(2 * count, dtype=jnp.int32)
    return jnp.where(slots < count, slots, slots + (size - 2 * count))


def phase_block(rows, cols, size, sign):
    angle = ((rows[:, None] * cols[None, :]) % size).astype(jnp.float32) * (2.0 * math.pi / size)
    cosine = jnp.cos(angle)
    sine = sign * jnp.sin(angle)
    return jnp.stack([jnp.stack([cosine, sine], axis=1), jnp.stack([-sine, cosine], axis=1)], axis=0)


def contract(form, left, right):
    return jnp.einsum(form, left, right, precision=EXACT_DOT, preferred_element_type=jnp.float32)


def solution(mesh):
    row_devs = mesh.shape['ys']
    col_devs = mesh.shape['xs']

    def local_layers(field, spec_real, spec_imag, mix_weight, bias):
        batch, x_loc, y_loc, grid_z, width = field.shape
        modes = spec_real.shape[3]
        grid_x = x_loc * col_devs
        grid_y = y_loc * row_devs
        yz_modes = 2 * modes * modes
        yz_local = yz_modes // row_devs
        mode_local = 2 * modes * yz_local // col_devs
        x_index = lax.axis_index('xs')
        y_index = lax.axis_index('ys')
        x_pos = x_index * x_loc + jnp.arange(x_loc, dtype=jnp.int32)
        y_pos = y_index * y_loc + jnp.arange(y_loc, dtype=jnp.int32)
        z_pos = jnp.arange(grid_z, dtype=jnp.int32)
        kx_freq = kept_freqs(modes, grid_x)
        ky_freq = kept_freqs(modes, grid_y)
        kz_freq = jnp.arange(modes, dtype=jnp.int32)
        fwd_z = phase_block(z_pos, kz_freq, grid_z, -1.0)[0]
        fwd_y = phase_block(y_pos, ky_freq, grid_y, -1.0)
        fwd_x = phase_block(x_pos, kx_freq, grid_x, -1.0)
        inv_x = phase_block(kx_freq, x_pos, grid_x, 1.0)
        inv_y = phase_block(ky_freq, y_pos, grid_y, 1.0)
        z_weight = jnp.where(kz_freq == 0, 1.0, 2.0) / (grid_x * grid_y * grid_z)
        inv_z = phase_block(kz_freq, z_pos, grid_z, 1.0)[:, :, 0, :] * z_weight[None, :, None]
        for layer in range(spec_real.shape[0]):
            along_z = contract('bxyzc,zpk->pbxykc', field, fwd_z)
            along_y = contract('pbxykc,pyqj->qbxjkc', along_z, fwd_y)
            along_y = lax.psum_scatter(along_y.reshape(2, batch, x_loc, yz_modes, width), 'ys', scatter_dimension=3, tiled=True)
            along_x = contract('pbxmc,pxqj->qbjmc', along_y, fwd_x)
            spectrum = lax.psum_scatter(along_x.reshape(2, batch, 2 * modes * yz_local, width), 'xs', scatter_dimension=2, tiled=True)
            real_w = lax.dynamic_slice_in_dim(spec_real[layer].reshape(2 * modes, yz_modes, width, width), y_index * yz_local, yz_local, axis=1)
            real_w = lax.dynamic_slice_in_dim(real_w.reshape(2 * modes * yz_local, width, width), x_index * mode_local, mode_local, axis=0)
            imag_w = lax.dynamic_slice_in_dim(spec_imag[layer].reshape(2 * modes, yz_modes, width, width), y_index * yz_local, yz_local, axis=1)
            imag_w = lax.dynamic_slice_in_dim(imag_w.reshape(2 * modes * yz_local, width, width), x_index * mode_local, mode_local, axis=0)
            real_mix = contract('pbqi,qio->pbqo', spectrum, real_w)
            imag_mix = contract('pbqi,qio->pbqo', spectrum, imag_w)
            mixed = jnp.stack([real_mix[0] - imag_mix[1], imag_mix[0] + real_mix[1]], axis=0)
            mixed = lax.all_gather(mixed, 'xs', axis=2, tiled=True).reshape(2, batch, 2 * modes, yz_local, width)
            back_x = contract('pbjmc,pjqx->qbxmc', mixed, inv_x)
            back_x = lax.all_gather(back_x, 'ys', axis=3, tiled=True).reshape(2, batch, x_loc, 2 * modes, modes, width)
            back_y = contract('pbxjkc,pjqy->qbxykc', back_x, inv_y)
            spectral = contract('pbxykc,pkz->bxyzc', back_y, inv_z)
            pointwise = jnp.dot(field, mix_weight[layer], precision=EXACT_DOT, preferred_element_type=jnp.float32)
            field = jax.nn.gelu(spectral + pointwise + bias[layer], approximate=True)
        return field

    field_spec = P('data', 'xs', 'ys', None, None)
    return jax.shard_map(local_layers, mesh=mesh, in_specs=(field_spec, P(), P(), P(), P()), out_specs=field_spec, check_vma=False)
```

profile of v0, /device:TPU:0, one launch (start us, length us, event | category | flops | bytes accessed | tf_op | source)
XLA Modules:
  0.0 3900.3 jit_solution(18168963838235721688)
XLA Ops:
  7.4 119.5 %fusion.38 = f32[2,48,16,32,8,20]{1,4,5,3,2,0:T(8,128)} fusion(f32[48,16,32,40,20]{0,3,4,2,1:T(8,128)} %param.5, f32[40,1,8]{0,2,1:T(8,128)S(1)} %get-tuple-element.39, f32[40,1,8]{0,2,1:T(8,128)S(1)} %get-tuple-element.40), kind=kOutput, calls=%fused_computation.44 | convolution fusion | flops 3774874112 | bytes 110103040 | tf_op jit(solution)/shard_map/bxyzc,zpk->pbxykc/dot_general | solution.py:23
  126.9 110.2 %fusion.50 = f32[2,48,16,16,8,20]{1,3,5,4,2,0:T(8,128)} fusion(f32[2,48,16,32,8,20]{1,4,5,3,2,0:T(8,128)} %fusion.38, f32[1,32,2,16]{1,3,0,2:T(8,128)S(1)} %get-tuple-element.22, f32[1,32,2,16]{1,3,0,2:T(8,128)S(1)} %get-tuple-element.21), kind=kOutput, calls=%fused_computation.52 | convolution fusion | flops 3019900928 | bytes 47194112 | tf_op jit(solution)/shard_map/pbxykc,pyqj->qbxjkc/dot_general | solution.py:23
  237.1 45.6 %copy.184 = f32[2,48,16,16,8,20]{1,4,3,5,2,0:T(8,128)} copy(f32[2,48,16,16,8,20]{1,3,5,4,2,0:T(8,128)} %fusion.50) | data formatting | bytes 31457280 | tf_op jit(solution)/shard_map/pbxykc,pyqj->qbxjkc/transpose | solution.py:23
  284.2 457.7 %reduce-scatter.5.cloned.1.call-done = f32[2,48,16,64,20]{1,3,4,2,0:T(8,128)} async-done(((f32[2,48,16,128,20]{1,3,4,2,0:T(8,128)}), f32[2,48,16,64,20]{1,3,4,2,0:T(8,128)}) %reduce-scatter.5.cloned.1.call-update) | async-done | bytes 7864336 | tf_op jit(solution)/shard_map/reduce_scatter | solution.py:56
  741.9 20.0 copy.64
  761.8 20.8 fusion.60
  809.0 22.7 fusion.151
  831.7 16.4 copy.186
  855.9 15.9 constant_dynamic-slice_fusion.2
  885.0 22.6 fusion.150
  907.6 21.8 copy_bitcast_fusion.2
  989.1 49.8 %all-gather.5.cloned.1.call-done = f32[2,48,1024,20]{2,1,3,0:T(8,128)} async-done(((f32[2,48,256,20]{2,1,3,0:T(8,128)}), f32[2,48,1024,20]{2,1,3,0:T(8,128)}) %all-gather.5.cloned.1.call-update) | async-done | bytes 7864336 | tf_op jit(solution)/shard_map/all_gather | solution.py:66
  1066.5 20.8 convolution_bitcast_fusion.1
  1087.3 20.5 copy.74
  1107.9 297.6 %fusion.2 = f32[48,16,32,40,20]{0,4,3,2,1:T(8,128)} fusion(f32[48,16,32,40,20]{0,3,4,2,1:T(8,128)} %param.5, f32[1,20,20]{1,2,0:T(8,128)S(1)} %copy.133), kind=kOutput, calls=%fused_computation.4 | convolution fusion | flops 4718592000 | bytes 157288000 | tf_op jit(solution)/shard_map/dot_general | solution.py:71
  1405.4 182.4 %all-gather.7.cloned.1.call-done = f32[2,48,16,128,20]{1,2,4,0,3:T(8,128)} async-done(((f32[2,48,16,64,20]{1,2,4,0,3:T(8,128)}), f32[2,48,16,128,20]{1,2,4,0,3:T(8,128)}) %all-gather.7.cloned.1.call-update) | async-done | bytes 15728656 | tf_op jit(solution)/shard_map/all_gather | solution.py:68
  1587.9 103.3 %fusion.44 = f32[2,48,16,32,8,20]{1,3,5,4,2,0:T(8,128)} fusion(f32[2,48,16,16,8,20]{1,2,5,0,4,3:T(8,128)} %bitcast.300, f32[2,16,2,32,1,1,1]{3,1,0,6,5,4,2:T(8,128)S(1)} %copy-done.16), kind=kOutput, calls=%fused_computation.46 | convolution fusion | flops 3019898880 | bytes 47194112 | tf_op jit(solution)/shard_map/pbxjkc,pjqy->qbxykc/dot_general | solution.py:23
  1691.2 301.1 %fusion.10 = f32[48,16,32,40,20]{0,3,4,2,1:T(8,128)} fusion(f32[48,16,32,40,20]{0,4,3,2,1:T(8,128)} %fusion.2, f32[20]{0:T(128)S(1)} %copy-done.43, f32[2,48,16,32,8,20]{1,3,5,4,2,0:T(8,128)} %fusion.44, f32[2,8,40,1,1,1]{2,1,0,5,4,3:T(8,128)S(1)} %copy-done.32), kind=kOutput, calls=%fused_computation.12 | convolution fusion | flops 3971481600 | bytes 188746320 | tf_op jit(solution)/shard_map/pbxykc,pkz->bxyzc/dot_general | solution.py:23
  1992.4 119.4 %fusion.41 = f32[2,48,16,32,8,20]{1,4,5,3,2,0:T(8,128)} fusion(f32[48,16,32,40,20]{0,3,4,2,1:T(8,128)} %fusion.10, f32[40,1,8]{0,2,1:T(8,128)S(1)} %copy-done.24, f32[40,1,8]{0,2,1:T(8,128)S(1)} %copy-done.26), kind=kOutput, calls=%fused_computation.45 | convolution fusion | flops 3774874112 | bytes 110103040 | tf_op jit(solution)/shard_map/bxyzc,zpk->pbxykc/dot_general | solution.py:23
  2111.8 110.2 %fusion.53 = f32[2,48,16,16,8,20]{1,3,5,4,2,0:T(8,128)} fusion(f32[2,48,16,32,8,20]{1,4,5,3,2,0:T(8,128)} %fusion.41, f32[1,32,2,16]{1,3,0,2:T(8,128)S(1)} %copy-done.3, f32[1,32,2,16]{1,3,0,2:T(8,128)S(1)} %copy-done.1), kind=kOutput, calls=%fused_computation.53 | convolution fusion | flops 3019900928 | bytes 47194112 | tf_op jit(solution)/shard_map/pbxykc,pyqj->qbxjkc/dot_general | solution.py:23
  2222.0 45.7 %copy.183 = f32[2,48,16,16,8,20]{1,4,3,5,2,0:T(8,128)} copy(f32[2,48,16,16,8,20]{1,3,5,4,2,0:T(8,128)} %fusion.53) | data formatting | bytes 31457280 | tf_op jit(solution)/shard_map/pbxykc,pyqj->qbxjkc/transpose | solution.py:23
  2267.8 456.2 %reduce-scatter.9.cloned.1.call-done = f32[2,48,16,64,20]{1,3,4,2,0:T(8,128)} async-done(((f32[2,48,16,128,20]{1,3,4,2,0:T(8,128)}), f32[2,48,16,64,20]{1,3,4,2,0:T(8,128)}) %reduce-scatter.9.cloned.1.call-update) | async-done | bytes 7864336 | tf_op jit(solution)/shard_map/reduce_scatter | solution.py:56
  2724.0 20.1 copy.83
  2744.1 20.9 fusion.63
  2827.6 24.7 reduce-scatter.11.cloned.1.call-done
  2887.2 51.2 %all-gather.9.cloned.1.call-done = f32[2,48,1024,20]{2,1,3,0:T(8,128)} async-done(((f32[2,48,256,20]{2,1,3,0:T(8,128)}), f32[2,48,1024,20]{2,1,3,0:T(8,128)}) %all-gather.9.cloned.1.call-update) | async-done | bytes 7864336 | tf_op jit(solution)/shard_map/all_gather | solution.py:66
  2966.2 20.9 convolution_bitcast_fusion
  2987.1 20.5 copy.93
  3007.7 297.3 %fusion = f32[48,16,32,40,20]{0,4,3,2,1:T(8,128)} fusion(f32[48,16,32,40,20]{0,3,4,2,1:T(8,128)} %fusion.10, f32[1,20,20]{1,2,0:T(8,128)S(1)} %copy.134), kind=kOutput, calls=%fused_computation.2 | convolution fusion | flops 4718592000 | bytes 157288000 | tf_op jit(solution)/shard_map/dot_general | solution.py:71
  3305.0 182.7 %all-gather.11.cloned.1.call-done = f32[2,48,16,128,20]{1,2,4,0,3:T(8,128)} async-done(((f32[2,48,16,64,20]{1,2,4,0,3:T(8,128)}), f32[2,48,16,128,20]{1,2,4,0,3:T(8,128)}) %all-gather.11.cloned.1.call-update) | async-done | bytes 15728656 | tf_op jit(solution)/shard_map/all_gather | solution.py:68
  3487.8 103.3 %fusion.47 = f32[2,48,16,32,8,20]{1,3,5,4,2,0:T(8,128)} fusion(f32[2,48,16,16,8,20]{1,2,5,0,4,3:T(8,128)} %bitcast.301, f32[2,16,2,32,1,1,1]{3,1,0,6,5,4,2:T(8,128)S(1)} %copy-done.17), kind=kOutput, calls=%fused_computation.47 | convolution fusion | flops 3019898880 | bytes 47194112 | tf_op jit(solution)/shard_map/pbxjkc,pjqy->qbxykc/dot_general | solution.py:23
  3591.1 301.9 %fusion.17 = f32[48,16,32,40,20]{0,3,4,2,1:T(8,128)} fusion(f32[48,16,32,40,20]{0,4,3,2,1:T(8,128)} %fusion, f32[20]{0:T(128)S(1)} %copy-done.42, f32[2,48,16,32,8,20]{1,3,5,4,2,0:T(8,128)} %fusion.47, f32[2,8,40,1,1,1]{2,1,0,5,4,3:T(8,128)S(1)} %copy-done.31), kind=kOutput, calls=%fused_computation.19 | convolution fusion | flops 3971481600 | bytes 188746320 | tf_op jit(solution)/shard_map/pbxykc,pkz->bxyzc/dot_general | solution.py:23
  (156 shorter events, 261.9 us)
Async XLA Ops:
  6.5 735.3 %reduce-scatter.5.cloned.1.call-start = ((), (), s32[]{:S(2)}) async-start(), calls=%async_computation.4 | async-start | bytes 62914560 | tf_op jit(solution)/shard_map/reduce_scatter | solution.py:56
  6.6 120.3 %copy-start.23 = (f32[40,1,8]{0,2,1:T(8,128)}, f32[40,1,8]{0,2,1:T(8,128)S(1)}, u32[]{:S(2)}) copy-start(f32[40,1,8]{0,2,1:T(8,128)S(1)} %get-tuple-element.39) | copy-start | bytes 3844
  6.6 120.3 %copy-start.25 = (f32[40,1,8]{0,2,1:T(8,128)}, f32[40,1,8]{0,2,1:T(8,128)S(1)}, u32[]{:S(2)}) copy-start(f32[40,1,8]{0,2,1:T(8,128)S(1)} %get-tuple-element.40) | copy-start | bytes 3844
  6.6 120.3 %copy-start.36 = (s32[32]{0:T(128)}, s32[32]{0:T(128)S(1)}, u32[]{:S(2)}) copy-start(s32[32]{0:T(128)S(1)} %iota_add_fusion.1) | copy-start | bytes 388
  7.2 119.7 %copy-start.33 = (s32[16]{0:T(128)}, s32[16]{0:T(128)S(1)}, u32[]{:S(2)}) copy-start(s32[16]{0:T(128)S(1)} %get-tuple-element.41) | copy-start | bytes 196
  7.4 119.6 %copy-start = (f32[1,32,2,16]{1,3,0,2:T(8,128)}, f32[1,32,2,16]{1,3,0,2:T(8,128)S(1)}, u32[]{:S(2)}) copy-start(f32[1,32,2,16]{1,3,0,2:T(8,128)S(1)} %get-tuple-element.21) | copy-start | bytes 12292
  7.4 119.6 %copy-start.2 = (f32[1,32,2,16]{1,3,0,2:T(8,128)}, f32[1,32,2,16]{1,3,0,2:T(8,128)S(1)}, u32[]{:S(2)}) copy-start(f32[1,32,2,16]{1,3,0,2:T(8,128)S(1)} %get-tuple-element.22) | copy-start | bytes 12292
  282.8 669.9 %reduce-scatter.7.cloned.1.call-start = ((), (), s32[]{:S(2)}) async-start(), calls=%async_computation.5 | async-start | bytes 9830400 | tf_op jit(solution)/shard_map/reduce_scatter | solution.py:58
  284.2 498.5 %copy-start.4 = (f32[1,16,2,16]{1,3,0,2:T(8,128)}, f32[1,16,2,16]{1,3,0,2:T(8,128)S(1)}, u32[]{:S(2)}) copy-start(f32[1,16,2,16]{1,3,0,2:T(8,128)S(1)} %get-tuple-element.19) | copy-start | bytes 6148
  284.2 498.5 %copy-start.6 = (f32[1,16,2,16]{1,3,0,2:T(8,128)}, f32[1,16,2,16]{1,3,0,2:T(8,128)S(1)}, u32[]{:S(2)}) copy-start(f32[1,16,2,16]{1,3,0,2:T(8,128)S(1)} %get-tuple-element.20) | copy-start | bytes 6148
  808.9 230.0 %all-gather.5.cloned.1.call-start = ((), (), s32[]{:S(2)}) async-start(), calls=%async_computation.6 | async-start | bytes 9830400 | tf_op jit(solution)/shard_map/all_gather | solution.py:66
  986.0 601.8 %all-gather.7.cloned.1.call-start = ((), (), s32[]{:S(2)}) async-start(), calls=%async_computation.7 | async-start | bytes 62914560 | tf_op jit(solution)/shard_map/all_gather | solution.py:68
  986.8 100.5 %copy-start.38 = (f32[8]{0:T(128)}, f32[8]{0:T(128)S(1)}, u32[]{:S(2)}) copy-start(f32[8]{0:T(128)S(1)} %fusion.139) | copy-start | bytes 100
  987.8 99.5 %copy-start.8 = (f32[1,16,2,16]{1,3,2,0:T(8,128)}, f32[1,16,2,16]{1,3,2,0:T(8,128)S(1)}, u32[]{:S(2)}) copy-start(f32[1,16,2,16]{1,3,2,0:T(8,128)S(1)} %get-tuple-element.17) | copy-start | bytes 6148
  987.8 99.5 %copy-start.10 = (f32[1,16,2,16]{1,3,2,0:T(8,128)}, f32[1,16,2,16]{1,3,2,0:T(8,128)S(1)}, u32[]{:S(2)}) copy-start(f32[1,16,2,16]{1,3,2,0:T(8,128)S(1)} %get-tuple-element.18) | copy-start | bytes 6148
  1107.8 1616.2 %reduce-scatter.9.cloned.1.call-start = ((), (), s32[]{:S(2)}) async-start(), calls=%async_computation.8 | async-start | bytes 62914560 | tf_op jit(solution)/shard_map/reduce_scatter | solution.py:56
  1107.9 480.0 %copy-start.16 = (f32[2,16,2,32,1,1,1]{3,1,0,6,5,4,2:T(8,128)S(1)}, f32[2,16,2,32,1,1,1]{3,1,0,6,5,4,2:T(8,128)}, u32[]{:S(2)}) copy-start(f32[2,16,2,32,1,1,1]{3,1,0,6,5,4,2:T(8,128)} %maximum_bitcast_fusion.33) | copy-start | bytes 24580
  1587.9 103.3 %copy-start.32 = (f32[2,8,40,1,1,1]{2,1,0,5,4,3:T(8,128)S(1)}, f32[2,8,40,1,1,1]{2,1,0,5,4,3:T(8,128)}, u32[]{:S(2)}) copy-start(f32[2,8,40,1,1,1]{2,1,0,5,4,3:T(8,128)} %fusion.165) | copy-start | bytes 7684
  1587.9 103.3 %copy-start.43 = (f32[20]{0:T(128)S(1)}, f32[20]{0:T(128)}, u32[]{:S(2)}) copy-start(f32[20]{0:T(128)} %get-tuple-element.26) | copy-start | bytes 244
  1691.2 301.1 %copy-start.24 = (f32[40,1,8]{0,2,1:T(8,128)S(1)}, f32[40,1,8]{0,2,1:T(8,128)}, u32[]{:S(2)}) copy-start(f32[40,1,8]{0,2,1:T(8,128)} %copy-done.23) | copy-start | bytes 3844
  1691.2 301.1 %copy-start.26 = (f32[40,1,8]{0,2,1:T(8,128)S(1)}, f32[40,1,8]{0,2,1:T(8,128)}, u32[]{:S(2)}) copy-start(f32[40,1,8]{0,2,1:T(8,128)} %copy-done.25) | copy-start | bytes 3844
  1992.4 119.4 %copy-start.1 = (f32[1,32,2,16]{1,3,0,2:T(8,128)S(1)}, f32[1,32,2,16]{1,3,0,2:T(8,128)}, u32[]{:S(2)}) copy-start(f32[1,32,2,16]{1,3,0,2:T(8,128)} %copy-done) | copy-start | bytes 12292
  1992.4 119.4 %copy-start.3 = (f32[1,32,2,16]{1,3,0,2:T(8,128)S(1)}, f32[1,32,2,16]{1,3,0,2:T(8,128)}, u32[]{:S(2)}) copy-start(f32[1,32,2,16]{1,3,0,2:T(8,128)} %copy-done.2) | copy-start | bytes 12292
  2267.7 476.3 %copy-start.5 = (f32[1,16,2,16]{1,3,0,2:T(8,128)S(1)}, f32[1,16,2,16]{1,3,0,2:T(8,128)}, u32[]{:S(2)}) copy-start(f32[1,16,2,16]{1,3,0,2:T(8,128)} %copy-done.4) | copy-start | bytes 6148
  2267.8 476.3 %copy-start.7 = (f32[1,16,2,16]{1,3,0,2:T(8,128)S(1)}, f32[1,16,2,16]{1,3,0,2:T(8,128)}, u32[]{:S(2)}) copy-start(f32[1,16,2,16]{1,3,0,2:T(8,128)} %copy-done.6) | copy-start | bytes 6148
  2267.8 584.5 %reduce-scatter.11.cloned.1.call-start = ((), (), s32[]{:S(2)}) async-start(), calls=%async_computation.9 | async-start | bytes 9830400 | tf_op jit(solution)/shard_map/reduce_scatter | solution.py:58
  2791.1 147.4 %all-gather.9.cloned.1.call-start = ((), (), s32[]{:S(2)}) async-start(), calls=%async_computation.10 | async-start | bytes 9830400 | tf_op jit(solution)/shard_map/all_gather | solution.py:66
  2885.6 80.6 %copy-start.11 = (f32[1,16,2,16]{1,3,2,0:T(8,128)S(1)}, f32[1,16,2,16]{1,3,2,0:T(8,128)}, u32[]{:S(2)}) copy-start(f32[1,16,2,16]{1,3,2,0:T(8,128)} %copy-done.10) | copy-start | bytes 6148
  2885.6 602.2 %all-gather.11.cloned.1.call-start = ((), (), s32[]{:S(2)}) async-start(), calls=%async_computation.11 | async-start | bytes 62914560 | tf_op jit(solution)/shard_map/all_gather | solution.py:68
  3007.7 480.1 %copy-start.17 = (f32[2,16,2,32,1,1,1]{3,1,0,6,5,4,2:T(8,128)S(1)}, f32[2,16,2,32,1,1,1]{3,1,0,6,5,4,2:T(8,128)}, u32[]{:S(2)}) copy-start(f32[2,16,2,32,1,1,1]{3,1,0,6,5,4,2:T(8,128)} %maximum_bitcast_fusion.34) | copy-start | bytes 24580
  3487.8 103.3 %copy-start.31 = (f32[2,8,40,1,1,1]{2,1,0,5,4,3:T(8,128)S(1)}, f32[2,8,40,1,1,1]{2,1,0,5,4,3:T(8,128)}, u32[]{:S(2)}) copy-start(f32[2,8,40,1,1,1]{2,1,0,5,4,3:T(8,128)} %fusion.167) | copy-start | bytes 7684
  3487.8 103.3 %copy-start.42 = (f32[20]{0:T(128)S(1)}, f32[20]{0:T(128)}, u32[]{:S(2)}) copy-start(f32[20]{0:T(128)} %get-tuple-element.25) | copy-start | bytes 244
  (20 other events, 341.2 us)
Sparse Core Ops, SparseCore 0:
  282.9 458.9 reduce-scatter.4
  809.0 61.0 reduce-scatter.6
  986.2 52.6 all-gather.4
  1107.9 479.9 all-gather.6
  2267.9 456.1 reduce-scatter.8
  2791.2 61.0 reduce-scatter.10
  2885.7 52.6 all-gather.8
  3007.8 479.9 all-gather.10
where the time goes:
time: 3910 us; the launch traced here: 3900 us
  matrix products  1980 us (51%)
  waiting for transfers between devices  1400 us (36%)
  local copies, waits for them, and re-layouts  485 us (12%)
    dot_general x16, matrix products, contract(): jnp.einsum(form, left, right, precision=EXACT_DOT, preferred_element_type...  1390 us
    reduce_scatter x2, waiting for transfers between devices, local_layers(): lax.psum_scatter(along_y.reshape(2, batch, x_loc, yz_modes, width), 'ys',...  914 us
    dot_general x2, matrix products, local_layers(): jnp.dot(field, mix_weight[layer], precision=EXACT_DOT, preferred_element_...  595 us
    all_gather x2, waiting for transfers between devices, local_layers(): lax.all_gather(back_x, 'ys', axis=3, tiled=True)  365 us
    transpose x4, local copies, waits for them, and re-layouts, contract(): jnp.einsum(form, left, right, precision=EXACT_DOT, preferred_element_type...  132 us
    all_gather x2, waiting for transfers between devices, local_layers(): lax.all_gather(mixed, 'xs', axis=2, tiled=True)  101 us
  transfers between devices with their start and end apart: 8, of which 7 were waited for; matrix products, arithmetic and copies ran while one was open for 20% of the time, Pallas kernels for 0%

commit v1 on v0

v1 whole, which is shorter than its diff:
```python
import functools
import math

import jax
import jax.numpy as jnp
import ml_dtypes
import numpy as np
from jax import lax
from jax.experimental import pallas as pl
from jax.experimental.pallas import tpu as pltpu
from jax.sharding import PartitionSpec as P

F32 = jnp.float32
BF16 = jnp.bfloat16
VMEM_LIMIT = 64 * 1024 * 1024 - 65536

X_GROUP = 8
Y_BLOCK = 4
Z_BLOCK = 8
KZ_CLASS = ((0, 5), (1, 6, 4), (2, 7, 3))
KZ_ORDER = tuple(kz for group in KZ_CLASS for kz in group)
CLASS_ROWS = (0, 64, 160, 256)
ROOT5_4 = math.sqrt(5.0) / 4.0
SIN_1 = math.sin(2.0 * math.pi / 5.0)
SIN_RATIO = math.sin(4.0 * math.pi / 5.0) / SIN_1


def kz_sign(kz):
    return 0 if kz % 5 == 0 else (1 if kz % 5 < 3 else -1)


def kept(modes, size):
    return np.concatenate([np.arange(modes), np.arange(size - modes, size)])


def pieces(table):
    rest = np.asarray(table, np.float32)
    out = []
    for _ in range(3):
        out.append(rest.astype(ml_dtypes.bfloat16))
        rest = rest - out[-1].astype(np.float32)
    return out


def yz_angles(kz, y_pos, ky, grid_y, grid_z):
    z_pos = np.arange(Z_BLOCK)
    turn = (ky[:, None, None] * y_pos[None, :, None] % grid_y) / grid_y + kz * z_pos[None, None, :] / grid_z
    return 2.0 * math.pi * turn


def forward_table(group, y_pos, ky, grid_y, grid_z):
    rows = []
    for kz in group:
        t, s = yz_angles(kz, y_pos, ky, grid_y, grid_z), kz_sign(kz)
        real, imag = [np.cos(t)], [-np.sin(t)]
        if s:
            real.append(-s * SIN_1 * np.sin(t))
            imag.append(-s * SIN_1 * np.cos(t))
        rows += [np.stack(part, 1).reshape(len(ky), -1) for part in (real, imag)]
    return np.concatenate(rows, 0)


def inverse_table(group, y_pos, ky, grid_y, grid_z, points):
    cols = []
    for kz in group:
        t, s = yz_angles(kz, y_pos, ky, grid_y, grid_z).transpose(1, 2, 0), kz_sign(kz)
        w = (1.0 if kz == 0 else 2.0) / points
        real, imag = [w * np.cos(t)], [-w * np.sin(t)]
        if s:
            real.append(s * SIN_1 * w * np.sin(t))
            imag.append(s * SIN_1 * w * np.cos(t))
        cols += [np.stack(part, 0).reshape(-1, len(ky)) for part in (real, imag)]
    return np.concatenate(cols, 1)


def all_tables(blocks, ky, grid_y, grid_z, points):
    fwd, inv = [[], [], []], [[], [], [], [], []]
    for block in range(blocks):
        y_pos = np.arange(Y_BLOCK) + block * Y_BLOCK
        for k, group in enumerate(KZ_CLASS):
            a, b, c = pieces(forward_table(group, y_pos, ky, grid_y, grid_z))
            n = np.zeros_like(a)
            if k == 0:
                fwd[k].append(np.concatenate([a, a, a, b, b, c], 1))
            else:
                fwd[k].append(np.block([[a, a, a, b], [c, b, n, n]]))
            a, b, c = pieces(inverse_table(group, y_pos, ky, grid_y, grid_z, points))
            n = np.zeros_like(a)
            if k == 0:
                inv[0].append(np.block([[a, a, a], [b, b, n], [c, n, n]]))
            else:
                inv[2 * k - 1].append(np.block([[a, a], [b, b]]))
                inv[2 * k].append(np.concatenate([c, a], 1))
    return [np.stack(t) for t in fwd], [np.stack(t) for t in inv]


def split3(v):
    d1 = v.astype(BF16)
    rest = v - d1.astype(F32)
    d2 = rest.astype(BF16)
    return d1, d2, (rest - d2.astype(F32)).astype(BF16)


def dot(a, b):
    return jnp.dot(a, b, preferred_element_type=F32)


def z_forward(v):
    v0, v1, v2, v3, v4 = v
    t1, t2, e1, e2 = v1 + v4, v2 + v3, v1 - v4, v2 - v3
    total = t1 + t2
    mid, dif = v0 - 0.25 * total, ROOT5_4 * (t1 - t2)
    return v0 + total, mid + dif, e1 + SIN_RATIO * e2, mid - dif, SIN_RATIO * e1 - e2


def z_inverse(a0, a1, b1, a2, b2):
    total = a1 + a2
    mid, dif = a0 - 0.25 * total, ROOT5_4 * (a1 - a2)
    p, q = mid + dif, mid - dif
    r, s = b1 + SIN_RATIO * b2, SIN_RATIO * b1 - b2
    return a0 + total, p - r, q - s, q + s, p + r


def forward_yz(v, tables):
    lanes = v[0].shape[-1]
    chan = [split3(c.reshape(Y_BLOCK * Z_BLOCK, lanes)) for c in z_forward(v)]
    outs = [dot(tables[0], jnp.concatenate([chan[0][i] for i in (0, 1, 2, 0, 1, 0)], 0))]
    for k, (p, q) in ((1, (1, 2)), (2, (3, 4))):
        o = dot(tables[k], jnp.concatenate([chan[c][i] for i in (0, 1, 2, 0) for c in (p, q)], 0))
        half = o.shape[0] // 2
        outs.append(o[:half] + o[half:])
    return outs


def inverse_yz(part, tables):
    n = Y_BLOCK * Z_BLOCK
    o = dot(tables[0], jnp.concatenate([part(i, 0) for i in range(3)], 0))
    chan = [o[:n] + o[n:2 * n] + o[2 * n:]]
    for k in (1, 2):
        d1, d2, d3 = (part(i, k) for i in range(3))
        o = dot(tables[2 * k - 1], jnp.concatenate([d1, d2], 0))
        o = o[:2 * n] + o[2 * n:] + dot(tables[2 * k], jnp.concatenate([d1, d3], 0))
        chan += [o[:n], o[n:]]
    return chan


def gelu(u):
    k = math.sqrt(2.0 / math.pi)
    h = 0.5 * u
    return h + h * jnp.tanh(u * (k + (0.044715 * k) * (u * u)))


def field_lanes(x_ref, y, c):
    return jnp.concatenate([x_ref[x, y, c] for x in range(X_GROUP)], -1)


def zero_spectrum(f_ref):
    def clear(c, _):
        f_ref[c] = jnp.zeros(f_ref.shape[1:], F32)
        return 0
    lax.fori_loop(0, f_ref.shape[0], clear, 0)


def add_spectrum(f_ref, c, outs, unit):
    lanes = f_ref.shape[-1]
    for u in range(unit):
        for k, o in enumerate(outs):
            f_ref[c + u, CLASS_ROWS[k]:CLASS_ROWS[k + 1]] += o[:, u * lanes:(u + 1) * lanes]


def forward_kernel(unit, x_ref, t0, t1, t2, f_ref):
    f_ref = f_ref.at[0]
    width = x_ref.shape[2]

    @pl.when(pl.program_id(1) == 0)
    def _():
        zero_spectrum(f_ref)

    def body(i, _):
        c = i * unit
        rows = [jnp.concatenate([field_lanes(x_ref, y, c + u) for u in range(unit)], -1) for y in range(Y_BLOCK)]
        v = [jnp.stack([r[8 * j:8 * j + 8] for r in rows], 0) for j in range(5)]
        add_spectrum(f_ref, c, forward_yz(v, (t0[0], t1[0], t2[0])), unit)
        return 0
    lax.fori_loop(0, width // unit, body, 0)


def layer_kernel(unit, first, *refs):
    if first:
        bias, x_ref, w_ref, s_ref, *tabs, v_ref, f_hbm, f_ref, sem = refs
    else:
        bias, x_ref, w_ref, s_ref, *tabs, o_ref, v_ref = refs
        x_ref = x_ref.at[0]
    inv = [t[0] for t in tabs[:5]]
    width = w_ref.shape[1] // Z_BLOCK
    lanes = v_ref.shape[-1]
    batch = lanes // X_GROUP
    if first:
        v_ref = v_ref.at[0]

    def channels(y, z):
        if first:
            v = jnp.concatenate([x_ref[x, y, :, z, :] for x in range(X_GROUP)], -1)
        else:
            v = x_ref[y, :, z, :]
        d1, d2, d3 = split3(v.reshape(width * 8, lanes))
        a, b, c = w_ref[0], w_ref[1], w_ref[2]
        p = dot(a, d1) + dot(a, d2) + dot(a, d3) + dot(b, d1) + dot(b, d2) + dot(c, d1)
        v_ref[y, :, z, :] = p.reshape(width, 8, lanes)

    def z_block(j, _):
        for y in range(Y_BLOCK):
            channels(y, pl.ds(pl.multiple_of(j * 8, 8), 8))
        return 0
    lax.fori_loop(0, 5, z_block, 0)

    if first:
        @pl.when(pl.program_id(1) == 0)
        def _():
            zero_spectrum(f_ref)

    pair, per_step = unit

    def inverse(c):
        def part(p, k):
            return jnp.concatenate([s_ref[0, p, c + u, CLASS_ROWS[k]:CLASS_ROWS[k + 1]] for u in range(pair)], -1)
        return inverse_yz(part, inv)

    def finish(c, chan):
        new = []
        for j, s in enumerate(z_inverse(*chan)):
            s = s.reshape(Y_BLOCK, 8, pair * lanes)
            got = []
            for u in range(pair):
                g = gelu(s[..., u * lanes:(u + 1) * lanes] + v_ref[:, c + u, 8 * j:8 * j + 8, :] + bias[c + u])
                if first:
                    v_ref[:, c + u, 8 * j:8 * j + 8, :] = g
                else:
                    for x in range(X_GROUP):
                        o_ref[x, :, c + u, 8 * j:8 * j + 8, :] = g[..., batch * x:batch * (x + 1)]
                got.append(g)
            new.append(jnp.concatenate(got, -1))
        if first:
            add_spectrum(f_ref, c, forward_yz(new, [t[0] for t in tabs[5:]]), pair)

    def body(i, _):
        c = i * per_step
        chan = inverse(c)
        for u in range(0, per_step, pair):
            ahead = inverse(c + u + pair) if u + pair < per_step else None
            finish(c + u, chan)
            chan = ahead
        return 0
    lax.fori_loop(0, width // per_step, body, 0)

    if first:
        @pl.when(pl.program_id(1) == pl.num_programs(1) - 1)
        def _():
            copy = pltpu.make_async_copy(f_ref, f_hbm.at[pl.program_id(0)], sem)
            copy.start()
            copy.wait()


def split_dot(left, right):
    a, b, c = left
    d1, d2, d3 = split3(right)
    return dot(a, d1) + dot(a, d2) + dot(a, d3) + dot(b, d1) + dot(b, d2) + dot(c, d1)


def x_forward_kernel(m_ref, f_ref, s_ref):
    groups, width, lanes = f_ref.shape[0], f_ref.shape[1], f_ref.shape[-1]
    batch = lanes // X_GROUP
    rows = []
    for g in range(groups):
        for x in range(X_GROUP):
            for p in range(2):
                rows.append(jnp.concatenate([f_ref[g, c, 0, p, 0, :, x * batch:(x + 1) * batch] for c in range(width)], -1))
    out = split_dot((m_ref[0], m_ref[1], m_ref[2]), jnp.concatenate(rows, 0))
    s_ref[:, 0] = out.reshape(s_ref.shape[0], 2, 8, width * batch)


def x_inverse_kernel(m_ref, t_ref, s_ref):
    groups, width, lanes = s_ref.shape[0], s_ref.shape[2], s_ref.shape[-1]
    batch = lanes // X_GROUP
    n = t_ref.shape[0]
    right = t_ref[:, 0].reshape(n * 16, width * batch)
    out = split_dot((m_ref[0], m_ref[1], m_ref[2]), right).reshape(groups, X_GROUP, 2, 8, width * batch)
    for g in range(groups):
        for p in range(2):
            for c in range(width):
                row = jnp.concatenate([out[g, x, p, :, c * batch:(c + 1) * batch] for x in range(X_GROUP)], -1)
                for i, d in enumerate(split3(row)):
                    s_ref[g, i, c, 0, p, 0] = d


def mix_kernel(owner, s_ref, r_ref, i_ref, t_ref, rows, re_rows, im_rows, re_s, im_s, re_t, im_t):
    n_ky, width = r_ref.shape[2], r_ref.shape[3]
    slots = s_ref.shape[1]
    lanes = s_ref.shape[-1]
    batch = lanes // width
    modes = slots * n_ky

    for w_ref, out in ((r_ref, re_rows), (i_ref, im_rows)):
        def lay(c, _):
            for ky in range(n_ky):
                rows[ky * 8:ky * 8 + 8, 0:width] = w_ref[0, 0, ky, c]
            mat = jnp.concatenate([rows[pl.ds(h * 64 + kz, 8, stride=8), :] for kz in KZ_ORDER for h in range(n_ky // 8)], 0)
            out[c] = mat.T[0:24]
            return 0
        lax.fori_loop(0, width, lay, 0)
    re_s[...] = s_ref[0, :, 0].reshape(modes, lanes).T
    im_s[...] = s_ref[0, :, 1].reshape(modes, lanes).T

    pair = 2

    def outputs(i, _):
        d = i * pair

        def inner(c, acc):
            at = pl.ds(pl.multiple_of(c * batch, 8), batch)
            a, b = re_s[at, :], im_s[at, :]
            new = []
            for u in range(pair):
                p = jnp.broadcast_to(re_rows[c, pl.ds(d + u, 1), :], a.shape)
                q = jnp.broadcast_to(im_rows[c, pl.ds(d + u, 1), :], a.shape)
                new += [acc[2 * u] + (a * p - b * q), acc[2 * u + 1] + (a * q + b * p)]
            return tuple(new)
        zero = jnp.zeros((batch, modes), F32)
        acc = lax.fori_loop(0, width, inner, (zero,) * (2 * pair))
        for u in range(pair):
            at = pl.ds(pl.multiple_of((d + u) * batch, 8), batch)
            re_t[at, :] = acc[2 * u]
            im_t[at, :] = acc[2 * u + 1]
        return 0
    lax.fori_loop(0, width // pair, outputs, 0)
    t_ref[0, :, 0] = re_t[...].T.reshape(slots, n_ky, lanes)
    t_ref[0, :, 1] = im_t[...].T.reshape(slots, n_ky, lanes)


class Place:
    def __init__(self):
        xs, ys = lax.axis_index('xs'), lax.axis_index('ys')
        data = lax.axis_index('data')
        c, x, y = xs % 2, xs // 2, ys
        self.core = (data, ys, 2 * x + 1 - c)
        self.x_chip = (data, ys, 2 * (1 - x) + c)
        self.y_chip = (data, 1 - ys, xs)
        p, q = lambda a, b: 2 * a + b, lambda a, b: 4 + 2 * a + b
        self.mine, self.theirs = 8 * c, 8 * (1 - c)
        self.order = (p(1 - x, 1 - y), q(1 - y, 1 - x), p(1 - x, y), q(1 - y, x),
                      p(x, 1 - y), q(y, 1 - x), p(x, y), q(y, x))

    def enter(self):
        barrier = pltpu.get_barrier_semaphore()
        for device in (self.core, self.x_chip, self.y_chip):
            pl.semaphore_signal(barrier, inc=1, device_id=device, device_id_type=pl.DeviceIdType.MESH)
        pl.semaphore_wait(barrier, 3)


def remote(src, dst, send, recv, device):
    return pltpu.make_async_remote_copy(src_ref=src, dst_ref=dst, send_sem=send, recv_sem=recv, device_id=device,
                                        device_id_type=pl.DeviceIdType.MESH)


def reduce_kernel(s_hbm, out_ref, acc, r1, r2, r3, local_sem, send1, recv1, send2, recv2, send3, recv3):
    me = Place()
    local = [pltpu.make_async_copy(s_hbm.at[me.mine + me.order[t]], acc.at[t], local_sem.at[t]) for t in range(8)]
    for copy in local:
        copy.start()
    me.enter()
    first = [remote(s_hbm.at[me.theirs + me.order[t]], r1.at[t], send1.at[t], recv1.at[t], me.core) for t in range(8)]
    for copy in first:
        copy.start()
    slots = acc.shape[1]

    def add(dst, a, b):
        def row(i, _):
            dst[i] = a[i] + b[i]
            return 0
        lax.fori_loop(0, slots, row, 0)

    second = []
    for t in range(8):
        local[t].wait()
        first[t].wait_recv()
        add(acc.at[t], acc.at[t], r1.at[t])
        if t < 4:
            copy = remote(acc.at[t], r2.at[t], send2.at[t], recv2.at[t], (me.x_chip, me.y_chip)[t % 2])
            copy.start()
            second.append(copy)
    third = []
    for t in range(4):
        second[t].wait_recv()
        add(acc.at[4 + t], acc.at[4 + t], r2.at[t])
        if t < 2:
            copy = remote(acc.at[4 + t], r3.at[t], send3.at[t], recv3.at[t], (me.y_chip, me.x_chip)[t])
            copy.start()
            third.append(copy)
    for t in range(2):
        third[t].wait_recv()
        add(out_ref.at[t], acc.at[6 + t], r3.at[t])
    for copy in first + second + third:
        copy.wait_send()


def gather_kernel(t_ref, out, local_sem, send, recv):
    me = Place()
    p3, q3, p2, q2, p1, q1, p0, q0 = (me.mine + o for o in me.order)
    local = [pltpu.make_async_copy(t_ref.at[i], out.at[k], local_sem.at[i]) for i, k in enumerate((p0, q0))]
    for copy in local:
        copy.start()
    me.enter()
    count = [0]

    def push(src, k, device):
        n = count[0]
        count[0] += 1
        copy = remote(src, out.at[k], send.at[n], recv.at[n], device)
        copy.start()
        return copy
    a = push(t_ref.at[0], p0, me.y_chip)
    b = push(t_ref.at[1], q0, me.x_chip)
    c = push(t_ref.at[0], p0, me.x_chip)
    d = push(t_ref.at[1], q0, me.y_chip)
    sent = [a, b, c, d, push(t_ref.at[0], p0, me.core), push(t_ref.at[1], q0, me.core)]
    core = sent[4:]
    a.wait_recv()
    e = push(out.at[p1], p1, me.x_chip)
    b.wait_recv()
    f = push(out.at[q1], q1, me.y_chip)
    sent += [e, f]
    late = [push(out.at[p1], p1, me.core), push(out.at[q1], q1, me.core)]
    for copy, k in ((c, p2), (d, q2), (e, p3), (f, q3)):
        copy.wait_recv()
        late.append(push(out.at[k], k, me.core))
    for copy in core + late:
        copy.wait_recv()
    for copy in sent + late:
        copy.wait_send()
    for copy in local:
        copy.wait()


def block(shape, index, **kwargs):
    def index_map(*at):
        return tuple(0 if k == 'o' else at['ij'.index(k)] for k in index)
    return pl.BlockSpec(shape, index_map, **kwargs)


def bf16_addends(table):
    out = []
    for _ in range(3):
        out.append(lax.reduce_precision(table, exponent_bits=8, mantissa_bits=7))
        table = table - out[-1]
    return jnp.stack(out).astype(BF16)


def solution(mesh):
    row_devs, col_devs = mesh.shape['ys'], mesh.shape['xs']

    def local_layers(field, spec_real, spec_imag, mix_weight, bias):
        batch, x_loc, y_loc, grid_z, width = field.shape
        modes = spec_real.shape[3]
        grid_x, grid_y = x_loc * col_devs, y_loc * row_devs
        groups, blocks = x_loc // X_GROUP, y_loc // Y_BLOCK
        lanes = X_GROUP * batch
        kx, ky = kept(modes, grid_x), kept(modes, grid_y)
        n_kx, n_ky = len(kx), len(ky)
        x_index, y_index = lax.axis_index('xs'), lax.axis_index('ys')
        fwd_np, inv_np = all_tables(blocks, ky, grid_y, grid_z, grid_x * grid_y * grid_z)
        fwd, inv = [jnp.asarray(t) for t in fwd_np], [jnp.asarray(t) for t in inv_np]

        turn = 2.0 * math.pi * (kx[:, None] * np.arange(grid_x)[None, :] % grid_x) / grid_x
        cos, sin = np.cos(turn), np.sin(turn)
        fwd_x = np.stack([np.stack([cos, sin], -1), np.stack([-sin, cos], -1)], 1)
        inv_x = np.transpose(fwd_x, (2, 3, 0, 1))
        fwd_x = fwd_x.reshape(n_kx, 2, col_devs, x_loc, 2).transpose(2, 0, 1, 3, 4).reshape(col_devs, 2 * n_kx, 2 * x_loc)
        inv_x = inv_x.reshape(col_devs, 2 * x_loc, 2 * n_kx)
        odd = (jnp.arange(16 * x_loc) % 2 * y_index)[:, None]

        def x_table(tables):
            wide = np.kron(tables, np.eye(8)).astype(np.float32)
            t = lax.dynamic_index_in_dim(jnp.asarray(wide), x_index, 0, keepdims=False)
            return bf16_addends(jnp.where(odd == 1, -t, t))
        fwd_x, inv_x = x_table(fwd_x), x_table(inv_x)
        eye = jnp.eye(Z_BLOCK, dtype=F32)
        point_w = [bf16_addends((mix_weight[layer].T[:, None, :, None] * eye[None, :, None, :]).reshape(width * 8, width * 8))
                   for layer in range(2)]

        real_w, imag_w = (jnp.transpose(w, (0, 1, 2, 4, 3, 5)) for w in (spec_real, spec_imag))
        v = jnp.transpose(field, (1, 2, 4, 3, 0))
        grid = (groups, blocks)
        params = pltpu.CompilerParams(vmem_limit_bytes=VMEM_LIMIT)
        one = pl.Buffered(1)
        spec_shape = jax.ShapeDtypeStruct((groups, width, 256, lanes), F32)
        in_block = block((X_GROUP, Y_BLOCK, width, grid_z, batch), 'ijooo')
        mid_block = block((1, Y_BLOCK, width, grid_z, lanes), 'ijooo')
        part_block = block((1, 3, width, 256, lanes), 'ioooo', pipeline_mode=one)
        w_block = block((3, width * 8, width * 8), 'ooo')

        def table_specs(tables):
            return [block((1,) + t.shape[1:], 'joo') for t in tables]

        f = pl.pallas_call(
            functools.partial(forward_kernel, 4), grid=grid, out_shape=spec_shape,
            in_specs=[in_block] + table_specs(fwd),
            out_specs=block((1, width, 256, lanes), 'iooo'),
            compiler_params=params, name='forward')(v, *fwd)

        own = 2
        core, x_chip = x_index % 2, x_index // 2
        owner = jnp.stack([8 * core + 2 * x_chip + y_index, 8 * core + 4 + 2 * y_index + x_chip]).astype(jnp.int32)
        full = (n_kx, 8, 2, n_ky, width * batch)

        def across(f, layer):
            s = pl.pallas_call(
                x_forward_kernel, grid=(8, n_ky // 8), out_shape=jax.ShapeDtypeStruct(full, F32),
                in_specs=[block((3, 256, 256), 'ooo'),
                          block((groups, width, 1, 2, 1, 8, lanes), 'ooiojoo')],
                out_specs=block((n_kx, 1, 2, 8, width * batch), 'oiojo'),
                compiler_params=params, name='x_forward')(
                    fwd_x, f.reshape(groups, width, 8, 2, n_ky // 8, 8, lanes))
            unit = full[1:]
            s = pl.pallas_call(
                reduce_kernel, out_shape=jax.ShapeDtypeStruct((own,) + unit, F32),
                in_specs=[pl.BlockSpec(memory_space=pl.ANY)], out_specs=pl.BlockSpec(memory_space=pltpu.VMEM),
                scratch_shapes=[pltpu.VMEM((n,) + unit, F32) for n in (8, 8, 4, 2)]
                + [pltpu.SemaphoreType.DMA((n,)) for n in (8, 8, 8, 4, 4, 2, 2)],
                compiler_params=pltpu.CompilerParams(
                    vmem_limit_bytes=VMEM_LIMIT, collective_id=2 * layer, has_side_effects=True), name='reduce')(s)
            r_spec = pl.BlockSpec((1, 1, n_ky, width, 8, width), lambda i, o: (layer, o[i], 0, 0, 0, 0))
            s_spec = block((1,) + full[1:], 'ioooo')
            t = pl.pallas_call(
                mix_kernel, out_shape=jax.ShapeDtypeStruct((own,) + full[1:], F32),
                grid_spec=pltpu.PrefetchScalarGridSpec(
                    num_scalar_prefetch=1, grid=(own,), in_specs=[s_spec, r_spec, r_spec], out_specs=s_spec,
                    scratch_shapes=[pltpu.VMEM((n_ky * 8, 128), F32)] + [pltpu.VMEM((width, 24, 128), F32)] * 2
                    + [pltpu.VMEM((width * batch, 8 * n_ky), F32)] * 4),
                compiler_params=params, name='mix')(owner, s, real_w, imag_w)
            t = pl.pallas_call(
                gather_kernel, out_shape=jax.ShapeDtypeStruct(full, F32),
                in_specs=[pl.BlockSpec(memory_space=pltpu.VMEM)], out_specs=pl.BlockSpec(memory_space=pl.ANY),
                scratch_shapes=[pltpu.SemaphoreType.DMA((2,)), pltpu.SemaphoreType.DMA((14,)), pltpu.SemaphoreType.DMA((14,))],
                compiler_params=pltpu.CompilerParams(
                    vmem_limit_bytes=VMEM_LIMIT, collective_id=2 * layer + 1, has_side_effects=True), name='gather')(t)
            parts = pl.pallas_call(
                x_inverse_kernel, grid=(8, n_ky // 8),
                out_shape=jax.ShapeDtypeStruct((groups, 3, width, 8, 2, n_ky // 8, 8, lanes), BF16),
                in_specs=[block((3, 256, 256), 'ooo'),
                          block((n_kx, 1, 2, 8, width * batch), 'oiojo')],
                out_specs=block((groups, 3, width, 1, 2, 1, 8, lanes), 'oooiojoo'),
                compiler_params=params, name='x_inverse')(inv_x, t)
            return parts.reshape(groups, 3, width, 256, lanes)

        smem = pl.BlockSpec(memory_space=pltpu.SMEM)
        parts = across(f, 0)
        v1, f = pl.pallas_call(
            functools.partial(layer_kernel, (2, 10), True), grid=grid,
            out_shape=(jax.ShapeDtypeStruct((groups, y_loc, width, grid_z, lanes), F32), spec_shape),
            in_specs=[smem, in_block, w_block, part_block] + table_specs(inv) + table_specs(fwd),
            out_specs=(mid_block, pl.BlockSpec(memory_space=pl.ANY)),
            scratch_shapes=[pltpu.VMEM((width, 256, lanes), F32), pltpu.SemaphoreType.DMA],
            compiler_params=params, name='layer_first')(bias[0], v, point_w[0], parts, *inv, *fwd)
        parts = across(f, 1)
        out = pl.pallas_call(
            functools.partial(layer_kernel, (1, 10), False), grid=grid,
            out_shape=jax.ShapeDtypeStruct((x_loc, y_loc, width, grid_z, batch), F32),
            in_specs=[smem, mid_block, w_block, part_block] + table_specs(inv),
            out_specs=in_block,
            scratch_shapes=[pltpu.VMEM((Y_BLOCK, width, grid_z, lanes), F32)],
            compiler_params=params, name='layer_last')(bias[1], v1, point_w[1], parts, *inv)
        return jnp.transpose(out, (4, 0, 1, 3, 2))

    field_spec = P('data', 'xs', 'ys', None, None)
    return jax.shard_map(local_layers, mesh=mesh, in_specs=(field_spec, P(), P(), P(), P()), out_specs=field_spec, check_vma=False)
```

time: 3910 us -> 1030 us (0.26)
  matrix products: 1980 us -> 0 us
  waiting for transfers between devices: 1400 us -> 0 us
  Pallas kernels: 0 us -> 1020 us
  local copies, waits for them, and re-layouts: 485 us -> 4.87 us
    dot_general x18 -> x0, matrix products: 1980 us -> none  [the longest x16 1390 us: contract(): jnp.einsum(form, left, right, precision=EXACT_DOT, preferred_element_type...]
    pallas_call x0 -> x13, Pallas kernels: none -> 1020 us  [the longest x1 247 us: local_layers(): pl.pallas_call(functools.partial(layer_kernel, (2, 10), True), grid=grid,...]
    reduce_scatter x4 -> x0, waiting for transfers between devices: 939 us -> none  [the longest x2 914 us: local_layers(): lax.psum_scatter(along_y.reshape(2, batch, x_loc, yz_modes, width), 'ys',...]
    all_gather x4 -> x0, waiting for transfers between devices: 466 us -> none  [the longest x2 365 us: local_layers(): lax.all_gather(back_x, 'ys', axis=3, tiled=True)]
    transpose x4 -> x2, local copies, waits for them, and re-layouts: 132 us -> 0.19 us  [local_layers(): mix_weight[layer].T[:, None, :, None] * eye[None, :, None, :]]
    dynamic_slice x7 -> x0, local copies, waits for them, and re-layouts: 88.7 us -> none  [the longest x4 46.5 us: local_layers(): lax.dynamic_slice_in_dim(spec_imag[layer].reshape(2 * modes, yz_modes, wi...]
    reshape x6 -> x0, local copies, waits for them, and re-layouts: 82.9 us -> none  [the longest x4 52.3 us: local_layers(): along_x.reshape(2, batch, 2 * modes * yz_local, width)]
    slice x5 -> x1, local copies, waits for them, and re-layouts: 70.2 us -> 0.82 us  [local_layers(): mix_weight[layer].T[:, None, :, None] * eye[None, :, None, :]]
  transfers between devices with their start and end apart: 8 -> 0, of which waited for: 7 -> 0; matrix products, arithmetic and copies ran while one was open for 20% -> 0% of each run, Pallas kernels for 0% -> 0%
where the time goes in v1:
time: 1030 us
  Pallas kernels  1020 us (99%)
    pallas_call x1, Pallas kernels, local_layers(): pl.pallas_call(functools.partial(layer_kernel, (2, 10), True), grid=grid,...  247 us
    pallas_call x1, Pallas kernels, local_layers(): pl.pallas_call(functools.partial(layer_kernel, (1, 10), False), grid=grid...  199 us
    pallas_call x2, Pallas kernels, across(): pl.pallas_call(reduce_kernel, out_shape=jax.ShapeDtypeStruct((own,) + uni...  155 us
    pallas_call x2, Pallas kernels, across(): pl.pallas_call(gather_kernel, out_shape=jax.ShapeDtypeStruct(full, F32),...  151 us
    pallas_call x1, Pallas kernels, local_layers(): pl.pallas_call(functools.partial(forward_kernel, 4), grid=grid, out_shape...  107 us
    pallas_call x2, Pallas kernels, across(): pl.pallas_call(x_inverse_kernel, grid=(8, n_ky // 8), out_shape=jax.Shape...  61.2 us
    pallas_call x2, Pallas kernels, across(): pl.pallas_call(x_forward_kernel, grid=(8, n_ky // 8), out_shape=jax.Shape...  60.4 us
    pallas_call x2, Pallas kernels, across(): pl.pallas_call(mix_kernel, out_shape=jax.ShapeDtypeStruct((own,) + full[1...  41.4 us

profile of v1, /device:TPU:0, one launch (start us, length us, event | category | flops | bytes accessed | tf_op | source)
XLA Modules:
  0.0 1032.9 jit_solution(16280725183893731434)
XLA Ops:
  0.0 0.7 pad_add_fusion.owner
  0.7 1.4 slice_bitcast_fusion
  2.0 0.8 fusion.11
  2.9 0.1 copy.25
  3.0 0.1 copy.24
  3.0 1.2 reduce-precision_convert_fusion.1
  4.3 1.0 pad_maximum_fusion
  5.3 1.6 broadcast_multiply_fusion
  6.8 2.0 mul.95
  8.9 0.7 pad_maximum_fusion.3.refs_2_
  9.7 0.5 mul.87
  10.2 0.8 pad_maximum_fusion.2.refs_2_
  11.0 106.6 %forward.1 = f32[2,20,256,384]{3,2,1,0:T(8,128)} custom-call(f32[16,32,20,40,48]{4,3,2,1,0:T(8,128)} %bitcast.2.x_ref.refs_1_, bf16[8,64,192]{2,1,0:T(8,128)(2,1)} %constant.73.clone.t0.refs_9_, bf16[8,192,256]{2,1,0:T(8,128)(2,1)} %constant.74.clone.t1.refs_10_, bf16[8,192,256]{2,1,0:T(8,128)(2,1)} %constant.75.clone.t2.refs_11_), custom_call_target="tpu_custom_call" | custom-call | tf_op jit(solution)/shard_map/forward/pallas_call | solution.py:504
  117.6 30.2 %x_forward.2.s_hbm = f32[16,8,2,16,960]{4,3,2,1,0:T(8,128)} custom-call(bf16[3,256,256]{2,1,0:T(8,128)(2,1)} %get-tuple-element.31.m_ref, f32[2,20,8,2,2,8,384]{6,5,4,3,2,1,0:T(8,128)} %bitcast.28), custom_call_target="tpu_custom_call" | custom-call | tf_op jit(solution)/shard_map/x_forward/pallas_call | solution.py:516
  147.8 78.8 %reduce.2.s_ref = f32[2,8,2,16,960]{4,3,2,1,0:T(8,128)} custom-call(f32[16,8,2,16,960]{4,3,2,1,0:T(8,128)} %x_forward.2.s_hbm), custom_call_target="tpu_custom_call" | custom-call | tf_op jit(solution)/shard_map/reduce/pallas_call | solution.py:524
  226.6 20.6 %mix.2.t_ref = f32[2,8,2,16,960]{4,3,2,1,0:T(8,128)} custom-call(s32[2]{0:T(128)} %pad_add_fusion.owner, f32[2,8,2,16,960]{4,3,2,1,0:T(8,128)} %reduce.2.s_ref, f32[2,16,16,20,8,20]{5,4,3,2,1,0:T(8,128)} %bitcast.22, f32[2,16,16,20,8,20]{5,4,3,2,1,0:T(8,128)} %bitcast.24), custom_call_target="tpu_custom_call" | custom-call | tf_op jit(solution)/shard_map/mix/pallas_call | solution.py:533
  247.2 75.8 %gather.2.t_ref = f32[16,8,2,16,960]{4,3,2,1,0:T(8,128)} custom-call(f32[2,8,2,16,960]{4,3,2,1,0:T(8,128)} %mix.2.t_ref), custom_call_target="tpu_custom_call" | custom-call | tf_op jit(solution)/shard_map/gather/pallas_call | solution.py:540
  323.0 30.6 %x_inverse.2 = bf16[2,3,20,8,2,2,8,384]{7,6,5,4,3,2,1,0:T(8,128)(2,1)} custom-call(bf16[3,256,256]{2,1,0:T(8,128)(2,1)} %get-tuple-element.30.m_ref, f32[16,8,2,16,960]{4,3,2,1,0:T(8,128)} %gather.2.t_ref), custom_call_target="tpu_custom_call" | custom-call | tf_op jit(solution)/shard_map/x_inverse/pallas_call | solution.py:546
  353.5 246.6 %layer_first.1 = (f32[2,32,20,40,384]{4,3,2,1,0:T(8,128)}, f32[2,20,256,384]{3,2,1,0:T(8,128)}) custom-call(f32[20]{0:T(128)} %get-tuple-element.25.refs_0_, f32[16,32,20,40,48]{4,3,2,1,0:T(8,128)} %bitcast.2.x_ref.refs_1_, bf16[3,160,160]{2,1,0:T(8,128)(2,1)} %pad_maximum_fusion.2.refs_2_, bf16[2,3,20,256,384]{4,3,2,1,0:T(8,128)(2,1)} %bitcast.27, ...), custom_call_target="tpu_custom_call" | custom-call | tf_op jit(solution)/shard_map/layer_first/pallas_call | solution.py:557
  600.2 30.2 %x_forward.3.s_hbm = f32[16,8,2,16,960]{4,3,2,1,0:T(8,128)} custom-call(bf16[3,256,256]{2,1,0:T(8,128)(2,1)} %get-tuple-element.31.m_ref, f32[2,20,8,2,2,8,384]{6,5,4,3,2,1,0:T(8,128)} %bitcast.29), custom_call_target="tpu_custom_call" | custom-call | tf_op jit(solution)/shard_map/x_forward/pallas_call | solution.py:516
  630.4 76.7 %reduce.3.s_ref = f32[2,8,2,16,960]{4,3,2,1,0:T(8,128)} custom-call(f32[16,8,2,16,960]{4,3,2,1,0:T(8,128)} %x_forward.3.s_hbm), custom_call_target="tpu_custom_call" | custom-call | tf_op jit(solution)/shard_map/reduce/pallas_call | solution.py:524
  707.1 20.8 %mix.3.t_ref = f32[2,8,2,16,960]{4,3,2,1,0:T(8,128)} custom-call(s32[2]{0:T(128)} %pad_add_fusion.owner, f32[2,8,2,16,960]{4,3,2,1,0:T(8,128)} %reduce.3.s_ref, f32[2,16,16,20,8,20]{5,4,3,2,1,0:T(8,128)} %bitcast.23, f32[2,16,16,20,8,20]{5,4,3,2,1,0:T(8,128)} %bitcast.25), custom_call_target="tpu_custom_call" | custom-call | tf_op jit(solution)/shard_map/mix/pallas_call | solution.py:533
  727.8 75.5 %gather.3.t_ref = f32[16,8,2,16,960]{4,3,2,1,0:T(8,128)} custom-call(f32[2,8,2,16,960]{4,3,2,1,0:T(8,128)} %mix.3.t_ref), custom_call_target="tpu_custom_call" | custom-call | tf_op jit(solution)/shard_map/gather/pallas_call | solution.py:540
  803.4 30.6 %x_inverse.3 = bf16[2,3,20,8,2,2,8,384]{7,6,5,4,3,2,1,0:T(8,128)(2,1)} custom-call(bf16[3,256,256]{2,1,0:T(8,128)(2,1)} %get-tuple-element.30.m_ref, f32[16,8,2,16,960]{4,3,2,1,0:T(8,128)} %gather.3.t_ref), custom_call_target="tpu_custom_call" | custom-call | tf_op jit(solution)/shard_map/x_inverse/pallas_call | solution.py:546
  834.0 198.9 %layer_last.1 = f32[16,32,20,40,48]{4,3,2,1,0:T(8,128)} custom-call(f32[20]{0:T(128)} %get-tuple-element.26.refs_0_, f32[2,32,20,40,384]{4,3,2,1,0:T(8,128)} %get-tuple-element.7.refs_1_, bf16[3,160,160]{2,1,0:T(8,128)(2,1)} %pad_maximum_fusion.3.refs_2_, bf16[2,3,20,256,384]{4,3,2,1,0:T(8,128)(2,1)} %bitcast.26, ...), custom_call_target="tpu_custom_call" | custom-call | tf_op jit(solution)/shard_map/layer_last/pallas_call | solution.py:565
  (4 shorter events, 0.1 us)

commit v2 on v1

--- a/solution.py
+++ b/solution.py
@@ -14,8 +14,10 @@
 BF16 = jnp.bfloat16
 VMEM_LIMIT = 64 * 1024 * 1024 - 65536
 
+SUB = 8
 X_GROUP = 8
 Y_BLOCK = 4
+HALF_BLOCK = 2
 Z_BLOCK = 8
 KZ_CLASS = ((0, 5), (1, 6, 4), (2, 7, 3))
 KZ_ORDER = tuple(kz for group in KZ_CLASS for kz in group)
@@ -179,40 +181,38 @@
     def body(i, _):
         c = i * unit
         rows = [jnp.concatenate([field_lanes(x_ref, y, c + u) for u in range(unit)], -1) for y in range(Y_BLOCK)]
-        v = [jnp.stack([r[8 * j:8 * j + 8] for r in rows], 0) for j in range(5)]
+        v = [jnp.stack([r[SUB * j:SUB * j + SUB] for r in rows], 0) for j in range(5)]
         add_spectrum(f_ref, c, forward_yz(v, (t0[0], t1[0], t2[0])), unit)
         return 0
     lax.fori_loop(0, width // unit, body, 0)
 
 
+def channel_product(first, x_ref, w_ref, p_ref):
+    blocks, width, _, lanes = p_ref.shape
+
+    def z_block(j, _):
+        z = pl.ds(pl.multiple_of(j * SUB, SUB), SUB)
+        for y in range(blocks):
+            if first:
+                v = jnp.concatenate([x_ref[x, y, :, z, :] for x in range(X_GROUP)], -1)
+            else:
+                v = x_ref[0, y, :, z, :]
+            p_ref[y, :, z, :] = split_dot((w_ref[0], w_ref[1], w_ref[2]), v.reshape(width * SUB, lanes)).reshape(width, SUB, lanes)
+        return 0
+    lax.fori_loop(0, p_ref.shape[2] // SUB, z_block, 0)
+
+
 def layer_kernel(unit, first, *refs):
-    if first:
-        bias, x_ref, w_ref, s_ref, *tabs, v_ref, f_hbm, f_ref, sem = refs
-    else:
-        bias, x_ref, w_ref, s_ref, *tabs, o_ref, v_ref = refs
-        x_ref = x_ref.at[0]
-    inv = [t[0] for t in tabs[:5]]
-    width = w_ref.shape[1] // Z_BLOCK
-    lanes = v_ref.shape[-1]
+    bias, p_ref, s_ref, *tabs = refs
+    p_ref = p_ref.at[0]
+    width, lanes = p_ref.shape[1], p_ref.shape[-1]
     batch = lanes // X_GROUP
     if first:
+        *tabs, v_ref, f_hbm, f_ref, sem = tabs
         v_ref = v_ref.at[0]
-
-    def channels(y, z):
-        if first:
-            v = jnp.concatenate([x_ref[x, y, :, z, :] for x in range(X_GROUP)], -1)
-        else:
-            v = x_ref[y, :, z, :]
-        d1, d2, d3 = split3(v.reshape(width * 8, lanes))
-        a, b, c = w_ref[0], w_ref[1], w_ref[2]
-        p = dot(a, d1) + dot(a, d2) + dot(a, d3) + dot(b, d1) + dot(b, d2) + dot(c, d1)
-        v_ref[y, :, z, :] = p.reshape(width, 8, lanes)
-
-    def z_block(j, _):
-        for y in range(Y_BLOCK):
-            channels(y, pl.ds(pl.multiple_of(j * 8, 8), 8))
-        return 0
-    lax.fori_loop(0, 5, z_block, 0)
+    else:
+        *tabs, o_ref = tabs
+    inv = [t[0] for t in tabs[:5]]
 
     if first:
         @pl.when(pl.program_id(1) == 0)
@@ -229,15 +229,15 @@
     def finish(c, chan):
         new = []
         for j, s in enumerate(z_inverse(*chan)):
-            s = s.reshape(Y_BLOCK, 8, pair * lanes)
+            s = s.reshape(Y_BLOCK, SUB, pair * lanes)
             got = []
             for u in range(pair):
-                g = gelu(s[..., u * lanes:(u + 1) * lanes] + v_ref[:, c + u, 8 * j:8 * j + 8, :] + bias[c + u])
+                g = gelu(s[..., u * lanes:(u + 1) * lanes] + p_ref[:, c + u, SUB * j:SUB * j + SUB, :] + bias[c + u])
                 if first:
-                    v_ref[:, c + u, 8 * j:8 * j + 8, :] = g
+                    v_ref[:, c + u, SUB * j:SUB * j + SUB, :] = g
                 else:
                     for x in range(X_GROUP):
-                        o_ref[x, :, c + u, 8 * j:8 * j + 8, :] = g[..., batch * x:batch * (x + 1)]
+                        o_ref[x, :, c + u, SUB * j:SUB * j + SUB, :] = g[..., batch * x:batch * (x + 1)]
                 got.append(g)
             new.append(jnp.concatenate(got, -1))
         if first:
@@ -276,7 +276,7 @@
             for p in range(2):
                 rows.append(jnp.concatenate([f_ref[g, c, 0, p, 0, :, x * batch:(x + 1) * batch] for c in range(width)], -1))
     out = split_dot((m_ref[0], m_ref[1], m_ref[2]), jnp.concatenate(rows, 0))
-    s_ref[:, 0] = out.reshape(s_ref.shape[0], 2, 8, width * batch)
+    s_ref[:, 0] = out.reshape(s_ref.shape[0], 2, SUB, width * batch)
 
 
 def x_inverse_kernel(m_ref, t_ref, s_ref):
@@ -284,7 +284,7 @@
     batch = lanes // X_GROUP
     n = t_ref.shape[0]
     right = t_ref[:, 0].reshape(n * 16, width * batch)
-    out = split_dot((m_ref[0], m_ref[1], m_ref[2]), right).reshape(groups, X_GROUP, 2, 8, width * batch)
+    out = split_dot((m_ref[0], m_ref[1], m_ref[2]), right).reshape(groups, X_GROUP, 2, SUB, width * batch)
     for g in range(groups):
         for p in range(2):
             for c in range(width):
@@ -303,8 +303,8 @@
     for w_ref, out in ((r_ref, re_rows), (i_ref, im_rows)):
         def lay(c, _):
             for ky in range(n_ky):
-                rows[ky * 8:ky * 8 + 8, 0:width] = w_ref[0, 0, ky, c]
-            mat = jnp.concatenate([rows[pl.ds(h * 64 + kz, 8, stride=8), :] for kz in KZ_ORDER for h in range(n_ky // 8)], 0)
+                rows[ky * SUB:ky * SUB + SUB, 0:width] = w_ref[0, 0, ky, c]
+            mat = jnp.concatenate([rows[pl.ds(h * 64 + kz, SUB, stride=SUB), :] for kz in KZ_ORDER for h in range(n_ky // SUB)], 0)
             out[c] = mat.T[0:24]
             return 0
         lax.fori_loop(0, width, lay, 0)
@@ -317,7 +317,7 @@
         d = i * pair
 
         def inner(c, acc):
-            at = pl.ds(pl.multiple_of(c * batch, 8), batch)
+            at = pl.ds(pl.multiple_of(c * batch, SUB), batch)
             a, b = re_s[at, :], im_s[at, :]
             new = []
             for u in range(pair):
@@ -328,7 +328,7 @@
         zero = jnp.zeros((batch, modes), F32)
         acc = lax.fori_loop(0, width, inner, (zero,) * (2 * pair))
         for u in range(pair):
-            at = pl.ds(pl.multiple_of((d + u) * batch, 8), batch)
+            at = pl.ds(pl.multiple_of((d + u) * batch, SUB), batch)
             re_t[at, :] = acc[2 * u]
             im_t[at, :] = acc[2 * u + 1]
         return 0
@@ -346,7 +346,7 @@
         self.x_chip = (data, ys, 2 * (1 - x) + c)
         self.y_chip = (data, 1 - ys, xs)
         p, q = lambda a, b: 2 * a + b, lambda a, b: 4 + 2 * a + b
-        self.mine, self.theirs = 8 * c, 8 * (1 - c)
+        self.mine, self.theirs = SUB * c, SUB * (1 - c)
         self.order = (p(1 - x, 1 - y), q(1 - y, 1 - x), p(1 - x, y), q(1 - y, x),
                       p(x, 1 - y), q(y, 1 - x), p(x, y), q(y, x))
 
@@ -362,83 +362,108 @@
                                         device_id_type=pl.DeviceIdType.MESH)
 
 
-def reduce_kernel(s_hbm, out_ref, acc, r1, r2, r3, local_sem, send1, recv1, send2, recv2, send3, recv3):
+def reduce_kernel(first, s_hbm, x_ref, w_ref, out_ref, p_ref, acc, r1, r2, r3, local_sem, send1, recv1, send2, recv2, send3, recv3):
     me = Place()
-    local = [pltpu.make_async_copy(s_hbm.at[me.mine + me.order[t]], acc.at[t], local_sem.at[t]) for t in range(8)]
-    for copy in local:
-        copy.start()
-    me.enter()
-    first = [remote(s_hbm.at[me.theirs + me.order[t]], r1.at[t], send1.at[t], recv1.at[t], me.core) for t in range(8)]
-    for copy in first:
-        copy.start()
-    slots = acc.shape[1]
+    step, last = pl.program_id(0), pl.num_programs(0) - 1
+    local = [pltpu.make_async_copy(s_hbm.at[me.mine + me.order[t]], acc.at[t], local_sem.at[t]) for t in range(SUB)]
+    one = [remote(s_hbm.at[me.theirs + me.order[t]], r1.at[t], send1.at[t], recv1.at[t], me.core) for t in range(SUB)]
+    two = [remote(acc.at[t], r2.at[t], send2.at[t], recv2.at[t], (me.x_chip, me.y_chip)[t % 2]) for t in range(4)]
+    three = [remote(acc.at[4 + t], r3.at[t], send3.at[t], recv3.at[t], (me.y_chip, me.x_chip)[t]) for t in range(2)]
 
     def add(dst, a, b):
         def row(i, _):
             dst[i] = a[i] + b[i]
             return 0
-        lax.fori_loop(0, slots, row, 0)
-
-    second = []
-    for t in range(8):
+        lax.fori_loop(0, acc.shape[1], row, 0)
+
+    def from_core(t):
         local[t].wait()
-        first[t].wait_recv()
+        one[t].wait_recv()
         add(acc.at[t], acc.at[t], r1.at[t])
-        if t < 4:
-            copy = remote(acc.at[t], r2.at[t], send2.at[t], recv2.at[t], (me.x_chip, me.y_chip)[t % 2])
+
+    def from_chip(t):
+        two[t].wait_recv()
+        add(acc.at[4 + t], acc.at[4 + t], r2.at[t])
+
+    @pl.when(step == 0)
+    def _():
+        for copy in local:
             copy.start()
-            second.append(copy)
-    third = []
-    for t in range(4):
-        second[t].wait_recv()
-        add(acc.at[4 + t], acc.at[4 + t], r2.at[t])
-        if t < 2:
-            copy = remote(acc.at[4 + t], r3.at[t], send3.at[t], recv3.at[t], (me.y_chip, me.x_chip)[t])
+        me.enter()
+        for copy in one:
             copy.start()
-            third.append(copy)
-    for t in range(2):
-        third[t].wait_recv()
-        add(out_ref.at[t], acc.at[6 + t], r3.at[t])
-    for copy in first + second + third:
-        copy.wait_send()
-
-
-def gather_kernel(t_ref, out, local_sem, send, recv):
+
+    @pl.when(step == 1)
+    def _():
+        for t in range(4):
+            from_core(t)
+            two[t].start()
+
+    @pl.when(step == 2)
+    def _():
+        for t in range(4, SUB):
+            from_core(t)
+
+    @pl.when(step == last // 2)
+    def _():
+        for t in range(2):
+            from_chip(t)
+            three[t].start()
+
+    channel_product(first, x_ref, w_ref, p_ref.at[0])
+
+    @pl.when(step == last)
+    def _():
+        for t in range(2, 4):
+            from_chip(t)
+        for t in range(2):
+            three[t].wait_recv()
+            add(out_ref.at[t], acc.at[6 + t], r3.at[t])
+        for copy in one + two + three:
+            copy.wait_send()
+
+
+def gather_kernel(first, t_ref, x_ref, w_ref, p_in, out, p_ref, local_sem, send, recv):
     me = Place()
+    step, last = pl.program_id(0), pl.num_programs(0) - 1
     p3, q3, p2, q2, p1, q1, p0, q0 = (me.mine + o for o in me.order)
-    local = [pltpu.make_async_copy(t_ref.at[i], out.at[k], local_sem.at[i]) for i, k in enumerate((p0, q0))]
-    for copy in local:
-        copy.start()
-    me.enter()
-    count = [0]
-
-    def push(src, k, device):
-        n = count[0]
-        count[0] += 1
-        copy = remote(src, out.at[k], send.at[n], recv.at[n], device)
-        copy.start()
-        return copy
-    a = push(t_ref.at[0], p0, me.y_chip)
-    b = push(t_ref.at[1], q0, me.x_chip)
-    c = push(t_ref.at[0], p0, me.x_chip)
-    d = push(t_ref.at[1], q0, me.y_chip)
-    sent = [a, b, c, d, push(t_ref.at[0], p0, me.core), push(t_ref.at[1], q0, me.core)]
-    core = sent[4:]
-    a.wait_recv()
-    e = push(out.at[p1], p1, me.x_chip)
-    b.wait_recv()
-    f = push(out.at[q1], q1, me.y_chip)
-    sent += [e, f]
-    late = [push(out.at[p1], p1, me.core), push(out.at[q1], q1, me.core)]
-    for copy, k in ((c, p2), (d, q2), (e, p3), (f, q3)):
-        copy.wait_recv()
-        late.append(push(out.at[k], k, me.core))
-    for copy in core + late:
-        copy.wait_recv()
-    for copy in sent + late:
-        copy.wait_send()
-    for copy in local:
-        copy.wait()
+    own = (t_ref.at[0], t_ref.at[1])
+    local = [pltpu.make_async_copy(own[i], out.at[k], local_sem.at[i]) for i, k in enumerate((p0, q0))]
+    plan = [(own[0], p0, me.y_chip), (own[1], q0, me.x_chip), (own[0], p0, me.x_chip), (own[1], q0, me.y_chip),
+            (own[0], p0, me.core), (own[1], q0, me.core),
+            (out.at[p1], p1, me.x_chip), (out.at[q1], q1, me.y_chip)]
+    plan += [(out.at[k], k, me.core) for k in (p1, q1, p2, q2, p3, q3)]
+    copies = [remote(src, out.at[k], send.at[n], recv.at[n], device) for n, (src, k, device) in enumerate(plan)]
+
+    @pl.when(step == 0)
+    def _():
+        for copy in local:
+            copy.start()
+        me.enter()
+        for copy in copies[:6]:
+            copy.start()
+
+    @pl.when(step == last // 2)
+    def _():
+        for n in range(2):
+            copies[n].wait_recv()
+            copies[6 + n].start()
+        for n in range(2):
+            copies[SUB + n].start()
+
+    channel_product(first, x_ref, w_ref, p_ref.at[0])
+
+    @pl.when(step == last)
+    def _():
+        for n, arrived in enumerate((2, 3, 6, 7)):
+            copies[arrived].wait_recv()
+            copies[10 + n].start()
+        for n in (4, 5, SUB, 9, 10, 11, 12, 13):
+            copies[n].wait_recv()
+        for copy in copies:
+            copy.wait_send()
+        for copy in local:
+            copy.wait()
 
 
 def block(shape, index, **kwargs):
@@ -450,7 +475,7 @@
 def bf16_addends(table):
     out = []
     for _ in range(3):
-        out.append(lax.reduce_precision(table, exponent_bits=8, mantissa_bits=7))
+        out.append(lax.reduce_precision(table, exponent_bits=SUB, mantissa_bits=7))
         table = table - out[-1]
     return jnp.stack(out).astype(BF16)
 
@@ -479,12 +504,12 @@
         odd = (jnp.arange(16 * x_loc) % 2 * y_index)[:, None]
 
         def x_table(tables):
-            wide = np.kron(tables, np.eye(8)).astype(np.float32)
+            wide = np.kron(tables, np.eye(SUB)).astype(np.float32)
             t = lax.dynamic_index_in_dim(jnp.asarray(wide), x_index, 0, keepdims=False)
             return bf16_addends(jnp.where(odd == 1, -t, t))
         fwd_x, inv_x = x_table(fwd_x), x_table(inv_x)
         eye = jnp.eye(Z_BLOCK, dtype=F32)
-        point_w = [bf16_addends((mix_weight[layer].T[:, None, :, None] * eye[None, :, None, :]).reshape(width * 8, width * 8))
+        point_w = [bf16_addends((mix_weight[layer].T[:, None, :, None] * eye[None, :, None, :]).reshape(width * SUB, width * SUB))
                    for layer in range(2)]
 
         real_w, imag_w = (jnp.transpose(w, (0, 1, 2, 4, 3, 5)) for w in (spec_real, spec_imag))
@@ -496,7 +521,16 @@
         in_block = block((X_GROUP, Y_BLOCK, width, grid_z, batch), 'ijooo')
         mid_block = block((1, Y_BLOCK, width, grid_z, lanes), 'ijooo')
         part_block = block((1, 3, width, 256, lanes), 'ioooo', pipeline_mode=one)
-        w_block = block((3, width * 8, width * 8), 'ooo')
+        mid_shape = jax.ShapeDtypeStruct((groups, y_loc, width, grid_z, lanes), F32)
+        steps = y_loc // HALF_BLOCK
+        anywhere, vmem = pl.BlockSpec(memory_space=pl.ANY), pl.BlockSpec(memory_space=pltpu.VMEM)
+        w_block = block((3, width * SUB, width * SUB), 'ooo')
+
+        def half_block(first, half):
+            shape = (HALF_BLOCK, width, grid_z)
+            if first:
+                return pl.BlockSpec((X_GROUP,) + shape + (batch,), lambda j: (half, j, 0, 0, 0))
+            return pl.BlockSpec((1,) + shape + (lanes,), lambda j: (half, j, 0, 0, 0))
 
         def table_specs(tables):
             return [block((1,) + t.shape[1:], 'joo') for t in tables]
@@ -509,66 +543,71 @@
 
         own = 2
         core, x_chip = x_index % 2, x_index // 2
-        owner = jnp.stack([8 * core + 2 * x_chip + y_index, 8 * core + 4 + 2 * y_index + x_chip]).astype(jnp.int32)
-        full = (n_kx, 8, 2, n_ky, width * batch)
-
-        def across(f, layer):
+        owner = jnp.stack([SUB * core + 2 * x_chip + y_index, SUB * core + 4 + 2 * y_index + x_chip]).astype(jnp.int32)
+        full = (n_kx, SUB, 2, n_ky, width * batch)
+
+        def across(f, layer, source):
             s = pl.pallas_call(
-                x_forward_kernel, grid=(8, n_ky // 8), out_shape=jax.ShapeDtypeStruct(full, F32),
+                x_forward_kernel, grid=(SUB, n_ky // SUB), out_shape=jax.ShapeDtypeStruct(full, F32),
                 in_specs=[block((3, 256, 256), 'ooo'),
-                          block((groups, width, 1, 2, 1, 8, lanes), 'ooiojoo')],
-                out_specs=block((n_kx, 1, 2, 8, width * batch), 'oiojo'),
+                          block((groups, width, 1, 2, 1, SUB, lanes), 'ooiojoo')],
+                out_specs=block((n_kx, 1, 2, SUB, width * batch), 'oiojo'),
                 compiler_params=params, name='x_forward')(
-                    fwd_x, f.reshape(groups, width, 8, 2, n_ky // 8, 8, lanes))
+                    fwd_x, f.reshape(groups, width, SUB, 2, n_ky // SUB, SUB, lanes))
             unit = full[1:]
-            s = pl.pallas_call(
-                reduce_kernel, out_shape=jax.ShapeDtypeStruct((own,) + unit, F32),
-                in_specs=[pl.BlockSpec(memory_space=pl.ANY)], out_specs=pl.BlockSpec(memory_space=pltpu.VMEM),
-                scratch_shapes=[pltpu.VMEM((n,) + unit, F32) for n in (8, 8, 4, 2)]
-                + [pltpu.SemaphoreType.DMA((n,)) for n in (8, 8, 8, 4, 4, 2, 2)],
+            first = layer == 0
+            own_block = block((own,) + unit, 'ooooo')
+            s, p = pl.pallas_call(
+                functools.partial(reduce_kernel, first), grid=(steps,),
+                out_shape=(jax.ShapeDtypeStruct((own,) + unit, F32), mid_shape),
+                in_specs=[anywhere, half_block(first, 0), w_block],
+                out_specs=(own_block, half_block(False, 0)),
+                scratch_shapes=[pltpu.VMEM((n,) + unit, F32) for n in (SUB, SUB, 4, 2)]
+                + [pltpu.SemaphoreType.DMA((n,)) for n in (SUB, SUB, SUB, 4, 4, 2, 2)],
                 compiler_params=pltpu.CompilerParams(
-                    vmem_limit_bytes=VMEM_LIMIT, collective_id=2 * layer, has_side_effects=True), name='reduce')(s)
-            r_spec = pl.BlockSpec((1, 1, n_ky, width, 8, width), lambda i, o: (layer, o[i], 0, 0, 0, 0))
+                    vmem_limit_bytes=VMEM_LIMIT, collective_id=2 * layer, has_side_effects=True),
+                name='reduce')(s, source, point_w[layer])
+            r_spec = pl.BlockSpec((1, 1, n_ky, width, SUB, width), lambda i, o: (layer, o[i], 0, 0, 0, 0))
             s_spec = block((1,) + full[1:], 'ioooo')
             t = pl.pallas_call(
                 mix_kernel, out_shape=jax.ShapeDtypeStruct((own,) + full[1:], F32),
                 grid_spec=pltpu.PrefetchScalarGridSpec(
                     num_scalar_prefetch=1, grid=(own,), in_specs=[s_spec, r_spec, r_spec], out_specs=s_spec,
-                    scratch_shapes=[pltpu.VMEM((n_ky * 8, 128), F32)] + [pltpu.VMEM((width, 24, 128), F32)] * 2
-                    + [pltpu.VMEM((width * batch, 8 * n_ky), F32)] * 4),
+                    scratch_shapes=[pltpu.VMEM((n_ky * SUB, 128), F32)] + [pltpu.VMEM((width, 24, 128), F32)] * 2
+                    + [pltpu.VMEM((width * batch, SUB * n_ky), F32)] * 4),
                 compiler_params=params, name='mix')(owner, s, real_w, imag_w)
-            t = pl.pallas_call(
-                gather_kernel, out_shape=jax.ShapeDtypeStruct(full, F32),
-                in_specs=[pl.BlockSpec(memory_space=pltpu.VMEM)], out_specs=pl.BlockSpec(memory_space=pl.ANY),
+            t, p = pl.pallas_call(
+                functools.partial(gather_kernel, first), grid=(steps,),
+                out_shape=(jax.ShapeDtypeStruct(full, F32), mid_shape),
+                in_specs=[own_block, half_block(first, 1), w_block, anywhere],
+                out_specs=(anywhere, half_block(False, 1)), input_output_aliases={3: 1},
                 scratch_shapes=[pltpu.SemaphoreType.DMA((2,)), pltpu.SemaphoreType.DMA((14,)), pltpu.SemaphoreType.DMA((14,))],
                 compiler_params=pltpu.CompilerParams(
-                    vmem_limit_bytes=VMEM_LIMIT, collective_id=2 * layer + 1, has_side_effects=True), name='gather')(t)
+                    vmem_limit_bytes=VMEM_LIMIT, collective_id=2 * layer + 1, has_side_effects=True),
+                name='gather')(t, source, point_w[layer], p)
             parts = pl.pallas_call(
-                x_inverse_kernel, grid=(8, n_ky // 8),
-                out_shape=jax.ShapeDtypeStruct((groups, 3, width, 8, 2, n_ky // 8, 8, lanes), BF16),
+                x_inverse_kernel, grid=(SUB, n_ky // SUB),
+                out_shape=jax.ShapeDtypeStruct((groups, 3, width, SUB, 2, n_ky // SUB, SUB, lanes), BF16),
                 in_specs=[block((3, 256, 256), 'ooo'),
-                          block((n_kx, 1, 2, 8, width * batch), 'oiojo')],
-                out_specs=block((groups, 3, width, 1, 2, 1, 8, lanes), 'oooiojoo'),
+                          block((n_kx, 1, 2, SUB, width * batch), 'oiojo')],
+                out_specs=block((groups, 3, width, 1, 2, 1, SUB, lanes), 'oooiojoo'),
                 compiler_params=params, name='x_inverse')(inv_x, t)
-            return parts.reshape(groups, 3, width, 256, lanes)
+            return parts.reshape(groups, 3, width, 256, lanes), p
 
         smem = pl.BlockSpec(memory_space=pltpu.SMEM)
-        parts = across(f, 0)
+        parts, p = across(f, 0, v)
         v1, f = pl.pallas_call(
-            functools.partial(layer_kernel, (2, 10), True), grid=grid,
-            out_shape=(jax.ShapeDtypeStruct((groups, y_loc, width, grid_z, lanes), F32), spec_shape),
-            in_specs=[smem, in_block, w_block, part_block] + table_specs(inv) + table_specs(fwd),
-            out_specs=(mid_block, pl.BlockSpec(memory_space=pl.ANY)),
+            functools.partial(layer_kernel, (2, 10), True), grid=grid, out_shape=(mid_shape, spec_shape),
+            in_specs=[smem, mid_block, part_block] + table_specs(inv) + table_specs(fwd),
+            out_specs=(mid_block, anywhere),
             scratch_shapes=[pltpu.VMEM((width, 256, lanes), F32), pltpu.SemaphoreType.DMA],
-            compiler_params=params, name='layer_first')(bias[0], v, point_w[0], parts, *inv, *fwd)
-        parts = across(f, 1)
+            compiler_params=params, name='layer_first')(bias[0], p, parts, *inv, *fwd)
+        parts, p = across(f, 1, v1)
         out = pl.pallas_call(
             functools.partial(layer_kernel, (1, 10), False), grid=grid,
             out_shape=jax.ShapeDtypeStruct((x_loc, y_loc, width, grid_z, batch), F32),
-            in_specs=[smem, mid_block, w_block, part_block] + table_specs(inv),
-            out_specs=in_block,
-            scratch_shapes=[pltpu.VMEM((Y_BLOCK, width, grid_z, lanes), F32)],
-            compiler_params=params, name='layer_last')(bias[1], v1, point_w[1], parts, *inv)
+            in_specs=[smem, mid_block, part_block] + table_specs(inv), out_specs=in_block,
+            compiler_params=params, name='layer_last')(bias[1], p, parts, *inv)
         return jnp.transpose(out, (4, 0, 1, 3, 2))
 
     field_spec = P('data', 'xs', 'ys', None, None)

time: 1030 us -> 857 us (0.83)
  Pallas kernels: 1020 us -> 844 us
    pallas_call x1, Pallas kernels: 247 us -> 131 us  [local_layers(): pl.pallas_call(functools.partial(layer_kernel, (2, 10), True), grid=grid,...]
    pallas_call x1, Pallas kernels: 199 us -> 117 us  [local_layers(): pl.pallas_call(functools.partial(layer_kernel, (1, 10), False), grid=grid...]
    pallas_call x8, Pallas kernels: 428 us -> 448 us  [the longest x2 163 us: across(): pl.pallas_call(functools.partial(gather_kernel, first), grid=(steps,), ou...]
where the time goes in v2:
time: 857 us; the launch traced here: 855 us
  Pallas kernels  844 us (98%)
    pallas_call x2, Pallas kernels, across(): pl.pallas_call(functools.partial(gather_kernel, first), grid=(steps,), ou...  163 us
    pallas_call x2, Pallas kernels, across(): pl.pallas_call(functools.partial(reduce_kernel, first), grid=(steps,), ou...  163 us
    pallas_call x1, Pallas kernels, local_layers(): pl.pallas_call(functools.partial(layer_kernel, (2, 10), True), grid=grid,...  131 us
    pallas_call x1, Pallas kernels, local_layers(): pl.pallas_call(functools.partial(layer_kernel, (1, 10), False), grid=grid...  117 us
    pallas_call x1, Pallas kernels, local_layers(): pl.pallas_call(functools.partial(forward_kernel, 4), grid=grid, out_shape...  107 us
    pallas_call x2, Pallas kernels, across(): pl.pallas_call(x_inverse_kernel, grid=(SUB, n_ky // SUB), out_shape=jax.S...  61.3 us
    pallas_call x2, Pallas kernels, across(): pl.pallas_call(x_forward_kernel, grid=(SUB, n_ky // SUB), out_shape=jax.S...  60.4 us
    pallas_call x2, Pallas kernels, across(): pl.pallas_call(mix_kernel, out_shape=jax.ShapeDtypeStruct((own,) + full[1...  41.3 us

profile of v2, /device:TPU:0, one launch (start us, length us, event | category | flops | bytes accessed | tf_op | source)
XLA Modules:
  0.0 855.1 jit_solution(10087508398626674368)
XLA Ops:
  0.0 0.7 pad_add_fusion.owner
  0.7 1.3 slice_bitcast_fusion
  2.0 0.8 fusion.11
  2.8 0.1 copy.27
  2.9 0.1 copy.26
  3.0 1.2 reduce-precision_convert_fusion.1
  4.3 1.0 pad_maximum_fusion
  5.2 1.6 broadcast_multiply_fusion
  6.8 2.0 mul.95
  8.9 0.7 pad_maximum_fusion.3.w_ref
  9.6 0.5 mul.92
  10.1 0.7 pad_maximum_fusion.2.w_ref
  10.9 106.6 %forward.1 = f32[2,20,256,384]{3,2,1,0:T(8,128)} custom-call(f32[16,32,20,40,48]{4,3,2,1,0:T(8,128)} %bitcast.4.x_ref, bf16[8,64,192]{2,1,0:T(8,128)(2,1)} %constant.73.clone.t0.refs_8_, bf16[8,192,256]{2,1,0:T(8,128)(2,1)} %constant.74.clone.t1.refs_9_, bf16[8,192,256]{2,1,0:T(8,128)(2,1)} %constant.75.clone.t2.refs_10_), custom_call_target="tpu_custom_call" | custom-call | tf_op jit(solution)/shard_map/forward/pallas_call | solution.py:538
  117.5 30.2 %x_forward.2.s_hbm = f32[16,8,2,16,960]{4,3,2,1,0:T(8,128)} custom-call(bf16[3,256,256]{2,1,0:T(8,128)(2,1)} %get-tuple-element.46.m_ref, f32[2,20,8,2,2,8,384]{6,5,4,3,2,1,0:T(8,128)} %bitcast.28), custom_call_target="tpu_custom_call" | custom-call | tf_op jit(solution)/shard_map/x_forward/pallas_call | solution.py:550
  147.7 84.1 %reduce.2 = (f32[2,8,2,16,960]{4,3,2,1,0:T(8,128)}, f32[2,32,20,40,384]{4,3,2,1,0:T(8,128)}) custom-call(f32[16,8,2,16,960]{4,3,2,1,0:T(8,128)} %x_forward.2.s_hbm, f32[16,32,20,40,48]{4,3,2,1,0:T(8,128)} %bitcast.4.x_ref, bf16[3,160,160]{2,1,0:T(8,128)(2,1)} %pad_maximum_fusion.2.w_ref), custom_call_target="tpu_custom_call" | custom-call | tf_op jit(solution)/shard_map/reduce/pallas_call | solution.py:560
  231.8 20.6 %mix.2.t_ref = f32[2,8,2,16,960]{4,3,2,1,0:T(8,128)} custom-call(s32[2]{0:T(128)} %pad_add_fusion.owner, f32[2,8,2,16,960]{4,3,2,1,0:T(8,128)} %get-tuple-element.15.s_ref, f32[2,16,16,20,8,20]{5,4,3,2,1,0:T(8,128)} %bitcast.22, f32[2,16,16,20,8,20]{5,4,3,2,1,0:T(8,128)} %bitcast.24), custom_call_target="tpu_custom_call" | custom-call | tf_op jit(solution)/shard_map/mix/pallas_call | solution.py:572
  252.4 85.6 %gather.2 = (f32[16,8,2,16,960]{4,3,2,1,0:T(8,128)}, f32[2,32,20,40,384]{4,3,2,1,0:T(8,128)}) custom-call(f32[2,8,2,16,960]{4,3,2,1,0:T(8,128)} %mix.2.t_ref, f32[16,32,20,40,48]{4,3,2,1,0:T(8,128)} %bitcast.4.x_ref, bf16[3,160,160]{2,1,0:T(8,128)(2,1)} %pad_maximum_fusion.2.w_ref, ...), custom_call_target="tpu_custom_call", output_to_operand_aliasing={{1}: (3, {})} | custom-call | tf_op jit(solution)/shard_map/gather/pallas_call | solution.py:579
  338.0 30.7 %x_inverse.2 = bf16[2,3,20,8,2,2,8,384]{7,6,5,4,3,2,1,0:T(8,128)(2,1)} custom-call(bf16[3,256,256]{2,1,0:T(8,128)(2,1)} %get-tuple-element.47.m_ref, f32[16,8,2,16,960]{4,3,2,1,0:T(8,128)} %get-tuple-element.18.t_ref), custom_call_target="tpu_custom_call" | custom-call | tf_op jit(solution)/shard_map/x_inverse/pallas_call | solution.py:588
  368.7 131.3 %layer_first.1 = (f32[2,32,20,40,384]{4,3,2,1,0:T(8,128)}, f32[2,20,256,384]{3,2,1,0:T(8,128)}) custom-call(f32[20]{0:T(128)} %get-tuple-element.41.refs_0_, f32[2,32,20,40,384]{4,3,2,1,0:T(8,128)} %get-tuple-element.17.refs_1_, bf16[2,3,20,256,384]{4,3,2,1,0:T(8,128)(2,1)} %bitcast.27, bf16[8,96,192]{2,1,0:T(8,128)(2,1)} %constant.76.clone.refs_3_, ...), custom_call_target="tpu_custom_call" | custom-call | tf_op jit(solution)/shard_map/layer_first/pallas_call | solution.py:599
  500.0 30.2 %x_forward.3.s_hbm = f32[16,8,2,16,960]{4,3,2,1,0:T(8,128)} custom-call(bf16[3,256,256]{2,1,0:T(8,128)(2,1)} %get-tuple-element.46.m_ref, f32[2,20,8,2,2,8,384]{6,5,4,3,2,1,0:T(8,128)} %bitcast.29), custom_call_target="tpu_custom_call" | custom-call | tf_op jit(solution)/shard_map/x_forward/pallas_call | solution.py:550
  530.2 79.1 %reduce.3 = (f32[2,8,2,16,960]{4,3,2,1,0:T(8,128)}, f32[2,32,20,40,384]{4,3,2,1,0:T(8,128)}) custom-call(f32[16,8,2,16,960]{4,3,2,1,0:T(8,128)} %x_forward.3.s_hbm, f32[2,32,20,40,384]{4,3,2,1,0:T(8,128)} %get-tuple-element.20.x_ref, bf16[3,160,160]{2,1,0:T(8,128)(2,1)} %pad_maximum_fusion.3.w_ref), custom_call_target="tpu_custom_call" | custom-call | tf_op jit(solution)/shard_map/reduce/pallas_call | solution.py:560
  609.4 20.7 %mix.3.t_ref = f32[2,8,2,16,960]{4,3,2,1,0:T(8,128)} custom-call(s32[2]{0:T(128)} %pad_add_fusion.owner, f32[2,8,2,16,960]{4,3,2,1,0:T(8,128)} %get-tuple-element.21.s_ref, f32[2,16,16,20,8,20]{5,4,3,2,1,0:T(8,128)} %bitcast.23, f32[2,16,16,20,8,20]{5,4,3,2,1,0:T(8,128)} %bitcast.25), custom_call_target="tpu_custom_call" | custom-call | tf_op jit(solution)/shard_map/mix/pallas_call | solution.py:572
  630.1 77.8 %gather.3 = (f32[16,8,2,16,960]{4,3,2,1,0:T(8,128)}, f32[2,32,20,40,384]{4,3,2,1,0:T(8,128)}) custom-call(f32[2,8,2,16,960]{4,3,2,1,0:T(8,128)} %mix.3.t_ref, f32[2,32,20,40,384]{4,3,2,1,0:T(8,128)} %get-tuple-element.20.x_ref, bf16[3,160,160]{2,1,0:T(8,128)(2,1)} %pad_maximum_fusion.3.w_ref, ...), custom_call_target="tpu_custom_call", output_to_operand_aliasing={{1}: (3, {})} | custom-call | tf_op jit(solution)/shard_map/gather/pallas_call | solution.py:579
  707.9 30.6 %x_inverse.3 = bf16[2,3,20,8,2,2,8,384]{7,6,5,4,3,2,1,0:T(8,128)(2,1)} custom-call(bf16[3,256,256]{2,1,0:T(8,128)(2,1)} %get-tuple-element.47.m_ref, f32[16,8,2,16,960]{4,3,2,1,0:T(8,128)} %get-tuple-element.24.t_ref), custom_call_target="tpu_custom_call" | custom-call | tf_op jit(solution)/shard_map/x_inverse/pallas_call | solution.py:588
  738.5 116.6 %layer_last.1 = f32[16,32,20,40,48]{4,3,2,1,0:T(8,128)} custom-call(f32[20]{0:T(128)} %get-tuple-element.42.refs_0_, f32[2,32,20,40,384]{4,3,2,1,0:T(8,128)} %get-tuple-element.23.refs_1_, bf16[2,3,20,256,384]{4,3,2,1,0:T(8,128)(2,1)} %bitcast.26, bf16[8,96,192]{2,1,0:T(8,128)(2,1)} %constant.76.clone.refs_3_, bf16[8,128,192]{2,1,0:T(8,128)(2,1)} %constant.77.clone.refs_4_, ...), custom_call_target="tpu_custom_call" | custom-call | tf_op jit(solution)/shard_map/layer_last/pallas_call | solution.py:606
  (4 shorter events, 0.1 us)

commit v3 on v2

--- a/solution.py
+++ b/solution.py
@@ -22,6 +22,9 @@
 KZ_CLASS = ((0, 5), (1, 6, 4), (2, 7, 3))
 KZ_ORDER = tuple(kz for group in KZ_CLASS for kz in group)
 CLASS_ROWS = (0, 64, 160, 256)
+FORWARD_UNIT = (2, 10)
+FIRST_UNIT = (2, 10)
+LAST_UNIT = (1, 10)
 ROOT5_4 = math.sqrt(5.0) / 4.0
 SIN_1 = math.sin(2.0 * math.pi / 5.0)
 SIN_RATIO = math.sin(4.0 * math.pi / 5.0) / SIN_1
@@ -66,7 +69,7 @@
     cols = []
     for kz in group:
         t, s = yz_angles(kz, y_pos, ky, grid_y, grid_z).transpose(1, 2, 0), kz_sign(kz)
-        w = (1.0 if kz == 0 else 2.0) / points
+        w = (0.5 if kz == 0 else 1.0) / points
         real, imag = [w * np.cos(t)], [-w * np.sin(t)]
         if s:
             real.append(s * SIN_1 * w * np.sin(t))
@@ -123,33 +126,61 @@
     return a0 + total, p - r, q - s, q + s, p + r
 
 
-def forward_yz(v, tables):
-    lanes = v[0].shape[-1]
-    chan = [split3(c.reshape(Y_BLOCK * Z_BLOCK, lanes)) for c in z_forward(v)]
-    outs = [dot(tables[0], jnp.concatenate([chan[0][i] for i in (0, 1, 2, 0, 1, 0)], 0))]
-    for k, (p, q) in ((1, (1, 2)), (2, (3, 4))):
-        o = dot(tables[k], jnp.concatenate([chan[c][i] for i in (0, 1, 2, 0) for c in (p, q)], 0))
-        half = o.shape[0] // 2
-        outs.append(o[:half] + o[half:])
-    return outs
-
-
-def inverse_yz(part, tables):
-    n = Y_BLOCK * Z_BLOCK
+def split_tiles(u_ref, channels):
+    rows, lanes = u_ref.shape[1:]
+    out = [[], [], []]
+    for k in channels:
+        for r in range(0, rows, 2 * SUB):
+            cells = [split3(u_ref[k, r:r + 2 * SUB, lane:lane + 128]) for lane in range(0, lanes, 128)]
+            for i in range(3):
+                out[i].append(jnp.concatenate([cell[i] for cell in cells], -1))
+    return [jnp.concatenate(rows, 0) for rows in out]
+
+
+def add_tiles(o, n, lanes, first=0):
+    for r in range(0, n, SUB):
+        for lane in range(0, lanes, 128):
+            cells = [o[b + r:b + r + SUB, lane:lane + 128] for b in range(0, o.shape[0], n)]
+            yield r, lane, functools.reduce(jnp.add, cells)
+
+
+def forward_stage(u_ref, tables, f_ref, c, pair):
+    lanes = f_ref.shape[-1]
+    for k, channels in enumerate(((0,), (1, 2), (3, 4))):
+        d = split_tiles(u_ref, channels)
+        o = dot(tables[k], jnp.concatenate([d[i] for i in ((0, 1, 2, 0) if k else (0, 1, 2, 0, 1, 0))], 0))
+        n = CLASS_ROWS[k + 1] - CLASS_ROWS[k]
+        for r, lane, v in add_tiles(o, n, pair * lanes):
+            at = (c + lane // lanes, slice(CLASS_ROWS[k] + r, CLASS_ROWS[k] + r + SUB), slice(lane % lanes, lane % lanes + 128))
+            f_ref[at] += v
+
+
+def inverse_stage(s_ref, c, pair, tables, u_ref):
+    n, lanes = u_ref.shape[1:]
+
+    def part(i, k):
+        return jnp.concatenate([s_ref[0, i, c + u, CLASS_ROWS[k]:CLASS_ROWS[k + 1]] for u in range(pair)], -1)
     o = dot(tables[0], jnp.concatenate([part(i, 0) for i in range(3)], 0))
-    chan = [o[:n] + o[n:2 * n] + o[2 * n:]]
+    for r, lane, v in add_tiles(o, n, lanes):
+        u_ref[0, r:r + SUB, lane:lane + 128] = v
     for k in (1, 2):
         d1, d2, d3 = (part(i, k) for i in range(3))
-        o = dot(tables[2 * k - 1], jnp.concatenate([d1, d2], 0))
-        o = o[:2 * n] + o[2 * n:] + dot(tables[2 * k], jnp.concatenate([d1, d3], 0))
-        chan += [o[:n], o[n:]]
-    return chan
-
-
-def gelu(u):
-    k = math.sqrt(2.0 / math.pi)
-    h = 0.5 * u
-    return h + h * jnp.tanh(u * (k + (0.044715 * k) * (u * u)))
+        o = jnp.concatenate([dot(tables[2 * k - 1], jnp.concatenate([d1, d2], 0)),
+                             dot(tables[2 * k], jnp.concatenate([d1, d3], 0))], 0)
+        for r, lane, v in add_tiles(o, 2 * n, lanes):
+            u_ref[2 * k - 1 + r // n, r % n:r % n + SUB, lane:lane + 128] = v
+
+
+def registers(pair, lanes):
+    for u in range(pair):
+        for y in range(Y_BLOCK):
+            for lane in range(0, lanes, 128):
+                yield u, y, lane, (slice(y * SUB, (y + 1) * SUB), slice(u * lanes + lane, u * lanes + lane + 128))
+
+
+def gelu(h):
+    k = 2.0 * math.sqrt(2.0 / math.pi)
+    return h + h * jnp.tanh(h * (k + (4.0 * 0.044715 * k) * (h * h)))
 
 
 def field_lanes(x_ref, y, c):
@@ -163,31 +194,36 @@
     lax.fori_loop(0, f_ref.shape[0], clear, 0)
 
 
-def add_spectrum(f_ref, c, outs, unit):
-    lanes = f_ref.shape[-1]
-    for u in range(unit):
-        for k, o in enumerate(outs):
-            f_ref[c + u, CLASS_ROWS[k]:CLASS_ROWS[k + 1]] += o[:, u * lanes:(u + 1) * lanes]
-
-
-def forward_kernel(unit, x_ref, t0, t1, t2, f_ref):
+def forward_kernel(unit, x_ref, t0, t1, t2, f_ref, u_ref):
     f_ref = f_ref.at[0]
-    width = x_ref.shape[2]
+    width, lanes = x_ref.shape[2], f_ref.shape[-1]
+    pair, per_step = unit
+    tables = (t0[0], t1[0], t2[0])
 
     @pl.when(pl.program_id(1) == 0)
     def _():
         zero_spectrum(f_ref)
 
+    def load(c, slot):
+        for u in range(pair):
+            for y in range(Y_BLOCK):
+                row = field_lanes(x_ref, y, c + u)
+                for k, v in enumerate(z_forward([row[SUB * j:SUB * j + SUB] for j in range(5)])):
+                    u_ref[slot, k, y * SUB:(y + 1) * SUB, u * lanes:(u + 1) * lanes] = v
+
     def body(i, _):
-        c = i * unit
-        rows = [jnp.concatenate([field_lanes(x_ref, y, c + u) for u in range(unit)], -1) for y in range(Y_BLOCK)]
-        v = [jnp.stack([r[SUB * j:SUB * j + SUB] for r in rows], 0) for j in range(5)]
-        add_spectrum(f_ref, c, forward_yz(v, (t0[0], t1[0], t2[0])), unit)
+        c = i * per_step
+        count = per_step // pair
+        for n in range(count + 1):
+            if n < count:
+                load(c + n * pair, n)
+            if n:
+                forward_stage(u_ref.at[n - 1], tables, f_ref, c + (n - 1) * pair, pair)
         return 0
-    lax.fori_loop(0, width // unit, body, 0)
-
-
-def channel_product(first, x_ref, w_ref, p_ref):
+    lax.fori_loop(0, width // per_step, body, 0)
+
+
+def channel_product(first, x_ref, w_ref, b_ref, p_ref):
     blocks, width, _, lanes = p_ref.shape
 
     def z_block(j, _):
@@ -197,59 +233,59 @@
                 v = jnp.concatenate([x_ref[x, y, :, z, :] for x in range(X_GROUP)], -1)
             else:
                 v = x_ref[0, y, :, z, :]
-            p_ref[y, :, z, :] = split_dot((w_ref[0], w_ref[1], w_ref[2]), v.reshape(width * SUB, lanes)).reshape(width, SUB, lanes)
+            p = split_dot((w_ref[0], w_ref[1], w_ref[2]), v.reshape(width * SUB, lanes))
+            for c in range(width):
+                p_ref[y, c, z, :] = p[c * SUB:(c + 1) * SUB] + b_ref[c]
         return 0
     lax.fori_loop(0, p_ref.shape[2] // SUB, z_block, 0)
 
 
 def layer_kernel(unit, first, *refs):
-    bias, p_ref, s_ref, *tabs = refs
+    p_ref, s_ref, *tabs = refs
     p_ref = p_ref.at[0]
     width, lanes = p_ref.shape[1], p_ref.shape[-1]
     batch = lanes // X_GROUP
     if first:
-        *tabs, v_ref, f_hbm, f_ref, sem = tabs
+        *tabs, v_ref, f_hbm, a_ref, u_ref, f_ref, sem = tabs
         v_ref = v_ref.at[0]
-    else:
-        *tabs, o_ref = tabs
-    inv = [t[0] for t in tabs[:5]]
-
-    if first:
+
         @pl.when(pl.program_id(1) == 0)
         def _():
             zero_spectrum(f_ref)
-
+    else:
+        *tabs, o_ref, a_ref = tabs
+    inv, fwd = [t[0] for t in tabs[:5]], [t[0] for t in tabs[5:]]
     pair, per_step = unit
 
-    def inverse(c):
-        def part(p, k):
-            return jnp.concatenate([s_ref[0, p, c + u, CLASS_ROWS[k]:CLASS_ROWS[k + 1]] for u in range(pair)], -1)
-        return inverse_yz(part, inv)
-
-    def finish(c, chan):
-        new = []
-        for j, s in enumerate(z_inverse(*chan)):
-            s = s.reshape(Y_BLOCK, SUB, pair * lanes)
-            got = []
-            for u in range(pair):
-                g = gelu(s[..., u * lanes:(u + 1) * lanes] + p_ref[:, c + u, SUB * j:SUB * j + SUB, :] + bias[c + u])
+    def activate(c, slot):
+        kept_rows = {}
+        for u, y, lane, at in registers(pair, lanes):
+            new = []
+            for j, s in enumerate(z_inverse(*(a_ref[(slot, k) + at] for k in range(5)))):
+                g = gelu(s + p_ref[y, c + u, SUB * j:SUB * j + SUB, lane:lane + 128])
+                new.append(g)
                 if first:
-                    v_ref[:, c + u, SUB * j:SUB * j + SUB, :] = g
+                    v_ref[y, c + u, SUB * j:SUB * j + SUB, lane:lane + 128] = g
                 else:
-                    for x in range(X_GROUP):
-                        o_ref[x, :, c + u, SUB * j:SUB * j + SUB, :] = g[..., batch * x:batch * (x + 1)]
-                got.append(g)
-            new.append(jnp.concatenate(got, -1))
-        if first:
-            add_spectrum(f_ref, c, forward_yz(new, [t[0] for t in tabs[5:]]), pair)
+                    kept_rows[j] = kept_rows.get(j, ()) + (g,)
+            if first:
+                for k, v in enumerate(z_forward(new)):
+                    u_ref[(slot, k) + at] = v
+            elif lane + 128 == lanes:
+                for j, row in kept_rows.items():
+                    store_field(o_ref, y, c + u, SUB * j, row, batch)
+                kept_rows = {}
 
     def body(i, _):
         c = i * per_step
-        chan = inverse(c)
-        for u in range(0, per_step, pair):
-            ahead = inverse(c + u + pair) if u + pair < per_step else None
-            finish(c + u, chan)
-            chan = ahead
+        count = per_step // pair
+        for n in range(count + 2):
+            if n < count:
+                inverse_stage(s_ref, c + n * pair, pair, inv, a_ref.at[n])
+            if 0 < n <= count:
+                activate(c + (n - 1) * pair, n - 1)
+            if first and n > 1:
+                forward_stage(u_ref.at[n - 2], fwd, f_ref, c + (n - 2) * pair, pair)
         return 0
     lax.fori_loop(0, width // per_step, body, 0)
 
@@ -259,6 +295,18 @@
             copy = pltpu.make_async_copy(f_ref, f_hbm.at[pl.program_id(0)], sem)
             copy.start()
             copy.wait()
+
+
+def store_field(o_ref, y, c, z, row, batch):
+    lane = lax.broadcasted_iota(jnp.int32, row[0].shape, 1)
+    for x in range(X_GROUP):
+        at, off = divmod(x * batch, 128)
+        piece = row[at]
+        if off + batch > 128:
+            piece = jnp.where(lane < off, row[at + 1], piece)
+        if off:
+            piece = pltpu.roll(piece, 128 - off, 1)
+        o_ref[x, y, c, z:z + SUB, :] = piece[:, :batch]
 
 
 def split_dot(left, right):
@@ -362,7 +410,7 @@
                                         device_id_type=pl.DeviceIdType.MESH)
 
 
-def reduce_kernel(first, s_hbm, x_ref, w_ref, out_ref, p_ref, acc, r1, r2, r3, local_sem, send1, recv1, send2, recv2, send3, recv3):
+def reduce_kernel(first, b_ref, s_hbm, x_ref, w_ref, out_ref, p_ref, acc, r1, r2, r3, local_sem, send1, recv1, send2, recv2, send3, recv3):
     me = Place()
     step, last = pl.program_id(0), pl.num_programs(0) - 1
     local = [pltpu.make_async_copy(s_hbm.at[me.mine + me.order[t]], acc.at[t], local_sem.at[t]) for t in range(SUB)]
@@ -410,7 +458,7 @@
             from_chip(t)
             three[t].start()
 
-    channel_product(first, x_ref, w_ref, p_ref.at[0])
+    channel_product(first, x_ref, w_ref, b_ref, p_ref.at[0])
 
     @pl.when(step == last)
     def _():
@@ -423,7 +471,7 @@
             copy.wait_send()
 
 
-def gather_kernel(first, t_ref, x_ref, w_ref, p_in, out, p_ref, local_sem, send, recv):
+def gather_kernel(first, b_ref, t_ref, x_ref, w_ref, p_in, out, p_ref, local_sem, send, recv):
     me = Place()
     step, last = pl.program_id(0), pl.num_programs(0) - 1
     p3, q3, p2, q2, p1, q1, p0, q0 = (me.mine + o for o in me.order)
@@ -451,7 +499,7 @@
         for n in range(2):
             copies[SUB + n].start()
 
-    channel_product(first, x_ref, w_ref, p_ref.at[0])
+    channel_product(first, x_ref, w_ref, b_ref, p_ref.at[0])
 
     @pl.when(step == last)
     def _():
@@ -509,7 +557,8 @@
             return bf16_addends(jnp.where(odd == 1, -t, t))
         fwd_x, inv_x = x_table(fwd_x), x_table(inv_x)
         eye = jnp.eye(Z_BLOCK, dtype=F32)
-        point_w = [bf16_addends((mix_weight[layer].T[:, None, :, None] * eye[None, :, None, :]).reshape(width * SUB, width * SUB))
+        half_w, half_b = 0.5 * mix_weight, 0.5 * bias
+        point_w = [bf16_addends((half_w[layer].T[:, None, :, None] * eye[None, :, None, :]).reshape(width * SUB, width * SUB))
                    for layer in range(2)]
 
         real_w, imag_w = (jnp.transpose(w, (0, 1, 2, 4, 3, 5)) for w in (spec_real, spec_imag))
@@ -523,7 +572,10 @@
         part_block = block((1, 3, width, 256, lanes), 'ioooo', pipeline_mode=one)
         mid_shape = jax.ShapeDtypeStruct((groups, y_loc, width, grid_z, lanes), F32)
         steps = y_loc // HALF_BLOCK
-        anywhere, vmem = pl.BlockSpec(memory_space=pl.ANY), pl.BlockSpec(memory_space=pltpu.VMEM)
+        anywhere, smem = pl.BlockSpec(memory_space=pl.ANY), pl.BlockSpec(memory_space=pltpu.SMEM)
+
+        def stage(unit):
+            return pltpu.VMEM((unit[1] // unit[0], 5, Y_BLOCK * SUB, unit[0] * lanes), F32)
         w_block = block((3, width * SUB, width * SUB), 'ooo')
 
         def half_block(first, half):
@@ -536,10 +588,10 @@
             return [block((1,) + t.shape[1:], 'joo') for t in tables]
 
         f = pl.pallas_call(
-            functools.partial(forward_kernel, 4), grid=grid, out_shape=spec_shape,
+            functools.partial(forward_kernel, FORWARD_UNIT), grid=grid, out_shape=spec_shape,
             in_specs=[in_block] + table_specs(fwd),
             out_specs=block((1, width, 256, lanes), 'iooo'),
-            compiler_params=params, name='forward')(v, *fwd)
+            scratch_shapes=[stage(FORWARD_UNIT)], compiler_params=params, name='forward')(v, *fwd)
 
         own = 2
         core, x_chip = x_index % 2, x_index // 2
@@ -560,13 +612,13 @@
             s, p = pl.pallas_call(
                 functools.partial(reduce_kernel, first), grid=(steps,),
                 out_shape=(jax.ShapeDtypeStruct((own,) + unit, F32), mid_shape),
-                in_specs=[anywhere, half_block(first, 0), w_block],
+                in_specs=[smem, anywhere, half_block(first, 0), w_block],
                 out_specs=(own_block, half_block(False, 0)),
                 scratch_shapes=[pltpu.VMEM((n,) + unit, F32) for n in (SUB, SUB, 4, 2)]
                 + [pltpu.SemaphoreType.DMA((n,)) for n in (SUB, SUB, SUB, 4, 4, 2, 2)],
                 compiler_params=pltpu.CompilerParams(
                     vmem_limit_bytes=VMEM_LIMIT, collective_id=2 * layer, has_side_effects=True),
-                name='reduce')(s, source, point_w[layer])
+                name='reduce')(half_b[layer], s, source, point_w[layer])
             r_spec = pl.BlockSpec((1, 1, n_ky, width, SUB, width), lambda i, o: (layer, o[i], 0, 0, 0, 0))
             s_spec = block((1,) + full[1:], 'ioooo')
             t = pl.pallas_call(
@@ -579,12 +631,12 @@
             t, p = pl.pallas_call(
                 functools.partial(gather_kernel, first), grid=(steps,),
                 out_shape=(jax.ShapeDtypeStruct(full, F32), mid_shape),
-                in_specs=[own_block, half_block(first, 1), w_block, anywhere],
-                out_specs=(anywhere, half_block(False, 1)), input_output_aliases={3: 1},
+                in_specs=[smem, own_block, half_block(first, 1), w_block, anywhere],
+                out_specs=(anywhere, half_block(False, 1)), input_output_aliases={4: 1},
                 scratch_shapes=[pltpu.SemaphoreType.DMA((2,)), pltpu.SemaphoreType.DMA((14,)), pltpu.SemaphoreType.DMA((14,))],
                 compiler_params=pltpu.CompilerParams(
                     vmem_limit_bytes=VMEM_LIMIT, collective_id=2 * layer + 1, has_side_effects=True),
-                name='gather')(t, source, point_w[layer], p)
+                name='gather')(half_b[layer], t, source, point_w[layer], p)
             parts = pl.pallas_call(
                 x_inverse_kernel, grid=(SUB, n_ky // SUB),
                 out_shape=jax.ShapeDtypeStruct((groups, 3, width, SUB, 2, n_ky // SUB, SUB, lanes), BF16),
@@ -594,20 +646,19 @@
                 compiler_params=params, name='x_inverse')(inv_x, t)
             return parts.reshape(groups, 3, width, 256, lanes), p
 
-        smem = pl.BlockSpec(memory_space=pltpu.SMEM)
         parts, p = across(f, 0, v)
         v1, f = pl.pallas_call(
-            functools.partial(layer_kernel, (2, 10), True), grid=grid, out_shape=(mid_shape, spec_shape),
-            in_specs=[smem, mid_block, part_block] + table_specs(inv) + table_specs(fwd),
+            functools.partial(layer_kernel, FIRST_UNIT, True), grid=grid, out_shape=(mid_shape, spec_shape),
+            in_specs=[mid_block, part_block] + table_specs(inv) + table_specs(fwd),
             out_specs=(mid_block, anywhere),
-            scratch_shapes=[pltpu.VMEM((width, 256, lanes), F32), pltpu.SemaphoreType.DMA],
-            compiler_params=params, name='layer_first')(bias[0], p, parts, *inv, *fwd)
+            scratch_shapes=[stage(FIRST_UNIT)] * 2 + [pltpu.VMEM((width, 256, lanes), F32), pltpu.SemaphoreType.DMA],
+            compiler_params=params, name='layer_first')(p, parts, *inv, *fwd)
         parts, p = across(f, 1, v1)
         out = pl.pallas_call(
-            functools.partial(layer_kernel, (1, 10), False), grid=grid,
+            functools.partial(layer_kernel, LAST_UNIT, False), grid=grid,
             out_shape=jax.ShapeDtypeStruct((x_loc, y_loc, width, grid_z, batch), F32),
-            in_specs=[smem, mid_block, part_block] + table_specs(inv), out_specs=in_block,
-            compiler_params=params, name='layer_last')(bias[1], p, parts, *inv)
+            in_specs=[mid_block, part_block] + table_specs(inv), out_specs=in_block, scratch_shapes=[stage(LAST_UNIT)],
+            compiler_params=params, name='layer_last')(p, parts, *inv)
         return jnp.transpose(out, (4, 0, 1, 3, 2))
 
     field_spec = P('data', 'xs', 'ys', None, None)

time: 857 us -> 829 us (0.967)
  Pallas kernels: 844 us -> 817 us
    pallas_call x3, Pallas kernels: 355 us -> 326 us  [the longest x1 128 us: local_layers(): pl.pallas_call(functools.partial(layer_kernel, FIRST_UNIT, True), grid=gr...]
where the time goes in v3:
time: 829 us; the launch traced here: 827 us
  Pallas kernels  817 us (99%)
    pallas_call x2, Pallas kernels, across(): pl.pallas_call(functools.partial(gather_kernel, first), grid=(steps,), ou...  164 us
    pallas_call x2, Pallas kernels, across(): pl.pallas_call(functools.partial(reduce_kernel, first), grid=(steps,), ou...  164 us
    pallas_call x1, Pallas kernels, local_layers(): pl.pallas_call(functools.partial(layer_kernel, FIRST_UNIT, True), grid=gr...  128 us
    pallas_call x1, Pallas kernels, local_layers(): pl.pallas_call(functools.partial(layer_kernel, LAST_UNIT, False), grid=gr...  114 us
    pallas_call x1, Pallas kernels, local_layers(): pl.pallas_call(functools.partial(forward_kernel, FORWARD_UNIT), grid=grid...  83.7 us
    pallas_call x2, Pallas kernels, across(): pl.pallas_call(x_inverse_kernel, grid=(SUB, n_ky // SUB), out_shape=jax.S...  61.3 us
    pallas_call x2, Pallas kernels, across(): pl.pallas_call(x_forward_kernel, grid=(SUB, n_ky // SUB), out_shape=jax.S...  60.6 us
    pallas_call x2, Pallas kernels, across(): pl.pallas_call(mix_kernel, out_shape=jax.ShapeDtypeStruct((own,) + full[1...  41.3 us

profile of v3, /device:TPU:0, one launch (start us, length us, event | category | flops | bytes accessed | tf_op | source)
XLA Modules:
  0.0 827.3 jit_solution(1523010285095466760)
XLA Ops:
  0.0 0.7 pad_add_fusion.owner
  0.7 0.7 broadcast_multiply_fusion.2
  1.4 0.5 slice_bitcast_fusion.2
  1.9 0.7 copy_multiply_fusion
  2.6 0.1 copy.22
  2.7 0.1 copy.21
  2.8 1.2 reduce-precision_convert_fusion.1
  4.1 1.0 pad_maximum_fusion
  5.0 1.6 broadcast_multiply_fusion
  6.6 2.0 mul.111
  8.7 0.7 pad_maximum_fusion.3.w_ref
  9.4 0.5 mul.108
  9.9 0.7 pad_maximum_fusion.2.w_ref
  10.7 83.7 %forward.1 = f32[2,20,256,384]{3,2,1,0:T(8,128)} custom-call(f32[16,32,20,40,48]{4,3,2,1,0:T(8,128)} %bitcast.4.x_ref, bf16[8,64,192]{2,1,0:T(8,128)(2,1)} %constant.76.clone.t0.refs_7_, bf16[8,192,256]{2,1,0:T(8,128)(2,1)} %constant.77.clone.t1.refs_8_, bf16[8,192,256]{2,1,0:T(8,128)(2,1)} %constant.78.clone.t2.refs_9_), custom_call_target="tpu_custom_call" | custom-call | tf_op jit(solution)/shard_map/forward/pallas_call | solution.py:590
  94.4 30.2 %x_forward.2.s_hbm = f32[16,8,2,16,960]{4,3,2,1,0:T(8,128)} custom-call(bf16[3,256,256]{2,1,0:T(8,128)(2,1)} %get-tuple-element.46.m_ref, f32[2,20,8,2,2,8,384]{6,5,4,3,2,1,0:T(8,128)} %bitcast.28), custom_call_target="tpu_custom_call" | custom-call | tf_op jit(solution)/shard_map/x_forward/pallas_call | solution.py:602
  124.6 84.4 %reduce.2 = (f32[2,8,2,16,960]{4,3,2,1,0:T(8,128)}, f32[2,32,20,40,384]{4,3,2,1,0:T(8,128)}) custom-call(f32[20]{0:T(128)} %get-tuple-element.41.b_ref, f32[16,8,2,16,960]{4,3,2,1,0:T(8,128)} %x_forward.2.s_hbm, f32[16,32,20,40,48]{4,3,2,1,0:T(8,128)} %bitcast.4.x_ref, bf16[3,160,160]{2,1,0:T(8,128)(2,1)} %pad_maximum_fusion.2.w_ref), custom_call_target="tpu_custom_call" | custom-call | tf_op jit(solution)/shard_map/reduce/pallas_call | solution.py:612
  209.0 20.6 %mix.2.t_ref = f32[2,8,2,16,960]{4,3,2,1,0:T(8,128)} custom-call(s32[2]{0:T(128)} %pad_add_fusion.owner, f32[2,8,2,16,960]{4,3,2,1,0:T(8,128)} %get-tuple-element.15.s_ref, f32[2,16,16,20,8,20]{5,4,3,2,1,0:T(8,128)} %bitcast.22, f32[2,16,16,20,8,20]{5,4,3,2,1,0:T(8,128)} %bitcast.24), custom_call_target="tpu_custom_call" | custom-call | tf_op jit(solution)/shard_map/mix/pallas_call | solution.py:624
  229.6 86.0 %gather.2 = (f32[16,8,2,16,960]{4,3,2,1,0:T(8,128)}, f32[2,32,20,40,384]{4,3,2,1,0:T(8,128)}) custom-call(f32[20]{0:T(128)} %get-tuple-element.41.b_ref, f32[2,8,2,16,960]{4,3,2,1,0:T(8,128)} %mix.2.t_ref, f32[16,32,20,40,48]{4,3,2,1,0:T(8,128)} %bitcast.4.x_ref, bf16[3,160,160]{2,1,0:T(8,128)(2,1)} %pad_maximum_fusion.2.w_ref, ...), custom_call_target="tpu_custom_call", output_to_operand_aliasing={{1}: (4, {})} | custom-call | tf_op jit(solution)/shard_map/gather/pallas_call | solution.py:631
  315.6 30.6 %x_inverse.2 = bf16[2,3,20,8,2,2,8,384]{7,6,5,4,3,2,1,0:T(8,128)(2,1)} custom-call(bf16[3,256,256]{2,1,0:T(8,128)(2,1)} %get-tuple-element.47.m_ref, f32[16,8,2,16,960]{4,3,2,1,0:T(8,128)} %get-tuple-element.18.t_ref), custom_call_target="tpu_custom_call" | custom-call | tf_op jit(solution)/shard_map/x_inverse/pallas_call | solution.py:640
  346.2 128.2 %layer_first.1 = (f32[2,32,20,40,384]{4,3,2,1,0:T(8,128)}, f32[2,20,256,384]{3,2,1,0:T(8,128)}) custom-call(f32[2,32,20,40,384]{4,3,2,1,0:T(8,128)} %get-tuple-element.17.refs_0_, bf16[2,3,20,256,384]{4,3,2,1,0:T(8,128)(2,1)} %bitcast.27, bf16[8,96,192]{2,1,0:T(8,128)(2,1)} %constant.79.clone.refs_2_, bf16[8,128,192]{2,1,0:T(8,128)(2,1)} %constant.80.clone.refs_3_, ...), custom_call_target="tpu_custom_call" | custom-call | tf_op jit(solution)/shard_map/layer_first/pallas_call | solution.py:650
  474.5 30.4 %x_forward.3.s_hbm = f32[16,8,2,16,960]{4,3,2,1,0:T(8,128)} custom-call(bf16[3,256,256]{2,1,0:T(8,128)(2,1)} %get-tuple-element.46.m_ref, f32[2,20,8,2,2,8,384]{6,5,4,3,2,1,0:T(8,128)} %bitcast.29), custom_call_target="tpu_custom_call" | custom-call | tf_op jit(solution)/shard_map/x_forward/pallas_call | solution.py:602
  504.9 79.2 %reduce.3 = (f32[2,8,2,16,960]{4,3,2,1,0:T(8,128)}, f32[2,32,20,40,384]{4,3,2,1,0:T(8,128)}) custom-call(f32[20]{0:T(128)} %get-tuple-element.42.b_ref, f32[16,8,2,16,960]{4,3,2,1,0:T(8,128)} %x_forward.3.s_hbm, f32[2,32,20,40,384]{4,3,2,1,0:T(8,128)} %get-tuple-element.20.x_ref, bf16[3,160,160]{2,1,0:T(8,128)(2,1)} %pad_maximum_fusion.3.w_ref), custom_call_target="tpu_custom_call" | custom-call | tf_op jit(solution)/shard_map/reduce/pallas_call | solution.py:612
  584.1 20.7 %mix.3.t_ref = f32[2,8,2,16,960]{4,3,2,1,0:T(8,128)} custom-call(s32[2]{0:T(128)} %pad_add_fusion.owner, f32[2,8,2,16,960]{4,3,2,1,0:T(8,128)} %get-tuple-element.21.s_ref, f32[2,16,16,20,8,20]{5,4,3,2,1,0:T(8,128)} %bitcast.23, f32[2,16,16,20,8,20]{5,4,3,2,1,0:T(8,128)} %bitcast.25), custom_call_target="tpu_custom_call" | custom-call | tf_op jit(solution)/shard_map/mix/pallas_call | solution.py:624
  604.7 77.8 %gather.3 = (f32[16,8,2,16,960]{4,3,2,1,0:T(8,128)}, f32[2,32,20,40,384]{4,3,2,1,0:T(8,128)}) custom-call(f32[20]{0:T(128)} %get-tuple-element.42.b_ref, f32[2,8,2,16,960]{4,3,2,1,0:T(8,128)} %mix.3.t_ref, f32[2,32,20,40,384]{4,3,2,1,0:T(8,128)} %get-tuple-element.20.x_ref, ...), custom_call_target="tpu_custom_call", output_to_operand_aliasing={{1}: (4, {})} | custom-call | tf_op jit(solution)/shard_map/gather/pallas_call | solution.py:631
  682.5 30.6 %x_inverse.3 = bf16[2,3,20,8,2,2,8,384]{7,6,5,4,3,2,1,0:T(8,128)(2,1)} custom-call(bf16[3,256,256]{2,1,0:T(8,128)(2,1)} %get-tuple-element.47.m_ref, f32[16,8,2,16,960]{4,3,2,1,0:T(8,128)} %get-tuple-element.24.t_ref), custom_call_target="tpu_custom_call" | custom-call | tf_op jit(solution)/shard_map/x_inverse/pallas_call | solution.py:640
  713.2 114.1 %layer_last.1 = f32[16,32,20,40,48]{4,3,2,1,0:T(8,128)} custom-call(f32[2,32,20,40,384]{4,3,2,1,0:T(8,128)} %get-tuple-element.23.refs_0_, bf16[2,3,20,256,384]{4,3,2,1,0:T(8,128)(2,1)} %bitcast.26, bf16[8,96,192]{2,1,0:T(8,128)(2,1)} %constant.79.clone.refs_2_, bf16[8,128,192]{2,1,0:T(8,128)(2,1)} %constant.80.clone.refs_3_, ...), custom_call_target="tpu_custom_call" | custom-call | tf_op jit(solution)/shard_map/layer_last/pallas_call | solution.py:657
  (5 shorter events, 0.1 us)

commit v4 on v3

v4 whole, which is shorter than its diff:
```python
import functools
import math

import jax
import jax.numpy as jnp
import ml_dtypes
import numpy as np
from jax import lax
from jax.experimental import pallas as pl
from jax.experimental.pallas import tpu as pltpu
from jax.sharding import PartitionSpec as P

F32 = jnp.float32
BF16 = jnp.bfloat16
VMEM_LIMIT = 64 * 1024 * 1024 - 65536

SUB = 8
X_GROUP = 8
Y_BLOCK = 4
HALF_BLOCK = 2
Z_BLOCK = 8
KZ_CLASS = ((0, 5), (1, 6, 4), (2, 7, 3))
KZ_ORDER = tuple(kz for group in KZ_CLASS for kz in group)
CLASS_ROWS = (0, 64, 160, 256)
LANES = 128
FORWARD_UNIT = (2, 10)
FIRST_UNIT = (2, 10)
LAST_UNIT = (1, 10)
ROOT5_4 = math.sqrt(5.0) / 4.0
SIN_1 = math.sin(2.0 * math.pi / 5.0)
SIN_RATIO = math.sin(4.0 * math.pi / 5.0) / SIN_1


def kz_sign(kz):
    return 0 if kz % 5 == 0 else (1 if kz % 5 < 3 else -1)


def kept(modes, size):
    return np.concatenate([np.arange(modes), np.arange(size - modes, size)])


def pieces(table):
    rest = np.asarray(table, np.float32)
    out = []
    for _ in range(3):
        out.append(rest.astype(ml_dtypes.bfloat16))
        rest = rest - out[-1].astype(np.float32)
    return out


def yz_angles(kz, y_pos, ky, grid_y, grid_z):
    z_pos = np.arange(Z_BLOCK)
    turn = (ky[:, None, None] * y_pos[None, :, None] % grid_y) / grid_y + kz * z_pos[None, None, :] / grid_z
    return 2.0 * math.pi * turn


def forward_table(group, y_pos, ky, grid_y, grid_z):
    rows = []
    for kz in group:
        t, s = yz_angles(kz, y_pos, ky, grid_y, grid_z), kz_sign(kz)
        real, imag = [np.cos(t)], [-np.sin(t)]
        if s:
            real.append(-s * SIN_1 * np.sin(t))
            imag.append(-s * SIN_1 * np.cos(t))
        rows += [np.stack(part, 1).reshape(len(ky), -1) for part in (real, imag)]
    return np.concatenate(rows, 0)


def inverse_table(group, y_pos, ky, grid_y, grid_z, points):
    cols = []
    for kz in group:
        t, s = yz_angles(kz, y_pos, ky, grid_y, grid_z).transpose(1, 2, 0), kz_sign(kz)
        w = (0.5 if kz == 0 else 1.0) / points
        real, imag = [w * np.cos(t)], [-w * np.sin(t)]
        if s:
            real.append(s * SIN_1 * w * np.sin(t))
            imag.append(s * SIN_1 * w * np.cos(t))
        cols += [np.stack(part, 0).reshape(-1, len(ky)) for part in (real, imag)]
    return np.concatenate(cols, 1)


def all_tables(blocks, ky, grid_y, grid_z, points):
    fwd, inv = [[], [], []], [[], [], [], [], []]
    for block in range(blocks):
        y_pos = np.arange(Y_BLOCK) + block * Y_BLOCK
        for k, group in enumerate(KZ_CLASS):
            a, b, c = pieces(forward_table(group, y_pos, ky, grid_y, grid_z))
            n = np.zeros_like(a)
            if k == 0:
                fwd[k].append(np.concatenate([a, a, a, b, b, c], 1))
            else:
                fwd[k].append(np.block([[a, a, a, b], [c, b, n, n]]))
            a, b, c = pieces(inverse_table(group, y_pos, ky, grid_y, grid_z, points))
            n = np.zeros_like(a)
            if k == 0:
                inv[0].append(np.block([[a, a, a], [b, b, n], [c, n, n]]))
            else:
                inv[2 * k - 1].append(np.block([[a, a], [b, b]]))
                inv[2 * k].append(np.concatenate([c, a], 1))
    return [np.stack(t) for t in fwd], [np.stack(t) for t in inv]


def split3(v):
    d1 = v.astype(BF16)
    rest = v - d1.astype(F32)
    d2 = rest.astype(BF16)
    return d1, d2, (rest - d2.astype(F32)).astype(BF16)


def dot(a, b):
    return jnp.dot(a, b, preferred_element_type=F32)


def z_forward(v):
    v0, v1, v2, v3, v4 = v
    t1, t2, e1, e2 = v1 + v4, v2 + v3, v1 - v4, v2 - v3
    total = t1 + t2
    mid, dif = v0 - 0.25 * total, ROOT5_4 * (t1 - t2)
    return v0 + total, mid + dif, e1 + SIN_RATIO * e2, mid - dif, SIN_RATIO * e1 - e2


def z_inverse(a0, a1, b1, a2, b2):
    total = a1 + a2
    mid, dif = a0 - 0.25 * total, ROOT5_4 * (a1 - a2)
    p, q = mid + dif, mid - dif
    r, s = b1 + SIN_RATIO * b2, SIN_RATIO * b1 - b2
    return a0 + total, p - r, q - s, q + s, p + r


def split_tiles(u_ref, channels):
    rows, lanes = u_ref.shape[1:]
    out = [[], [], []]
    for k in channels:
        for r in range(0, rows, 2 * SUB):
            cells = [split3(u_ref[k, r:r + 2 * SUB, lane:lane + LANES]) for lane in range(0, lanes, LANES)]
            for i in range(3):
                out[i].append(jnp.concatenate([cell[i] for cell in cells], -1))
    return [jnp.concatenate(rows, 0) for rows in out]


def add_tiles(o, n, lanes, first=0):
    for r in range(0, n, SUB):
        for lane in range(0, lanes, LANES):
            cells = [o[b + r:b + r + SUB, lane:lane + LANES] for b in range(0, o.shape[0], n)]
            yield r, lane, functools.reduce(jnp.add, cells)


def forward_stage(u_ref, tables, f_ref, c, pair):
    lanes = f_ref.shape[-1]
    for k, channels in enumerate(((0,), (1, 2), (3, 4))):
        d = split_tiles(u_ref, channels)
        o = dot(tables[k], jnp.concatenate([d[i] for i in ((0, 1, 2, 0) if k else (0, 1, 2, 0, 1, 0))], 0))
        n = CLASS_ROWS[k + 1] - CLASS_ROWS[k]
        for r, lane, v in add_tiles(o, n, pair * lanes):
            at = (c + lane // lanes, slice(CLASS_ROWS[k] + r, CLASS_ROWS[k] + r + SUB), slice(lane % lanes, lane % lanes + LANES))
            f_ref[at] += v


def inverse_stage(s_ref, c, pair, tables, u_ref):
    n, lanes = u_ref.shape[1:]

    def part(i, k):
        return jnp.concatenate([s_ref[0, i, c + u, CLASS_ROWS[k]:CLASS_ROWS[k + 1]] for u in range(pair)], -1)
    o = dot(tables[0], jnp.concatenate([part(i, 0) for i in range(3)], 0))
    for r, lane, v in add_tiles(o, n, lanes):
        u_ref[0, r:r + SUB, lane:lane + LANES] = v
    for k in (1, 2):
        d1, d2, d3 = (part(i, k) for i in range(3))
        o = jnp.concatenate([dot(tables[2 * k - 1], jnp.concatenate([d1, d2], 0)),
                             dot(tables[2 * k], jnp.concatenate([d1, d3], 0))], 0)
        for r, lane, v in add_tiles(o, 2 * n, lanes):
            u_ref[2 * k - 1 + r // n, r % n:r % n + SUB, lane:lane + LANES] = v


def registers(pair, lanes):
    for u in range(pair):
        for y in range(Y_BLOCK):
            for lane in range(0, lanes, LANES):
                yield u, y, lane, (slice(y * SUB, (y + 1) * SUB), slice(u * lanes + lane, u * lanes + lane + LANES))


def gelu(h):
    k = 2.0 * math.sqrt(2.0 / math.pi)
    return h + h * jnp.tanh(h * (k + (4.0 * 0.044715 * k) * (h * h)))


def field_lanes(x_ref, y, c):
    return jnp.concatenate([x_ref[x, y, c] for x in range(X_GROUP)], -1)


def zero_spectrum(f_ref):
    def clear(c, _):
        f_ref[c] = jnp.zeros(f_ref.shape[1:], F32)
        return 0
    lax.fori_loop(0, f_ref.shape[0], clear, 0)


def forward_kernel(unit, x_ref, t0, t1, t2, f_ref, u_ref):
    f_ref = f_ref.at[0]
    width, lanes = x_ref.shape[2], f_ref.shape[-1]
    pair, per_step = unit
    tables = (t0[0], t1[0], t2[0])

    @pl.when(pl.program_id(1) == 0)
    def _():
        zero_spectrum(f_ref)

    def load(c, slot):
        for u in range(pair):
            for y in range(Y_BLOCK):
                row = field_lanes(x_ref, y, c + u)
                for k, v in enumerate(z_forward([row[SUB * j:SUB * j + SUB] for j in range(5)])):
                    u_ref[slot, k, y * SUB:(y + 1) * SUB, u * lanes:(u + 1) * lanes] = v

    def body(i, _):
        c = i * per_step
        count = per_step // pair
        for n in range(count + 1):
            if n < count:
                load(c + n * pair, n)
            if n:
                forward_stage(u_ref.at[n - 1], tables, f_ref, c + (n - 1) * pair, pair)
        return 0
    lax.fori_loop(0, width // per_step, body, 0)


def channel_product(first, x_ref, w_ref, p_ref):
    blocks, width, depth, lanes = p_ref.shape
    rows = width * SUB
    ones = jnp.ones((w_ref.shape[2] - rows, lanes), BF16)
    full, (a, b, c) = w_ref[0], (w_ref[i, :, :rows] for i in range(3))

    def z_block(j, _):
        z = pl.ds(pl.multiple_of(j * SUB, SUB), SUB)
        for y in range(blocks):
            if first:
                v = jnp.concatenate([x_ref[x, y, :, z, :] for x in range(X_GROUP)], -1)
            else:
                v = x_ref[0, y, :, z, :]
            d1, d2, d3 = split3(v.reshape(rows, lanes))
            p = dot(full, jnp.concatenate([d1, ones], 0)) + dot(a, d2) + dot(a, d3) + dot(b, d1) + dot(b, d2) + dot(c, d1)
            p_ref[y, :, z, :] = p.reshape(width, SUB, lanes)
        return 0
    lax.fori_loop(0, depth // SUB, z_block, 0)


def layer_kernel(unit, first, *refs):
    p_ref, s_ref, *tabs = refs
    p_ref = p_ref.at[0]
    width, lanes = p_ref.shape[1], p_ref.shape[-1]
    batch = lanes // X_GROUP
    if first:
        *tabs, v_ref, f_hbm, a_ref, u_ref, f_ref, sem = tabs
        v_ref = v_ref.at[0]

        @pl.when(pl.program_id(1) == 0)
        def _():
            zero_spectrum(f_ref)
    else:
        *tabs, o_ref, a_ref = tabs
    inv, fwd = [t[0] for t in tabs[:5]], [t[0] for t in tabs[5:]]
    pair, per_step = unit

    def activate(c, slot):
        kept_rows = {}
        for u, y, lane, at in registers(pair, lanes):
            new = []
            for j, s in enumerate(z_inverse(*(a_ref[(slot, k) + at] for k in range(5)))):
                g = gelu(s + p_ref[y, c + u, SUB * j:SUB * j + SUB, lane:lane + LANES])
                new.append(g)
                if first:
                    v_ref[y, c + u, SUB * j:SUB * j + SUB, lane:lane + LANES] = g
                else:
                    kept_rows[j] = kept_rows.get(j, ()) + (g,)
            if first:
                for k, v in enumerate(z_forward(new)):
                    u_ref[(slot, k) + at] = v
            elif lane + LANES == lanes:
                for j, row in kept_rows.items():
                    store_field(o_ref, y, c + u, SUB * j, row, batch)
                kept_rows = {}

    def body(i, _):
        c = i * per_step
        count = per_step // pair
        for n in range(count + 2):
            if n < count:
                inverse_stage(s_ref, c + n * pair, pair, inv, a_ref.at[n])
            if 0 < n <= count:
                activate(c + (n - 1) * pair, n - 1)
            if first and n > 1:
                forward_stage(u_ref.at[n - 2], fwd, f_ref, c + (n - 2) * pair, pair)
        return 0
    lax.fori_loop(0, width // per_step, body, 0)

    if first:
        @pl.when(pl.program_id(1) == pl.num_programs(1) - 1)
        def _():
            copy = pltpu.make_async_copy(f_ref, f_hbm.at[pl.program_id(0)], sem)
            copy.start()
            copy.wait()


def store_field(o_ref, y, c, z, row, batch):
    lane = lax.broadcasted_iota(jnp.int32, row[0].shape, 1)
    for x in range(X_GROUP):
        at, off = divmod(x * batch, LANES)
        piece = row[at]
        if off + batch > LANES:
            piece = jnp.where(lane < off, row[at + 1], piece)
        if off:
            piece = pltpu.roll(piece, LANES - off, 1)
        o_ref[x, y, c, z:z + SUB, :] = piece[:, :batch]


def split_dot(left, right):
    a, b, c = left
    d1, d2, d3 = split3(right)
    return dot(a, d1) + dot(a, d2) + dot(a, d3) + dot(b, d1) + dot(b, d2) + dot(c, d1)


def x_forward(m_ref, f_ref, s_ref, slot):
    groups, width, lanes = f_ref.shape[0], f_ref.shape[1], f_ref.shape[-1]
    batch = lanes // X_GROUP
    halves = range(f_ref.shape[4])
    rights = []
    for h in halves:
        rows = []
        for g in range(groups):
            for x in range(X_GROUP):
                for p in range(2):
                    rows.append(jnp.concatenate([f_ref[g, c, 0, p, h, :, x * batch:(x + 1) * batch] for c in range(width)], -1))
        rights.append(jnp.concatenate(rows, 0))
    for h in halves:
        out = split_dot((m_ref[0], m_ref[1], m_ref[2]), rights[h])
        s_ref[:, slot, :, h * SUB:(h + 1) * SUB, :] = out.reshape(s_ref.shape[0], 2, SUB, width * batch)


def x_inverse(m_ref, t_ref, slot, s_ref):
    groups, width, lanes = s_ref.shape[0], s_ref.shape[2], s_ref.shape[-1]
    batch = lanes // X_GROUP
    halves = range(s_ref.shape[5])
    outs = []
    for h in halves:
        right = t_ref[:, slot, :, h * SUB:(h + 1) * SUB, :].reshape(t_ref.shape[0] * 2 * SUB, width * batch)
        outs.append(split_dot((m_ref[0], m_ref[1], m_ref[2]), right).reshape(groups, X_GROUP, 2, SUB, width * batch))
    for h in halves:
        for g in range(groups):
            for p in range(2):
                for c in range(width):
                    row = jnp.concatenate([outs[h][g, x, p, :, c * batch:(c + 1) * batch] for x in range(X_GROUP)], -1)
                    for i, d in enumerate(split3(row)):
                        s_ref[g, i, c, 0, p, h] = d


def mix(s_ref, re_w, im_w, t_ref, to, half, rows, re_rows, im_rows, re_s, im_s, re_t, im_t):
    own, slots, _, n_ky, lanes = s_ref.shape
    width = re_w.shape[2]
    batch = lanes // width
    some = slots // 2
    part_modes = some * n_ky
    pick = slice(half * some, (half + 1) * some)

    for w_ref, out in ((re_w, re_rows), (im_w, im_rows)):
        def lay(c, _):
            for k in range(own):
                for ky in range(n_ky):
                    at = (k * n_ky + ky) * SUB
                    rows[at:at + SUB, 0:width] = w_ref[k, ky, c]
            mat = jnp.concatenate([rows[pl.ds((k * n_ky + h * SUB) * SUB + kz, SUB, stride=SUB), :]
                                   for k in range(own) for kz in KZ_ORDER[pick] for h in range(n_ky // SUB)], 0)
            out[c] = mat.T[0:out.shape[1]]
            return 0
        lax.fori_loop(0, width, lay, 0)
    for p, out in enumerate((re_s, im_s)):
        out[...] = jnp.concatenate([s_ref[k, pick, p].reshape(part_modes, lanes) for k in range(own)], 0).T
    pair = 2

    def outputs(i, _):
        d = i * pair

        def inner(c, acc):
            at = pl.ds(pl.multiple_of(c * batch, SUB), batch)
            a, b = re_s[at, :], im_s[at, :]
            new = []
            for u in range(pair):
                p = jnp.broadcast_to(re_rows[c, pl.ds(d + u, 1), :], a.shape)
                q = jnp.broadcast_to(im_rows[c, pl.ds(d + u, 1), :], a.shape)
                new += [acc[2 * u] + (a * p - b * q), acc[2 * u + 1] + (a * q + b * p)]
            return tuple(new)
        zero = jnp.zeros((batch, own * part_modes), F32)
        acc = lax.fori_loop(0, width, inner, (zero,) * (2 * pair))
        for u in range(pair):
            at = pl.ds(pl.multiple_of((d + u) * batch, SUB), batch)
            re_t[at, :] = acc[2 * u]
            im_t[at, :] = acc[2 * u + 1]
        return 0
    lax.fori_loop(0, width // pair, outputs, 0)
    for p, got in enumerate((re_t, im_t)):
        back = got[...].T
        for k in range(own):
            t_ref[to[k], pick, p] = back[k * part_modes:(k + 1) * part_modes].reshape(some, n_ky, lanes)


class Place:
    def __init__(self):
        xs, ys = lax.axis_index('xs'), lax.axis_index('ys')
        data = lax.axis_index('data')
        c, x, y = xs % 2, xs // 2, ys
        self.core = (data, ys, 2 * x + 1 - c)
        self.x_chip = (data, ys, 2 * (1 - x) + c)
        self.y_chip = (data, 1 - ys, xs)
        p, q = lambda a, b: 2 * a + b, lambda a, b: 4 + 2 * a + b
        self.mine = SUB * c
        self.order = (p(1 - x, 1 - y), q(1 - y, 1 - x), p(1 - x, y), q(1 - y, x),
                      p(x, 1 - y), q(y, 1 - x), p(x, y), q(y, x))

    def enter(self):
        barrier = pltpu.get_barrier_semaphore()
        for device in (self.core, self.x_chip, self.y_chip):
            pl.semaphore_signal(barrier, inc=1, device_id=device, device_id_type=pl.DeviceIdType.MESH)
        pl.semaphore_wait(barrier, 3)


def remote(src, dst, send, recv, device):
    return pltpu.make_async_remote_copy(src_ref=src, dst_ref=dst, send_sem=send, recv_sem=recv, device_id=device,
                                        device_id_type=pl.DeviceIdType.MESH)


def half_slots(ref, k, half):
    some = ref.shape[1] // 2
    return ref.at[k, pl.ds(half * some, some)]


def reduce_kernel(first, m_ref, f_ref, x_ref, w_ref, out_ref, p_ref, s_ref, r1, r2, r3,
                  send1, recv1, send2, recv2, send3, recv3):
    me = Place()
    step, last = pl.program_id(0), pl.num_programs(0) - 1
    one, two, three = [], [], []
    for h in range(2):
        mine = [half_slots(s_ref, k, h) for k in me.order]
        one.append([remote(half_slots(s_ref, SUB + me.order[t], h), half_slots(r1, t, h), send1.at[h, t], recv1.at[h, t], me.core)
                    for t in range(SUB)])
        two.append([remote(mine[t], half_slots(r2, t, h), send2.at[h, t], recv2.at[h, t], (me.x_chip, me.y_chip)[t % 2])
                    for t in range(4)])
        three.append([remote(mine[4 + t], half_slots(r3, t, h), send3.at[h, t], recv3.at[h, t], (me.y_chip, me.x_chip)[t])
                      for t in range(2)])

    def add(dst, a, b):
        def row(i, _):
            dst[i] = a[i] + b[i]
            return 0
        lax.fori_loop(0, dst.shape[0], row, 0)

    def from_core(h):
        for t in range(SUB):
            one[h][t].wait_recv()
            to = half_slots(s_ref, me.order[t], h)
            add(to, to, half_slots(r1, t, h))
            if t < 4:
                two[h][t].start()

    def from_chip(h, these):
        for t in these:
            two[h][t].wait_recv()
            to = half_slots(s_ref, me.order[4 + t], h)
            add(to, to, half_slots(r2, t, h))
            if t < 2:
                three[h][t].start()

    def finish(h):
        from_chip(h, (2, 3))
        for t in range(2):
            three[h][t].wait_recv()
            add(half_slots(out_ref, t, h), half_slots(s_ref, me.order[6 + t], h), half_slots(r3, t, h))

    def send_core(h):
        for copy in one[h]:
            copy.start()

    slots = s_ref.shape[1]
    events = ((0, me.enter), (slots // 2, lambda: send_core(0)), (slots // 2 + 1, lambda: from_core(0)),
              (slots - 1, lambda: from_chip(0, (0, 1))), (slots, lambda: send_core(1)), (slots + 2, lambda: from_core(1)),
              (slots + 4, lambda: finish(0)), (slots + 6, lambda: from_chip(1, (0, 1))))
    for at, event in events:
        pl.when(step == at)(event)

    @pl.when(step < slots)
    def _():
        x_forward(m_ref, f_ref, s_ref, step)

    @pl.when(step >= slots // 2)
    def _():
        channel_product(first, x_ref, w_ref, p_ref.at[0])

    @pl.when(step == last)
    def _():
        finish(1)
        for h in range(2):
            for copy in one[h] + two[h] + three[h]:
                copy.wait_send()


def gather_kernel(first, layer, m_ref, s_ref, re_hbm, im_hbm, x_ref, w_ref, p_in, parts_ref, p_ref, t_ref,
                  re_w, im_w, rows, re_rows, im_rows, re_s, im_s, re_t, im_t, w_sem, send, recv):
    me = Place()
    step, last = pl.program_id(0), pl.num_programs(0) - 1
    p3, q3, p2, q2, p1, q1, p0, q0 = me.order
    plan = [(p0, me.y_chip, 0), (q0, me.x_chip, 0), (p0, me.x_chip, 0), (q0, me.y_chip, 0), (p0, me.core, SUB), (q0, me.core, SUB),
            (p1, me.x_chip, 0), (q1, me.y_chip, 0)] + [(k, me.core, SUB) for k in (p1, q1, p2, q2, p3, q3)]
    copies = [[remote(half_slots(t_ref, k, h), half_slots(t_ref, k + up, h), send.at[h, n], recv.at[h, n], device)
               for n, (k, device, up) in enumerate(plan)] for h in range(2)]
    weights = [pltpu.make_async_copy(hbm.at[layer, me.mine + k], to.at[i], w_sem.at[n, i])
               for n, (hbm, to) in enumerate(((re_hbm, re_w), (im_hbm, im_w))) for i, k in enumerate((p0, q0))]

    def mix_half(h):
        mix(s_ref, re_w, im_w, t_ref, (p0, q0), h, rows, re_rows, im_rows, re_s, im_s, re_t, im_t)
        for copy in copies[h][:6]:
            copy.start()

    def begin():
        for copy in weights:
            copy.start()
        me.enter()
        for copy in weights:
            copy.wait()
        mix_half(0)

    def pass_on(h):
        for n in range(2):
            copies[h][n].wait_recv()
            copies[h][6 + n].start()
        for n in range(2):
            copies[h][SUB + n].start()

    def finish(h):
        for n, arrived in enumerate((2, 3, 6, 7)):
            copies[h][arrived].wait_recv()
            copies[h][10 + n].start()
        for n in (4, 5, *range(SUB, len(plan))):
            copies[h][n].wait_recv()

    slots = t_ref.shape[1]
    x_from = last + 1 - slots
    for at, event in ((0, begin), (1, lambda: mix_half(1)), (3, lambda: pass_on(0)), (x_from - 2, lambda: pass_on(1)),
                      (x_from, lambda: finish(0)), (x_from + slots // 2, lambda: finish(1))):
        pl.when(step == at)(event)

    @pl.when(step >= 2)
    def _():
        channel_product(first, x_ref, w_ref, p_ref.at[0])

    @pl.when(step >= x_from)
    def _():
        x_inverse(m_ref, t_ref, step - x_from, parts_ref)

    @pl.when(step == last)
    def _():
        for h in range(2):
            for copy in copies[h]:
                copy.wait_send()


def block(shape, index, slot=None, **kwargs):
    def index_map(*at):
        return tuple(0 if k == 'o' else slot(at[0]) if k == 's' else at['ij'.index(k)] for k in index)
    return pl.BlockSpec(shape, index_map, **kwargs)


def bf16_addends(table):
    out = []
    for _ in range(3):
        out.append(lax.reduce_precision(table, exponent_bits=SUB, mantissa_bits=7))
        table = table - out[-1]
    return jnp.stack(out).astype(BF16)


def solution(mesh):
    row_devs, col_devs = mesh.shape['ys'], mesh.shape['xs']

    def local_layers(field, spec_real, spec_imag, mix_weight, bias):
        batch, x_loc, y_loc, grid_z, width = field.shape
        modes = spec_real.shape[3]
        grid_x, grid_y = x_loc * col_devs, y_loc * row_devs
        groups, blocks = x_loc // X_GROUP, y_loc // Y_BLOCK
        lanes = X_GROUP * batch
        kx, ky = kept(modes, grid_x), kept(modes, grid_y)
        n_kx, n_ky = len(kx), len(ky)
        x_index, y_index = lax.axis_index('xs'), lax.axis_index('ys')
        fwd_np, inv_np = all_tables(blocks, ky, grid_y, grid_z, grid_x * grid_y * grid_z)
        fwd, inv = [jnp.asarray(t) for t in fwd_np], [jnp.asarray(t) for t in inv_np]

        turn = 2.0 * math.pi * (kx[:, None] * np.arange(grid_x)[None, :] % grid_x) / grid_x
        cos, sin = np.cos(turn), np.sin(turn)
        fwd_x = np.stack([np.stack([cos, sin], -1), np.stack([-sin, cos], -1)], 1)
        inv_x = np.transpose(fwd_x, (2, 3, 0, 1))
        fwd_x = fwd_x.reshape(n_kx, 2, col_devs, x_loc, 2).transpose(2, 0, 1, 3, 4).reshape(col_devs, 2 * n_kx, 2 * x_loc)
        inv_x = inv_x.reshape(col_devs, 2 * x_loc, 2 * n_kx)
        odd = (jnp.arange(16 * x_loc) % 2 * y_index)[:, None]

        core, x_chip = x_index % 2, x_index // 2

        def x_table(tables, axis):
            wide = np.kron(tables, np.eye(SUB)).astype(np.float32)
            t = lax.dynamic_index_in_dim(jnp.asarray(wide), x_index, 0, keepdims=False)
            t = jnp.where(core == 1, jnp.roll(t, SUB * n_kx, axis), t)
            return bf16_addends(jnp.where(odd == 1, -t, t))
        fwd_x, inv_x = x_table(fwd_x, 0), x_table(inv_x, 1)
        eye = jnp.eye(Z_BLOCK, dtype=F32)
        def point_table(layer):
            w = bf16_addends((0.5 * mix_weight[layer].T[:, None, :, None] * eye[None, :, None, :]).reshape(width * SUB, width * SUB))
            b = bf16_addends(jnp.broadcast_to(0.5 * bias[layer][:, None], (width, SUB)).reshape(width * SUB))
            b = jnp.pad(jnp.stack([b.T, 0 * b.T, 0 * b.T]), ((0, 0), (0, 0), (0, 2 * SUB - 3)))
            return jnp.concatenate([w, b], -1)
        point_w = [point_table(layer) for layer in range(2)]

        real_w, imag_w = (jnp.swapaxes(w, 3, 4) for w in (spec_real, spec_imag))
        v = jnp.swapaxes(jnp.moveaxis(field, 0, -1), 2, 3)
        grid = (groups, blocks)
        params = pltpu.CompilerParams(vmem_limit_bytes=VMEM_LIMIT)
        one = pl.Buffered(1)
        spec_shape = jax.ShapeDtypeStruct((groups, width, 256, lanes), F32)
        in_block = block((X_GROUP, Y_BLOCK, width, grid_z, batch), 'ijooo')
        mid_block = block((1, Y_BLOCK, width, grid_z, lanes), 'ijooo')
        part_block = block((1, 3, width, 256, lanes), 'ioooo', pipeline_mode=one)
        mid_shape = jax.ShapeDtypeStruct((groups, y_loc, width, grid_z, lanes), F32)
        anywhere = pl.BlockSpec(memory_space=pl.ANY)

        def stage(unit):
            return pltpu.VMEM((unit[1] // unit[0], 5, Y_BLOCK * SUB, unit[0] * lanes), F32)
        w_block = block((3, width * SUB, width * SUB + 2 * SUB), 'ooo')

        units = y_loc // HALF_BLOCK

        def half_block(first, half, start):
            shape = (HALF_BLOCK, width, grid_z) + ((batch,) if first else (lanes,))
            return pl.BlockSpec((X_GROUP if first else 1,) + shape,
                                lambda j: (half, jnp.clip(j - start, 0, units - 1), 0, 0, 0))

        def table_specs(tables):
            return [block((1,) + t.shape[1:], 'joo') for t in tables]

        f = pl.pallas_call(
            functools.partial(forward_kernel, FORWARD_UNIT), grid=grid, out_shape=spec_shape,
            in_specs=[in_block] + table_specs(fwd),
            out_specs=block((1, width, 256, lanes), 'iooo'),
            scratch_shapes=[stage(FORWARD_UNIT)], compiler_params=params, name='forward')(v, *fwd)

        own, slots, halves = 2, SUB, n_ky // SUB
        unit = (slots, 2, n_ky, width * batch)
        own_block = block((own,) + unit, 'ooooo')
        x_block = block((3, 16 * x_loc, 16 * x_loc), 'ooo')
        dma = pltpu.SemaphoreType.DMA

        def exchange(number):
            return pltpu.CompilerParams(vmem_limit_bytes=VMEM_LIMIT, collective_id=number, has_side_effects=True)

        def across(f, layer, source):
            first = layer == 0
            s, p = pl.pallas_call(
                functools.partial(reduce_kernel, first), grid=(slots // 2 + units,),
                out_shape=(jax.ShapeDtypeStruct((own,) + unit, F32), mid_shape),
                in_specs=[x_block,
                          block((groups, width, 1, 2, halves, SUB, lanes), 'oosoooo', lambda j: jnp.minimum(j, slots - 1)),
                          half_block(first, 0, slots // 2), w_block],
                out_specs=(own_block, half_block(False, 0, slots // 2)),
                scratch_shapes=[pltpu.VMEM((n,) + unit, F32) for n in (n_kx, SUB, 4, 2)]
                + [dma((2, n)) for n in (SUB, SUB, 4, 4, 2, 2)],
                compiler_params=exchange(2 * layer), name='reduce')(
                    fwd_x, f.reshape(groups, width, slots, 2, halves, SUB, lanes), source, point_w[layer])
            x_from = units + 2 - slots
            parts, p = pl.pallas_call(
                functools.partial(gather_kernel, first, layer), grid=(units + 2,),
                out_shape=(jax.ShapeDtypeStruct((groups, 3, width, slots, 2, halves, SUB, lanes), BF16), mid_shape),
                in_specs=[x_block, own_block, anywhere, anywhere, half_block(first, 1, 2), w_block, anywhere],
                out_specs=(block((groups, 3, width, 1, 2, halves, SUB, lanes), 'ooosoooo', lambda j: jnp.maximum(j - x_from, 0)),
                           half_block(False, 1, 2)),
                input_output_aliases={6: 1},
                scratch_shapes=[pltpu.VMEM((n_kx,) + unit, F32)]
                + [pltpu.VMEM((own, n_ky, width, SUB, width), F32)] * 2
                + [pltpu.VMEM((own * n_ky * SUB, LANES), F32)] + [pltpu.VMEM((width, 24, LANES), F32)] * 2
                + [pltpu.VMEM((width * batch, own * slots * n_ky // 2), F32)] * 4
                + [dma((2, 2)), dma((2, 14)), dma((2, 14))],
                compiler_params=exchange(2 * layer + 1), name='gather')(
                    inv_x, s, real_w, imag_w, source, point_w[layer], p)
            return parts.reshape(groups, 3, width, CLASS_ROWS[-1], lanes), p

        parts, p = across(f, 0, v)
        v1, f = pl.pallas_call(
            functools.partial(layer_kernel, FIRST_UNIT, True), grid=grid, out_shape=(mid_shape, spec_shape),
            in_specs=[mid_block, part_block] + table_specs(inv) + table_specs(fwd),
            out_specs=(mid_block, anywhere),
            scratch_shapes=[stage(FIRST_UNIT)] * 2 + [pltpu.VMEM((width, 256, lanes), F32), pltpu.SemaphoreType.DMA],
            compiler_params=params, name='layer_first')(p, parts, *inv, *fwd)
        parts, p = across(f, 1, v1)
        out = pl.pallas_call(
            functools.partial(layer_kernel, LAST_UNIT, False), grid=grid,
            out_shape=jax.ShapeDtypeStruct((x_loc, y_loc, width, grid_z, batch), F32),
            in_specs=[mid_block, part_block] + table_specs(inv), out_specs=in_block, scratch_shapes=[stage(LAST_UNIT)],
            compiler_params=params, name='layer_last')(p, parts, *inv)
        return jnp.moveaxis(jnp.swapaxes(out, 2, 3), -1, 0)

    field_spec = P('data', 'xs', 'ys', None, None)
    return jax.shard_map(local_layers, mesh=mesh, in_specs=(field_spec, P(), P(), P(), P()), out_specs=field_spec, check_vma=False)
```

time: 829 us -> 809 us (0.976)
  Pallas kernels: 817 us -> 796 us
    pallas_call x10 -> x4, Pallas kernels: 491 us -> 469 us  [the longest x2 272 us: across(): pl.pallas_call(functools.partial(gather_kernel, first, layer), grid=(unit...]
where the time goes in v4:
time: 809 us; the launch traced here: 808 us
  Pallas kernels  796 us (98%)
    pallas_call x2, Pallas kernels, across(): pl.pallas_call(functools.partial(gather_kernel, first, layer), grid=(unit...  272 us
    pallas_call x2, Pallas kernels, across(): pl.pallas_call(functools.partial(reduce_kernel, first), grid=(slots // 2...  197 us
    pallas_call x1, Pallas kernels, local_layers(): pl.pallas_call(functools.partial(layer_kernel, FIRST_UNIT, True), grid=gr...  129 us
    pallas_call x1, Pallas kernels, local_layers(): pl.pallas_call(functools.partial(layer_kernel, LAST_UNIT, False), grid=gr...  114 us
    pallas_call x1, Pallas kernels, local_layers(): pl.pallas_call(functools.partial(forward_kernel, FORWARD_UNIT), grid=grid...  83.8 us

profile of v4, /device:TPU:0, one launch (start us, length us, event | category | flops | bytes accessed | tf_op | source)
XLA Modules:
  0.0 808.2 jit_solution(8817898661308428692)
XLA Ops:
  0.0 0.8 multiply_bitcast_fusion
  0.8 0.1 broadcast_in_dim.28
  0.8 0.1 reshape.312
  1.0 0.1 broadcast_in_dim.16
  1.1 0.1 reshape.309
  1.2 0.8 fusion.25
  2.1 0.1 copy.32
  2.2 0.1 copy.29
  2.3 0.2 copy.30
  2.4 0.2 copy.33
  2.6 1.0 constant_dynamic-slice_fusion.1
  3.6 1.0 dynamic-slice_bitcast_fusion
  4.6 1.2 reduce-precision_convert_fusion.1
  5.9 1.0 pad_maximum_fusion
  6.8 1.6 broadcast_multiply_fusion
  8.4 2.0 mul.141
  10.5 0.8 fusion.7.w_ref
  11.3 0.5 mul.132
  11.8 0.8 fusion.6.w_ref
  12.6 83.8 %forward.1 = f32[2,20,256,384]{3,2,1,0:T(8,128)} custom-call(f32[16,32,20,40,48]{4,3,2,1,0:T(8,128)} %bitcast.3.x_ref, bf16[8,64,192]{2,1,0:T(8,128)(2,1)} %constant.67.clone.t0.refs_7_, bf16[8,192,256]{2,1,0:T(8,128)(2,1)} %constant.68.clone.t1.refs_8_, bf16[8,192,256]{2,1,0:T(8,128)(2,1)} %constant.69.clone.t2.refs_9_), custom_call_target="tpu_custom_call" | custom-call | tf_op jit(solution)/shard_map/forward/pallas_call | solution.py:643
  96.4 105.1 %reduce.2 = (f32[2,8,2,16,960]{4,3,2,1,0:T(8,128)}, f32[2,32,20,40,384]{4,3,2,1,0:T(8,128)}) custom-call(bf16[3,256,256]{2,1,0:T(8,128)(2,1)} %get-tuple-element.57.m_ref, f32[2,20,8,2,2,8,384]{6,5,4,3,2,1,0:T(8,128)} %bitcast.48, f32[16,32,20,40,48]{4,3,2,1,0:T(8,128)} %bitcast.3.x_ref, bf16[3,160,176]{2,1,0:T(8,128)(2,1)} %fusion.6.w_ref), custom_call_target="tpu_custom_call" | custom-call | tf_op jit(solution)/shard_map/reduce/pallas_call | solution.py:660
  201.6 140.8 %gather.2 = (bf16[2,3,20,8,2,2,8,384]{7,6,5,4,3,2,1,0:T(8,128)(2,1)}, f32[2,32,20,40,384]{4,3,2,1,0:T(8,128)}) custom-call(bf16[3,256,256]{2,1,0:T(8,128)(2,1)} %get-tuple-element.56.m_ref, f32[2,8,2,16,960]{4,3,2,1,0:T(8,128)} %get-tuple-element.15.s_ref, f32[2,16,16,20,8,20]{5,4,3,2,1,0:T(8,128)} %bitcast.44, ...), custom_call_target="tpu_custom_call", output_to_operand_aliasing={{1}: (6, {})} | custom-call | tf_op jit(solution)/shard_map/gather/pallas_call | solution.py:672
  342.3 128.5 %layer_first.1 = (f32[2,32,20,40,384]{4,3,2,1,0:T(8,128)}, f32[2,20,256,384]{3,2,1,0:T(8,128)}) custom-call(f32[2,32,20,40,384]{4,3,2,1,0:T(8,128)} %get-tuple-element.17.refs_0_, bf16[2,3,20,256,384]{4,3,2,1,0:T(8,128)(2,1)} %bitcast.50, bf16[8,96,192]{2,1,0:T(8,128)(2,1)} %constant.70.clone.refs_2_, bf16[8,128,192]{2,1,0:T(8,128)(2,1)} %constant.71.clone.refs_3_, ...), custom_call_target="tpu_custom_call" | custom-call | tf_op jit(solution)/shard_map/layer_first/pallas_call | solution.py:689
  470.9 92.0 %reduce.3 = (f32[2,8,2,16,960]{4,3,2,1,0:T(8,128)}, f32[2,32,20,40,384]{4,3,2,1,0:T(8,128)}) custom-call(bf16[3,256,256]{2,1,0:T(8,128)(2,1)} %get-tuple-element.57.m_ref, f32[2,20,8,2,2,8,384]{6,5,4,3,2,1,0:T(8,128)} %bitcast.51, f32[2,32,20,40,384]{4,3,2,1,0:T(8,128)} %get-tuple-element.20.x_ref, bf16[3,160,176]{2,1,0:T(8,128)(2,1)} %fusion.7.w_ref), custom_call_target="tpu_custom_call" | custom-call | tf_op jit(solution)/shard_map/reduce/pallas_call | solution.py:660
  562.9 131.3 %gather.3 = (bf16[2,3,20,8,2,2,8,384]{7,6,5,4,3,2,1,0:T(8,128)(2,1)}, f32[2,32,20,40,384]{4,3,2,1,0:T(8,128)}) custom-call(bf16[3,256,256]{2,1,0:T(8,128)(2,1)} %get-tuple-element.56.m_ref, f32[2,8,2,16,960]{4,3,2,1,0:T(8,128)} %get-tuple-element.21.s_ref, f32[2,16,16,20,8,20]{5,4,3,2,1,0:T(8,128)} %bitcast.45, ...), custom_call_target="tpu_custom_call", output_to_operand_aliasing={{1}: (6, {})} | custom-call | tf_op jit(solution)/shard_map/gather/pallas_call | solution.py:672
  694.2 114.1 %layer_last.1 = f32[16,32,20,40,48]{4,3,2,1,0:T(8,128)} custom-call(f32[2,32,20,40,384]{4,3,2,1,0:T(8,128)} %get-tuple-element.23.refs_0_, bf16[2,3,20,256,384]{4,3,2,1,0:T(8,128)(2,1)} %bitcast.49, bf16[8,96,192]{2,1,0:T(8,128)(2,1)} %constant.70.clone.refs_2_, bf16[8,128,192]{2,1,0:T(8,128)(2,1)} %constant.71.clone.refs_3_, ...), custom_call_target="tpu_custom_call" | custom-call | tf_op jit(solution)/shard_map/layer_last/pallas_call | solution.py:696
  (14 shorter events, 0.2 us)

commit v5 on v4

--- a/solution.py
+++ b/solution.py
@@ -23,6 +23,7 @@
 KZ_ORDER = tuple(kz for group in KZ_CLASS for kz in group)
 CLASS_ROWS = (0, 64, 160, 256)
 LANES = 128
+ADDENDS = 3
 FORWARD_UNIT = (2, 10)
 FIRST_UNIT = (2, 10)
 LAST_UNIT = (1, 10)
@@ -42,7 +43,7 @@
 def pieces(table):
     rest = np.asarray(table, np.float32)
     out = []
-    for _ in range(3):
+    for _ in range(ADDENDS):
         out.append(rest.astype(ml_dtypes.bfloat16))
         rest = rest - out[-1].astype(np.float32)
     return out
@@ -133,7 +134,7 @@
     for k in channels:
         for r in range(0, rows, 2 * SUB):
             cells = [split3(u_ref[k, r:r + 2 * SUB, lane:lane + LANES]) for lane in range(0, lanes, LANES)]
-            for i in range(3):
+            for i in range(ADDENDS):
                 out[i].append(jnp.concatenate([cell[i] for cell in cells], -1))
     return [jnp.concatenate(rows, 0) for rows in out]
 
@@ -161,11 +162,11 @@
 
     def part(i, k):
         return jnp.concatenate([s_ref[0, i, c + u, CLASS_ROWS[k]:CLASS_ROWS[k + 1]] for u in range(pair)], -1)
-    o = dot(tables[0], jnp.concatenate([part(i, 0) for i in range(3)], 0))
+    o = dot(tables[0], jnp.concatenate([part(i, 0) for i in range(ADDENDS)], 0))
     for r, lane, v in add_tiles(o, n, lanes):
         u_ref[0, r:r + SUB, lane:lane + LANES] = v
     for k in (1, 2):
-        d1, d2, d3 = (part(i, k) for i in range(3))
+        d1, d2, d3 = (part(i, k) for i in range(ADDENDS))
         o = jnp.concatenate([dot(tables[2 * k - 1], jnp.concatenate([d1, d2], 0)),
                              dot(tables[2 * k], jnp.concatenate([d1, d3], 0))], 0)
         for r, lane, v in add_tiles(o, 2 * n, lanes):
@@ -224,24 +225,31 @@
     lax.fori_loop(0, width // per_step, body, 0)
 
 
-def channel_product(first, x_ref, w_ref, p_ref):
+def channel_product(first, x_ref, w_ref, p_ref, d_ref):
     blocks, width, depth, lanes = p_ref.shape
     rows = width * SUB
-    ones = jnp.ones((w_ref.shape[2] - rows, lanes), BF16)
-    full, (a, b, c) = w_ref[0], (w_ref[i, :, :rows] for i in range(3))
-
-    def z_block(j, _):
-        z = pl.ds(pl.multiple_of(j * SUB, SUB), SUB)
+    ones = jnp.ones((w_ref.shape[2] - rows, blocks * lanes), BF16)
+    full, (a, b, c) = w_ref[0], (w_ref[i, :, :rows] for i in range(ADDENDS))
+
+    def load(j):
+        z = slice(j * SUB, (j + 1) * SUB)
+        if first:
+            v = [x_ref[x, y, :, z, :] for y in range(blocks) for x in range(X_GROUP)]
+        else:
+            v = [x_ref[0, y, :, z, :] for y in range(blocks)]
+        d_ref[j % 2] = jnp.concatenate(v, -1).reshape(rows, blocks * lanes)
+
+    def product(j):
+        d1, d2, d3 = split3(d_ref[j % 2])
+        p = dot(full, jnp.concatenate([d1, ones], 0)) + dot(a, d2) + dot(a, d3) + dot(b, d1) + dot(b, d2) + dot(c, d1)
         for y in range(blocks):
-            if first:
-                v = jnp.concatenate([x_ref[x, y, :, z, :] for x in range(X_GROUP)], -1)
-            else:
-                v = x_ref[0, y, :, z, :]
-            d1, d2, d3 = split3(v.reshape(rows, lanes))
-            p = dot(full, jnp.concatenate([d1, ones], 0)) + dot(a, d2) + dot(a, d3) + dot(b, d1) + dot(b, d2) + dot(c, d1)
-            p_ref[y, :, z, :] = p.reshape(width, SUB, lanes)
-        return 0
-    lax.fori_loop(0, depth // SUB, z_block, 0)
+            p_ref[y, :, j * SUB:(j + 1) * SUB, :] = p[:, y * lanes:(y + 1) * lanes].reshape(width, SUB, lanes)
+    count = depth // SUB
+    for j in range(count + 1):
+        if j < count:
+            load(j)
+        if j:
+            product(j - 1)
 
 
 def layer_kernel(unit, first, *refs):
@@ -432,15 +440,18 @@
     return ref.at[k, pl.ds(half * some, some)]
 
 
-def reduce_kernel(first, m_ref, f_ref, x_ref, w_ref, out_ref, p_ref, s_ref, r1, r2, r3,
+def reduce_kernel(first, m_ref, f_ref, x_ref, w_ref, out_ref, p_ref, d_ref, s_ref, r1, r2, r3,
                   send1, recv1, send2, recv2, send3, recv3):
     me = Place()
     step, last = pl.program_id(0), pl.num_programs(0) - 1
-    one, two, three = [], [], []
+    slots = s_ref.shape[1]
+    two, three = [], []
+
+    def to_core(slot):
+        return [remote(s_ref.at[SUB + me.order[t], slot], r1.at[t, slot], send1.at[slot, t], recv1.at[slot, t], me.core)
+                for t in range(SUB)]
     for h in range(2):
         mine = [half_slots(s_ref, k, h) for k in me.order]
-        one.append([remote(half_slots(s_ref, SUB + me.order[t], h), half_slots(r1, t, h), send1.at[h, t], recv1.at[h, t], me.core)
-                    for t in range(SUB)])
         two.append([remote(mine[t], half_slots(r2, t, h), send2.at[h, t], recv2.at[h, t], (me.x_chip, me.y_chip)[t % 2])
                     for t in range(4)])
         three.append([remote(mine[4 + t], half_slots(r3, t, h), send3.at[h, t], recv3.at[h, t], (me.y_chip, me.x_chip)[t])
@@ -453,8 +464,10 @@
         lax.fori_loop(0, dst.shape[0], row, 0)
 
     def from_core(h):
+        arriving = [to_core(slot) for slot in range(h * slots // 2, (h + 1) * slots // 2)]
         for t in range(SUB):
-            one[h][t].wait_recv()
+            for copies in arriving:
+                copies[t].wait_recv()
             to = half_slots(s_ref, me.order[t], h)
             add(to, to, half_slots(r1, t, h))
             if t < 4:
@@ -474,34 +487,34 @@
             three[h][t].wait_recv()
             add(half_slots(out_ref, t, h), half_slots(s_ref, me.order[6 + t], h), half_slots(r3, t, h))
 
-    def send_core(h):
-        for copy in one[h]:
-            copy.start()
-
-    slots = s_ref.shape[1]
-    events = ((0, me.enter), (slots // 2, lambda: send_core(0)), (slots // 2 + 1, lambda: from_core(0)),
-              (slots - 1, lambda: from_chip(0, (0, 1))), (slots, lambda: send_core(1)), (slots + 2, lambda: from_core(1)),
-              (slots + 4, lambda: finish(0)), (slots + 6, lambda: from_chip(1, (0, 1))))
+    events = ((0, me.enter), (slots // 2, lambda: from_core(0)), (slots - 1, lambda: from_chip(0, (0, 1))),
+              (slots + 1, lambda: from_core(1)), (slots + 3, lambda: finish(0)), (slots + 5, lambda: from_chip(1, (0, 1))))
     for at, event in events:
         pl.when(step == at)(event)
 
     @pl.when(step < slots)
     def _():
         x_forward(m_ref, f_ref, s_ref, step)
+        for copy in to_core(step):
+            copy.start()
 
     @pl.when(step >= slots // 2)
     def _():
-        channel_product(first, x_ref, w_ref, p_ref.at[0])
+        channel_product(first, x_ref, w_ref, p_ref.at[0], d_ref)
 
     @pl.when(step == last)
     def _():
         finish(1)
-        for h in range(2):
-            for copy in one[h] + two[h] + three[h]:
+        for copies in [to_core(slot) for slot in range(slots)] + two + three:
+            for copy in copies:
                 copy.wait_send()
 
 
-def gather_kernel(first, layer, m_ref, s_ref, re_hbm, im_hbm, x_ref, w_ref, p_in, parts_ref, p_ref, t_ref,
+def gather_steps(units, half):
+    return 2 + units // 2, 2 + units
+
+
+def gather_kernel(first, layer, m_ref, s_ref, re_hbm, im_hbm, x_ref, w_ref, p_in, parts_ref, p_ref, d_ref, t_ref,
                   re_w, im_w, rows, re_rows, im_rows, re_s, im_s, re_t, im_t, w_sem, send, recv):
     me = Place()
     step, last = pl.program_id(0), pl.num_programs(0) - 1
@@ -515,6 +528,8 @@
 
     def mix_half(h):
         mix(s_ref, re_w, im_w, t_ref, (p0, q0), h, rows, re_rows, im_rows, re_s, im_s, re_t, im_t)
+        if h:
+            pass_on(0)
         for copy in copies[h][:6]:
             copy.start()
 
@@ -540,19 +555,23 @@
         for n in (4, 5, *range(SUB, len(plan))):
             copies[h][n].wait_recv()
 
-    slots = t_ref.shape[1]
-    x_from = last + 1 - slots
-    for at, event in ((0, begin), (1, lambda: mix_half(1)), (3, lambda: pass_on(0)), (x_from - 2, lambda: pass_on(1)),
-                      (x_from, lambda: finish(0)), (x_from + slots // 2, lambda: finish(1))):
+    half = t_ref.shape[1] // 2
+    x_from, x_then = gather_steps(last + 1 - 2 - half, half)
+    for at, event in ((0, begin), (1, lambda: mix_half(1)), (x_from, lambda: finish(0)), (x_from + 2, lambda: pass_on(1)),
+                      (x_then, lambda: finish(1))):
         pl.when(step == at)(event)
 
-    @pl.when(step >= 2)
+    @pl.when((step >= 2) & (step < x_then))
     def _():
-        channel_product(first, x_ref, w_ref, p_ref.at[0])
-
-    @pl.when(step >= x_from)
+        channel_product(first, x_ref, w_ref, p_ref.at[0], d_ref)
+
+    @pl.when((step >= x_from) & (step < x_from + half))
     def _():
         x_inverse(m_ref, t_ref, step - x_from, parts_ref)
+
+    @pl.when(step >= x_then)
+    def _():
+        x_inverse(m_ref, t_ref, step - x_then + half, parts_ref)
 
     @pl.when(step == last)
     def _():
@@ -569,7 +588,7 @@
 
 def bf16_addends(table):
     out = []
-    for _ in range(3):
+    for _ in range(ADDENDS):
         out.append(lax.reduce_precision(table, exponent_bits=SUB, mantissa_bits=7))
         table = table - out[-1]
     return jnp.stack(out).astype(BF16)
@@ -618,17 +637,16 @@
         v = jnp.swapaxes(jnp.moveaxis(field, 0, -1), 2, 3)
         grid = (groups, blocks)
         params = pltpu.CompilerParams(vmem_limit_bytes=VMEM_LIMIT)
-        one = pl.Buffered(1)
         spec_shape = jax.ShapeDtypeStruct((groups, width, 256, lanes), F32)
         in_block = block((X_GROUP, Y_BLOCK, width, grid_z, batch), 'ijooo')
         mid_block = block((1, Y_BLOCK, width, grid_z, lanes), 'ijooo')
-        part_block = block((1, 3, width, 256, lanes), 'ioooo', pipeline_mode=one)
+        part_block = block((1, ADDENDS, width, CLASS_ROWS[-1], lanes), 'ioooo')
         mid_shape = jax.ShapeDtypeStruct((groups, y_loc, width, grid_z, lanes), F32)
         anywhere = pl.BlockSpec(memory_space=pl.ANY)
 
         def stage(unit):
             return pltpu.VMEM((unit[1] // unit[0], 5, Y_BLOCK * SUB, unit[0] * lanes), F32)
-        w_block = block((3, width * SUB, width * SUB + 2 * SUB), 'ooo')
+        w_block = block((ADDENDS, width * SUB, width * SUB + 2 * SUB), 'ooo')
 
         units = y_loc // HALF_BLOCK
 
@@ -649,8 +667,9 @@
         own, slots, halves = 2, SUB, n_ky // SUB
         unit = (slots, 2, n_ky, width * batch)
         own_block = block((own,) + unit, 'ooooo')
-        x_block = block((3, 16 * x_loc, 16 * x_loc), 'ooo')
+        x_block = block((ADDENDS, 16 * x_loc, 16 * x_loc), 'ooo')
         dma = pltpu.SemaphoreType.DMA
+        half_rows = pltpu.VMEM((2, width * SUB, HALF_BLOCK * lanes), F32)
 
         def exchange(number):
             return pltpu.CompilerParams(vmem_limit_bytes=VMEM_LIMIT, collective_id=number, has_side_effects=True)
@@ -664,26 +683,29 @@
                           block((groups, width, 1, 2, halves, SUB, lanes), 'oosoooo', lambda j: jnp.minimum(j, slots - 1)),
                           half_block(first, 0, slots // 2), w_block],
                 out_specs=(own_block, half_block(False, 0, slots // 2)),
-                scratch_shapes=[pltpu.VMEM((n,) + unit, F32) for n in (n_kx, SUB, 4, 2)]
-                + [dma((2, n)) for n in (SUB, SUB, 4, 4, 2, 2)],
+                scratch_shapes=[half_rows] + [pltpu.VMEM((n,) + unit, F32) for n in (n_kx, SUB, 4, 2)]
+                + [dma((slots, SUB))] * 2 + [dma((2, n)) for n in (4, 4, 2, 2)],
                 compiler_params=exchange(2 * layer), name='reduce')(
                     fwd_x, f.reshape(groups, width, slots, 2, halves, SUB, lanes), source, point_w[layer])
-            x_from = units + 2 - slots
+            x_from, x_then = gather_steps(units, slots // 2)
+
+            def inverse_slot(j):
+                return jnp.where(j < x_then, jnp.clip(j - x_from, 0, slots // 2 - 1), j - x_then + slots // 2)
             parts, p = pl.pallas_call(
-                functools.partial(gather_kernel, first, layer), grid=(units + 2,),
-                out_shape=(jax.ShapeDtypeStruct((groups, 3, width, slots, 2, halves, SUB, lanes), BF16), mid_shape),
+                functools.partial(gather_kernel, first, layer), grid=(units + 2 + slots // 2,),
+                out_shape=(jax.ShapeDtypeStruct((groups, ADDENDS, width, slots, 2, halves, SUB, lanes), BF16), mid_shape),
                 in_specs=[x_block, own_block, anywhere, anywhere, half_block(first, 1, 2), w_block, anywhere],
-                out_specs=(block((groups, 3, width, 1, 2, halves, SUB, lanes), 'ooosoooo', lambda j: jnp.maximum(j - x_from, 0)),
+                out_specs=(block((groups, ADDENDS, width, 1, 2, halves, SUB, lanes), 'ooosoooo', inverse_slot),
                            half_block(False, 1, 2)),
                 input_output_aliases={6: 1},
-                scratch_shapes=[pltpu.VMEM((n_kx,) + unit, F32)]
+                scratch_shapes=[half_rows, pltpu.VMEM((n_kx,) + unit, F32)]
                 + [pltpu.VMEM((own, n_ky, width, SUB, width), F32)] * 2
                 + [pltpu.VMEM((own * n_ky * SUB, LANES), F32)] + [pltpu.VMEM((width, 24, LANES), F32)] * 2
                 + [pltpu.VMEM((width * batch, own * slots * n_ky // 2), F32)] * 4
                 + [dma((2, 2)), dma((2, 14)), dma((2, 14))],
                 compiler_params=exchange(2 * layer + 1), name='gather')(
                     inv_x, s, real_w, imag_w, source, point_w[layer], p)
-            return parts.reshape(groups, 3, width, CLASS_ROWS[-1], lanes), p
+            return parts.reshape(groups, ADDENDS, width, CLASS_ROWS[-1], lanes), p
 
         parts, p = across(f, 0, v)
         v1, f = pl.pallas_call(

time: 809 us -> 739 us (0.913); the launches traced: 808 us -> 724 us
  Pallas kernels: 796 us -> 711 us
    pallas_call x2, Pallas kernels: 272 us -> 211 us  [across(): pl.pallas_call(functools.partial(gather_kernel, first, layer), grid=(unit...]
    pallas_call x2, Pallas kernels: 197 us -> 180 us  [across(): pl.pallas_call(functools.partial(reduce_kernel, first), grid=(slots // 2...]
where the time goes in v5:
time: 739 us; the launch traced here: 724 us
  Pallas kernels  711 us (96%)
    pallas_call x2, Pallas kernels, across(): pl.pallas_call(functools.partial(gather_kernel, first, layer), grid=(unit...  211 us
    pallas_call x2, Pallas kernels, across(): pl.pallas_call(functools.partial(reduce_kernel, first), grid=(slots // 2...  180 us
    pallas_call x1, Pallas kernels, local_layers(): pl.pallas_call(functools.partial(layer_kernel, FIRST_UNIT, True), grid=gr...  122 us
    pallas_call x1, Pallas kernels, local_layers(): pl.pallas_call(functools.partial(layer_kernel, LAST_UNIT, False), grid=gr...  114 us
    pallas_call x1, Pallas kernels, local_layers(): pl.pallas_call(functools.partial(forward_kernel, FORWARD_UNIT), grid=grid...  83.8 us

profile of v5, /device:TPU:0, one launch (start us, length us, event | category | flops | bytes accessed | tf_op | source)
XLA Modules:
  0.0 724.2 jit_solution(9436997075494881917)
XLA Ops:
  0.0 0.8 multiply_bitcast_fusion
  0.8 0.1 broadcast_in_dim.28
  0.8 0.1 reshape.312
  1.0 0.1 broadcast_in_dim.16
  1.1 0.1 reshape.309
  1.2 0.8 fusion.25
  2.1 0.1 copy.32
  2.2 0.1 copy.29
  2.3 0.2 copy.30
  2.4 0.2 copy.33
  2.6 1.0 constant_dynamic-slice_fusion.1
  3.6 1.0 dynamic-slice_bitcast_fusion
  4.6 1.2 reduce-precision_convert_fusion.1
  5.9 1.0 pad_maximum_fusion
  6.8 1.6 broadcast_multiply_fusion
  8.4 2.0 mul.141
  10.5 0.8 fusion.7.w_ref
  11.3 0.5 mul.132
  11.8 0.8 fusion.6.w_ref
  12.6 83.8 %forward.1 = f32[2,20,256,384]{3,2,1,0:T(8,128)} custom-call(f32[16,32,20,40,48]{4,3,2,1,0:T(8,128)} %bitcast.3.x_ref, bf16[8,64,192]{2,1,0:T(8,128)(2,1)} %constant.67.clone.t0.refs_7_, bf16[8,192,256]{2,1,0:T(8,128)(2,1)} %constant.68.clone.t1.refs_8_, bf16[8,192,256]{2,1,0:T(8,128)(2,1)} %constant.69.clone.t2.refs_9_), custom_call_target="tpu_custom_call" | custom-call | tf_op jit(solution)/shard_map/forward/pallas_call | solution.py:661
  96.4 92.2 %reduce.2 = (f32[2,8,2,16,960]{4,3,2,1,0:T(8,128)}, f32[2,32,20,40,384]{4,3,2,1,0:T(8,128)}) custom-call(bf16[3,256,256]{2,1,0:T(8,128)(2,1)} %get-tuple-element.57.m_ref, f32[2,20,8,2,2,8,384]{6,5,4,3,2,1,0:T(8,128)} %bitcast.48, f32[16,32,20,40,48]{4,3,2,1,0:T(8,128)} %bitcast.3.x_ref, bf16[3,160,176]{2,1,0:T(8,128)(2,1)} %fusion.6.w_ref), custom_call_target="tpu_custom_call" | custom-call | tf_op jit(solution)/shard_map/reduce/pallas_call | solution.py:679
  188.6 111.3 %gather.2 = (bf16[2,3,20,8,2,2,8,384]{7,6,5,4,3,2,1,0:T(8,128)(2,1)}, f32[2,32,20,40,384]{4,3,2,1,0:T(8,128)}) custom-call(bf16[3,256,256]{2,1,0:T(8,128)(2,1)} %get-tuple-element.56.m_ref, f32[2,8,2,16,960]{4,3,2,1,0:T(8,128)} %get-tuple-element.15.s_ref, f32[2,16,16,20,8,20]{5,4,3,2,1,0:T(8,128)} %bitcast.44, ...), custom_call_target="tpu_custom_call", output_to_operand_aliasing={{1}: (6, {})} | custom-call | tf_op jit(solution)/shard_map/gather/pallas_call | solution.py:694
  299.9 122.0 %layer_first.1 = (f32[2,32,20,40,384]{4,3,2,1,0:T(8,128)}, f32[2,20,256,384]{3,2,1,0:T(8,128)}) custom-call(f32[2,32,20,40,384]{4,3,2,1,0:T(8,128)} %get-tuple-element.17.refs_0_, bf16[2,3,20,256,384]{4,3,2,1,0:T(8,128)(2,1)} %bitcast.50, bf16[8,96,192]{2,1,0:T(8,128)(2,1)} %constant.70.clone.refs_2_, bf16[8,128,192]{2,1,0:T(8,128)(2,1)} %constant.71.clone.refs_3_, ...), custom_call_target="tpu_custom_call" | custom-call | tf_op jit(solution)/shard_map/layer_first/pallas_call | solution.py:711
  422.0 88.1 %reduce.3 = (f32[2,8,2,16,960]{4,3,2,1,0:T(8,128)}, f32[2,32,20,40,384]{4,3,2,1,0:T(8,128)}) custom-call(bf16[3,256,256]{2,1,0:T(8,128)(2,1)} %get-tuple-element.57.m_ref, f32[2,20,8,2,2,8,384]{6,5,4,3,2,1,0:T(8,128)} %bitcast.51, f32[2,32,20,40,384]{4,3,2,1,0:T(8,128)} %get-tuple-element.20.x_ref, bf16[3,160,176]{2,1,0:T(8,128)(2,1)} %fusion.7.w_ref), custom_call_target="tpu_custom_call" | custom-call | tf_op jit(solution)/shard_map/reduce/pallas_call | solution.py:679
  510.0 100.1 %gather.3 = (bf16[2,3,20,8,2,2,8,384]{7,6,5,4,3,2,1,0:T(8,128)(2,1)}, f32[2,32,20,40,384]{4,3,2,1,0:T(8,128)}) custom-call(bf16[3,256,256]{2,1,0:T(8,128)(2,1)} %get-tuple-element.56.m_ref, f32[2,8,2,16,960]{4,3,2,1,0:T(8,128)} %get-tuple-element.21.s_ref, f32[2,16,16,20,8,20]{5,4,3,2,1,0:T(8,128)} %bitcast.45, ...), custom_call_target="tpu_custom_call", output_to_operand_aliasing={{1}: (6, {})} | custom-call | tf_op jit(solution)/shard_map/gather/pallas_call | solution.py:694
  610.2 113.6 %layer_last.1 = f32[16,32,20,40,48]{4,3,2,1,0:T(8,128)} custom-call(f32[2,32,20,40,384]{4,3,2,1,0:T(8,128)} %get-tuple-element.23.refs_0_, bf16[2,3,20,256,384]{4,3,2,1,0:T(8,128)(2,1)} %bitcast.49, bf16[8,96,192]{2,1,0:T(8,128)(2,1)} %constant.70.clone.refs_2_, bf16[8,128,192]{2,1,0:T(8,128)(2,1)} %constant.71.clone.refs_3_, ...), custom_call_target="tpu_custom_call" | custom-call | tf_op jit(solution)/shard_map/layer_last/pallas_call | solution.py:718
  (14 shorter events, 0.2 us)

commit v6 on v5

--- a/solution.py
+++ b/solution.py
@@ -24,6 +24,7 @@
 CLASS_ROWS = (0, 64, 160, 256)
 LANES = 128
 ADDENDS = 3
+CHUNKS = ((0, 2), (2, 6), (6, 8))
 FORWARD_UNIT = (2, 10)
 FIRST_UNIT = (2, 10)
 LAST_UNIT = (1, 10)
@@ -201,8 +202,9 @@
     width, lanes = x_ref.shape[2], f_ref.shape[-1]
     pair, per_step = unit
     tables = (t0[0], t1[0], t2[0])
-
-    @pl.when(pl.program_id(1) == 0)
+    start = pl.program_id(2) * width
+
+    @pl.when((pl.program_id(1) == 0) & (start == 0))
     def _():
         zero_spectrum(f_ref)
 
@@ -220,7 +222,7 @@
             if n < count:
                 load(c + n * pair, n)
             if n:
-                forward_stage(u_ref.at[n - 1], tables, f_ref, c + (n - 1) * pair, pair)
+                forward_stage(u_ref.at[n - 1], tables, f_ref, start + c + (n - 1) * pair, pair)
         return 0
     lax.fori_loop(0, width // per_step, body, 0)
 
@@ -257,11 +259,12 @@
     p_ref = p_ref.at[0]
     width, lanes = p_ref.shape[1], p_ref.shape[-1]
     batch = lanes // X_GROUP
+    start = pl.program_id(2) * width
     if first:
         *tabs, v_ref, f_hbm, a_ref, u_ref, f_ref, sem = tabs
         v_ref = v_ref.at[0]
 
-        @pl.when(pl.program_id(1) == 0)
+        @pl.when((pl.program_id(1) == 0) & (start == 0))
         def _():
             zero_spectrum(f_ref)
     else:
@@ -293,16 +296,16 @@
         count = per_step // pair
         for n in range(count + 2):
             if n < count:
-                inverse_stage(s_ref, c + n * pair, pair, inv, a_ref.at[n])
+                inverse_stage(s_ref, start + c + n * pair, pair, inv, a_ref.at[n])
             if 0 < n <= count:
                 activate(c + (n - 1) * pair, n - 1)
             if first and n > 1:
-                forward_stage(u_ref.at[n - 2], fwd, f_ref, c + (n - 2) * pair, pair)
+                forward_stage(u_ref.at[n - 2], fwd, f_ref, start + c + (n - 2) * pair, pair)
         return 0
     lax.fori_loop(0, width // per_step, body, 0)
 
     if first:
-        @pl.when(pl.program_id(1) == pl.num_programs(1) - 1)
+        @pl.when((pl.program_id(1) == pl.num_programs(1) - 1) & (start > 0))
         def _():
             copy = pltpu.make_async_copy(f_ref, f_hbm.at[pl.program_id(0)], sem)
             copy.start()
@@ -361,13 +364,13 @@
                         s_ref[g, i, c, 0, p, h] = d
 
 
-def mix(s_ref, re_w, im_w, t_ref, to, half, rows, re_rows, im_rows, re_s, im_s, re_t, im_t):
-    own, slots, _, n_ky, lanes = s_ref.shape
+def mix(s_ref, re_w, im_w, t_ref, to, chunk, rows, re_rows, im_rows, re_s, im_s, re_t, im_t):
+    own, _, _, n_ky, lanes = s_ref.shape
     width = re_w.shape[2]
     batch = lanes // width
-    some = slots // 2
+    some = chunk[1] - chunk[0]
     part_modes = some * n_ky
-    pick = slice(half * some, (half + 1) * some)
+    pick, modes = slice(*chunk), slice(0, own * part_modes)
 
     for w_ref, out in ((re_w, re_rows), (im_w, im_rows)):
         def lay(c, _):
@@ -377,11 +380,11 @@
                     rows[at:at + SUB, 0:width] = w_ref[k, ky, c]
             mat = jnp.concatenate([rows[pl.ds((k * n_ky + h * SUB) * SUB + kz, SUB, stride=SUB), :]
                                    for k in range(own) for kz in KZ_ORDER[pick] for h in range(n_ky // SUB)], 0)
-            out[c] = mat.T[0:out.shape[1]]
+            out[c, :, modes] = mat.T[0:out.shape[1]]
             return 0
         lax.fori_loop(0, width, lay, 0)
     for p, out in enumerate((re_s, im_s)):
-        out[...] = jnp.concatenate([s_ref[k, pick, p].reshape(part_modes, lanes) for k in range(own)], 0).T
+        out[:, modes] = jnp.concatenate([s_ref[k, pick, p].reshape(part_modes, lanes) for k in range(own)], 0).T
     pair = 2
 
     def outputs(i, _):
@@ -389,23 +392,23 @@
 
         def inner(c, acc):
             at = pl.ds(pl.multiple_of(c * batch, SUB), batch)
-            a, b = re_s[at, :], im_s[at, :]
+            a, b = re_s[at, modes], im_s[at, modes]
             new = []
             for u in range(pair):
-                p = jnp.broadcast_to(re_rows[c, pl.ds(d + u, 1), :], a.shape)
-                q = jnp.broadcast_to(im_rows[c, pl.ds(d + u, 1), :], a.shape)
+                p = jnp.broadcast_to(re_rows[c, pl.ds(d + u, 1), modes], a.shape)
+                q = jnp.broadcast_to(im_rows[c, pl.ds(d + u, 1), modes], a.shape)
                 new += [acc[2 * u] + (a * p - b * q), acc[2 * u + 1] + (a * q + b * p)]
             return tuple(new)
         zero = jnp.zeros((batch, own * part_modes), F32)
         acc = lax.fori_loop(0, width, inner, (zero,) * (2 * pair))
         for u in range(pair):
             at = pl.ds(pl.multiple_of((d + u) * batch, SUB), batch)
-            re_t[at, :] = acc[2 * u]
-            im_t[at, :] = acc[2 * u + 1]
+            re_t[at, modes] = acc[2 * u]
+            im_t[at, modes] = acc[2 * u + 1]
         return 0
     lax.fori_loop(0, width // pair, outputs, 0)
     for p, got in enumerate((re_t, im_t)):
-        back = got[...].T
+        back = got[:, modes].T
         for k in range(own):
             t_ref[to[k], pick, p] = back[k * part_modes:(k + 1) * part_modes].reshape(some, n_ky, lanes)
 
@@ -435,9 +438,9 @@
                                         device_id_type=pl.DeviceIdType.MESH)
 
 
-def half_slots(ref, k, half):
-    some = ref.shape[1] // 2
-    return ref.at[k, pl.ds(half * some, some)]
+def chunk_of(ref, k, n):
+    low, high = CHUNKS[n]
+    return ref.at[k, pl.ds(low, high - low)]
 
 
 def reduce_kernel(first, m_ref, f_ref, x_ref, w_ref, out_ref, p_ref, d_ref, s_ref, r1, r2, r3,
@@ -450,11 +453,11 @@
     def to_core(slot):
         return [remote(s_ref.at[SUB + me.order[t], slot], r1.at[t, slot], send1.at[slot, t], recv1.at[slot, t], me.core)
                 for t in range(SUB)]
-    for h in range(2):
-        mine = [half_slots(s_ref, k, h) for k in me.order]
-        two.append([remote(mine[t], half_slots(r2, t, h), send2.at[h, t], recv2.at[h, t], (me.x_chip, me.y_chip)[t % 2])
+    for h in range(len(CHUNKS)):
+        mine = [chunk_of(s_ref, k, h) for k in me.order]
+        two.append([remote(mine[t], chunk_of(r2, t, h), send2.at[h, t], recv2.at[h, t], (me.x_chip, me.y_chip)[t % 2])
                     for t in range(4)])
-        three.append([remote(mine[4 + t], half_slots(r3, t, h), send3.at[h, t], recv3.at[h, t], (me.y_chip, me.x_chip)[t])
+        three.append([remote(mine[4 + t], chunk_of(r3, t, h), send3.at[h, t], recv3.at[h, t], (me.y_chip, me.x_chip)[t])
                       for t in range(2)])
 
     def add(dst, a, b):
@@ -464,20 +467,20 @@
         lax.fori_loop(0, dst.shape[0], row, 0)
 
     def from_core(h):
-        arriving = [to_core(slot) for slot in range(h * slots // 2, (h + 1) * slots // 2)]
+        arriving = [to_core(slot) for slot in range(*CHUNKS[h])]
         for t in range(SUB):
             for copies in arriving:
                 copies[t].wait_recv()
-            to = half_slots(s_ref, me.order[t], h)
-            add(to, to, half_slots(r1, t, h))
+            to = chunk_of(s_ref, me.order[t], h)
+            add(to, to, chunk_of(r1, t, h))
             if t < 4:
                 two[h][t].start()
 
     def from_chip(h, these):
         for t in these:
             two[h][t].wait_recv()
-            to = half_slots(s_ref, me.order[4 + t], h)
-            add(to, to, half_slots(r2, t, h))
+            to = chunk_of(s_ref, me.order[4 + t], h)
+            add(to, to, chunk_of(r2, t, h))
             if t < 2:
                 three[h][t].start()
 
@@ -485,10 +488,11 @@
         from_chip(h, (2, 3))
         for t in range(2):
             three[h][t].wait_recv()
-            add(half_slots(out_ref, t, h), half_slots(s_ref, me.order[6 + t], h), half_slots(r3, t, h))
-
-    events = ((0, me.enter), (slots // 2, lambda: from_core(0)), (slots - 1, lambda: from_chip(0, (0, 1))),
-              (slots + 1, lambda: from_core(1)), (slots + 3, lambda: finish(0)), (slots + 5, lambda: from_chip(1, (0, 1))))
+            add(chunk_of(out_ref, t, h), chunk_of(s_ref, me.order[6 + t], h), chunk_of(r3, t, h))
+
+    events = ((0, me.enter), (2, lambda: from_core(0)), (slots - 3, lambda: from_chip(0, (0, 1))), (slots - 2, lambda: from_core(1)),
+              (slots, lambda: from_core(2)), (slots + 3, lambda: finish(0)), (slots + 5, lambda: from_chip(1, (0, 1))),
+              (slots + 12, lambda: from_chip(2, (0, 1))))
     for at, event in events:
         pl.when(step == at)(event)
 
@@ -498,38 +502,39 @@
         for copy in to_core(step):
             copy.start()
 
-    @pl.when(step >= slots // 2)
+    @pl.when(step >= slots)
     def _():
         channel_product(first, x_ref, w_ref, p_ref.at[0], d_ref)
 
     @pl.when(step == last)
     def _():
         finish(1)
+        finish(2)
         for copies in [to_core(slot) for slot in range(slots)] + two + three:
             for copy in copies:
                 copy.wait_send()
 
 
-def gather_steps(units, half):
-    return 2 + units // 2, 2 + units
+def inverse_slot(step):
+    return jnp.where(step < SUB, jnp.clip(step - 6, 0, 1), jnp.clip(step - 14, 1, SUB - 1))
 
 
 def gather_kernel(first, layer, m_ref, s_ref, re_hbm, im_hbm, x_ref, w_ref, p_in, parts_ref, p_ref, d_ref, t_ref,
-                  re_w, im_w, rows, re_rows, im_rows, re_s, im_s, re_t, im_t, w_sem, send, recv):
+                  re_w, im_w, rows, re_rows, im_rows, re_s, im_s, re_t, im_t, w_sem, send_sem, recv_sem):
     me = Place()
     step, last = pl.program_id(0), pl.num_programs(0) - 1
     p3, q3, p2, q2, p1, q1, p0, q0 = me.order
     plan = [(p0, me.y_chip, 0), (q0, me.x_chip, 0), (p0, me.x_chip, 0), (q0, me.y_chip, 0), (p0, me.core, SUB), (q0, me.core, SUB),
             (p1, me.x_chip, 0), (q1, me.y_chip, 0)] + [(k, me.core, SUB) for k in (p1, q1, p2, q2, p3, q3)]
-    copies = [[remote(half_slots(t_ref, k, h), half_slots(t_ref, k + up, h), send.at[h, n], recv.at[h, n], device)
-               for n, (k, device, up) in enumerate(plan)] for h in range(2)]
+    copies = [[remote(chunk_of(t_ref, k, h), chunk_of(t_ref, k + up, h), send_sem.at[h, n], recv_sem.at[h, n], device)
+               for n, (k, device, up) in enumerate(plan)] for h in range(len(CHUNKS))]
     weights = [pltpu.make_async_copy(hbm.at[layer, me.mine + k], to.at[i], w_sem.at[n, i])
                for n, (hbm, to) in enumerate(((re_hbm, re_w), (im_hbm, im_w))) for i, k in enumerate((p0, q0))]
 
-    def mix_half(h):
-        mix(s_ref, re_w, im_w, t_ref, (p0, q0), h, rows, re_rows, im_rows, re_s, im_s, re_t, im_t)
-        if h:
-            pass_on(0)
+    def mixed(h):
+        mix(s_ref, re_w, im_w, t_ref, (p0, q0), CHUNKS[h], rows, re_rows, im_rows, re_s, im_s, re_t, im_t)
+
+    def send(h):
         for copy in copies[h][:6]:
             copy.start()
 
@@ -539,7 +544,12 @@
         me.enter()
         for copy in weights:
             copy.wait()
-        mix_half(0)
+        mixed(0)
+        send(0)
+
+    def follow(h):
+        pass_on(h)
+        send(h + 1)
 
     def pass_on(h):
         for n in range(2):
@@ -555,34 +565,32 @@
         for n in (4, 5, *range(SUB, len(plan))):
             copies[h][n].wait_recv()
 
-    half = t_ref.shape[1] // 2
-    x_from, x_then = gather_steps(last + 1 - 2 - half, half)
-    for at, event in ((0, begin), (1, lambda: mix_half(1)), (x_from, lambda: finish(0)), (x_from + 2, lambda: pass_on(1)),
-                      (x_then, lambda: finish(1))):
+    def second():
+        mixed(1)
+        follow(0)
+
+    for at, event in ((0, begin), (1, second), (2, lambda: mixed(2)), (6, lambda: finish(0)), (SUB, lambda: follow(1)),
+                      (16, lambda: finish(1)), (18, lambda: pass_on(2)), (20, lambda: finish(2))):
         pl.when(step == at)(event)
 
-    @pl.when((step >= 2) & (step < x_then))
+    @pl.when((step >= 3) & (step <= last - 3))
     def _():
         channel_product(first, x_ref, w_ref, p_ref.at[0], d_ref)
 
-    @pl.when((step >= x_from) & (step < x_from + half))
+    @pl.when((step == 6) | (step == 7) | (step >= 16))
     def _():
-        x_inverse(m_ref, t_ref, step - x_from, parts_ref)
-
-    @pl.when(step >= x_then)
-    def _():
-        x_inverse(m_ref, t_ref, step - x_then + half, parts_ref)
+        x_inverse(m_ref, t_ref, inverse_slot(step), parts_ref)
 
     @pl.when(step == last)
     def _():
-        for h in range(2):
-            for copy in copies[h]:
+        for some in copies:
+            for copy in some:
                 copy.wait_send()
 
 
 def block(shape, index, slot=None, **kwargs):
     def index_map(*at):
-        return tuple(0 if k == 'o' else slot(at[0]) if k == 's' else at['ij'.index(k)] for k in index)
+        return tuple(0 if k == 'o' else slot(at[0]) if k == 's' else at['ijk'.index(k)] for k in index)
     return pl.BlockSpec(shape, index_map, **kwargs)
 
 
@@ -635,11 +643,12 @@
 
         real_w, imag_w = (jnp.swapaxes(w, 3, 4) for w in (spec_real, spec_imag))
         v = jnp.swapaxes(jnp.moveaxis(field, 0, -1), 2, 3)
-        grid = (groups, blocks)
+        grid = (groups, blocks, 2)
+        part_width = width // 2
         params = pltpu.CompilerParams(vmem_limit_bytes=VMEM_LIMIT)
         spec_shape = jax.ShapeDtypeStruct((groups, width, 256, lanes), F32)
-        in_block = block((X_GROUP, Y_BLOCK, width, grid_z, batch), 'ijooo')
-        mid_block = block((1, Y_BLOCK, width, grid_z, lanes), 'ijooo')
+        in_block = block((X_GROUP, Y_BLOCK, part_width, grid_z, batch), 'ijkoo')
+        mid_block = block((1, Y_BLOCK, part_width, grid_z, lanes), 'ijkoo')
         part_block = block((1, ADDENDS, width, CLASS_ROWS[-1], lanes), 'ioooo')
         mid_shape = jax.ShapeDtypeStruct((groups, y_loc, width, grid_z, lanes), F32)
         anywhere = pl.BlockSpec(memory_space=pl.ANY)
@@ -677,32 +686,28 @@
         def across(f, layer, source):
             first = layer == 0
             s, p = pl.pallas_call(
-                functools.partial(reduce_kernel, first), grid=(slots // 2 + units,),
+                functools.partial(reduce_kernel, first), grid=(slots + units,),
                 out_shape=(jax.ShapeDtypeStruct((own,) + unit, F32), mid_shape),
                 in_specs=[x_block,
                           block((groups, width, 1, 2, halves, SUB, lanes), 'oosoooo', lambda j: jnp.minimum(j, slots - 1)),
-                          half_block(first, 0, slots // 2), w_block],
-                out_specs=(own_block, half_block(False, 0, slots // 2)),
+                          half_block(first, 0, slots), w_block],
+                out_specs=(own_block, half_block(False, 0, slots)),
                 scratch_shapes=[half_rows] + [pltpu.VMEM((n,) + unit, F32) for n in (n_kx, SUB, 4, 2)]
-                + [dma((slots, SUB))] * 2 + [dma((2, n)) for n in (4, 4, 2, 2)],
+                + [dma((slots, SUB))] * 2 + [dma((len(CHUNKS), n)) for n in (4, 4, 2, 2)],
                 compiler_params=exchange(2 * layer), name='reduce')(
                     fwd_x, f.reshape(groups, width, slots, 2, halves, SUB, lanes), source, point_w[layer])
-            x_from, x_then = gather_steps(units, slots // 2)
-
-            def inverse_slot(j):
-                return jnp.where(j < x_then, jnp.clip(j - x_from, 0, slots // 2 - 1), j - x_then + slots // 2)
             parts, p = pl.pallas_call(
-                functools.partial(gather_kernel, first, layer), grid=(units + 2 + slots // 2,),
+                functools.partial(gather_kernel, first, layer), grid=(units + 6,),
                 out_shape=(jax.ShapeDtypeStruct((groups, ADDENDS, width, slots, 2, halves, SUB, lanes), BF16), mid_shape),
-                in_specs=[x_block, own_block, anywhere, anywhere, half_block(first, 1, 2), w_block, anywhere],
+                in_specs=[x_block, own_block, anywhere, anywhere, half_block(first, 1, 3), w_block, anywhere],
                 out_specs=(block((groups, ADDENDS, width, 1, 2, halves, SUB, lanes), 'ooosoooo', inverse_slot),
-                           half_block(False, 1, 2)),
+                           half_block(False, 1, 3)),
                 input_output_aliases={6: 1},
                 scratch_shapes=[half_rows, pltpu.VMEM((n_kx,) + unit, F32)]
                 + [pltpu.VMEM((own, n_ky, width, SUB, width), F32)] * 2
                 + [pltpu.VMEM((own * n_ky * SUB, LANES), F32)] + [pltpu.VMEM((width, 24, LANES), F32)] * 2
-                + [pltpu.VMEM((width * batch, own * slots * n_ky // 2), F32)] * 4
-                + [dma((2, 2)), dma((2, 14)), dma((2, 14))],
+                + [pltpu.VMEM((width * batch, LANES), F32)] * 4
+                + [dma((2, 2))] + [dma((len(CHUNKS), 14))] * 2,
                 compiler_params=exchange(2 * layer + 1), name='gather')(
                     inv_x, s, real_w, imag_w, source, point_w[layer], p)
             return parts.reshape(groups, ADDENDS, width, CLASS_ROWS[-1], lanes), p

time: 739 us -> 733 us (level); the launches traced: 724 us -> 729 us
    pallas_call x2, Pallas kernels: 211 us -> 222 us  [across(): pl.pallas_call(functools.partial(gather_kernel, first, layer), grid=(unit...]
where the time goes in v6:
time: 733 us; the launch traced here: 729 us
  Pallas kernels  716 us (98%)
    pallas_call x2, Pallas kernels, across(): pl.pallas_call(functools.partial(gather_kernel, first, layer), grid=(unit...  222 us
    pallas_call x2, Pallas kernels, across(): pl.pallas_call(functools.partial(reduce_kernel, first), grid=(slots + uni...  174 us
    pallas_call x1, Pallas kernels, local_layers(): pl.pallas_call(functools.partial(layer_kernel, FIRST_UNIT, True), grid=gr...  118 us
    pallas_call x1, Pallas kernels, local_layers(): pl.pallas_call(functools.partial(layer_kernel, LAST_UNIT, False), grid=gr...  112 us
    pallas_call x1, Pallas kernels, local_layers(): pl.pallas_call(functools.partial(forward_kernel, FORWARD_UNIT), grid=grid...  90.2 us

profile of v6, /device:TPU:0, one launch (start us, length us, event | category | flops | bytes accessed | tf_op | source)
XLA Modules:
  0.0 729.0 jit_solution(12938242330209823924)
XLA Ops:
  0.0 0.8 multiply_bitcast_fusion
  0.8 0.1 broadcast_in_dim.28
  0.8 0.1 reshape.312
  1.0 0.1 broadcast_in_dim.16
  1.1 0.1 reshape.309
  1.2 0.8 fusion.25
  2.1 0.1 copy.32
  2.2 0.1 copy.29
  2.3 0.2 copy.30
  2.4 0.2 copy.33
  2.6 1.0 constant_dynamic-slice_fusion.1
  3.6 1.0 dynamic-slice_bitcast_fusion
  4.6 1.2 reduce-precision_convert_fusion.1
  5.9 1.0 pad_maximum_fusion
  6.8 1.6 broadcast_multiply_fusion
  8.4 2.0 mul.141
  10.5 0.8 fusion.7.w_ref
  11.3 0.5 mul.132
  11.8 0.8 fusion.6.w_ref
  12.6 90.2 %forward.1 = f32[2,20,256,384]{3,2,1,0:T(8,128)} custom-call(f32[16,32,20,40,48]{4,3,2,1,0:T(8,128)} %bitcast.3.x_ref, bf16[8,64,192]{2,1,0:T(8,128)(2,1)} %constant.67.clone.t0.refs_7_, bf16[8,192,256]{2,1,0:T(8,128)(2,1)} %constant.68.clone.t1.refs_8_, bf16[8,192,256]{2,1,0:T(8,128)(2,1)} %constant.69.clone.t2.refs_9_), custom_call_target="tpu_custom_call" | custom-call | tf_op jit(solution)/shard_map/forward/pallas_call | solution.py:670
  102.8 90.4 %reduce.2 = (f32[2,8,2,16,960]{4,3,2,1,0:T(8,128)}, f32[2,32,20,40,384]{4,3,2,1,0:T(8,128)}) custom-call(bf16[3,256,256]{2,1,0:T(8,128)(2,1)} %get-tuple-element.57.m_ref, f32[2,20,8,2,2,8,384]{6,5,4,3,2,1,0:T(8,128)} %bitcast.48, f32[16,32,20,40,48]{4,3,2,1,0:T(8,128)} %bitcast.3.x_ref, bf16[3,160,176]{2,1,0:T(8,128)(2,1)} %fusion.6.w_ref), custom_call_target="tpu_custom_call" | custom-call | tf_op jit(solution)/shard_map/reduce/pallas_call | solution.py:688
  193.2 117.7 %gather.2 = (bf16[2,3,20,8,2,2,8,384]{7,6,5,4,3,2,1,0:T(8,128)(2,1)}, f32[2,32,20,40,384]{4,3,2,1,0:T(8,128)}) custom-call(bf16[3,256,256]{2,1,0:T(8,128)(2,1)} %get-tuple-element.56.m_ref, f32[2,8,2,16,960]{4,3,2,1,0:T(8,128)} %get-tuple-element.15.s_ref, f32[2,16,16,20,8,20]{5,4,3,2,1,0:T(8,128)} %bitcast.44, ...), custom_call_target="tpu_custom_call", output_to_operand_aliasing={{1}: (6, {})} | custom-call | tf_op jit(solution)/shard_map/gather/pallas_call | solution.py:699
  310.9 118.2 %layer_first.1 = (f32[2,32,20,40,384]{4,3,2,1,0:T(8,128)}, f32[2,20,256,384]{3,2,1,0:T(8,128)}) custom-call(f32[2,32,20,40,384]{4,3,2,1,0:T(8,128)} %get-tuple-element.17.refs_0_, bf16[2,3,20,256,384]{4,3,2,1,0:T(8,128)(2,1)} %bitcast.50, bf16[8,96,192]{2,1,0:T(8,128)(2,1)} %constant.70.clone.refs_2_, bf16[8,128,192]{2,1,0:T(8,128)(2,1)} %constant.71.clone.refs_3_, ...), custom_call_target="tpu_custom_call" | custom-call | tf_op jit(solution)/shard_map/layer_first/pallas_call | solution.py:716
  429.2 83.5 %reduce.3 = (f32[2,8,2,16,960]{4,3,2,1,0:T(8,128)}, f32[2,32,20,40,384]{4,3,2,1,0:T(8,128)}) custom-call(bf16[3,256,256]{2,1,0:T(8,128)(2,1)} %get-tuple-element.57.m_ref, f32[2,20,8,2,2,8,384]{6,5,4,3,2,1,0:T(8,128)} %bitcast.51, f32[2,32,20,40,384]{4,3,2,1,0:T(8,128)} %get-tuple-element.20.x_ref, bf16[3,160,176]{2,1,0:T(8,128)(2,1)} %fusion.7.w_ref), custom_call_target="tpu_custom_call" | custom-call | tf_op jit(solution)/shard_map/reduce/pallas_call | solution.py:688
  512.7 104.2 %gather.3 = (bf16[2,3,20,8,2,2,8,384]{7,6,5,4,3,2,1,0:T(8,128)(2,1)}, f32[2,32,20,40,384]{4,3,2,1,0:T(8,128)}) custom-call(bf16[3,256,256]{2,1,0:T(8,128)(2,1)} %get-tuple-element.56.m_ref, f32[2,8,2,16,960]{4,3,2,1,0:T(8,128)} %get-tuple-element.21.s_ref, f32[2,16,16,20,8,20]{5,4,3,2,1,0:T(8,128)} %bitcast.45, ...), custom_call_target="tpu_custom_call", output_to_operand_aliasing={{1}: (6, {})} | custom-call | tf_op jit(solution)/shard_map/gather/pallas_call | solution.py:699
  616.9 112.1 %layer_last.1 = f32[16,32,20,40,48]{4,3,2,1,0:T(8,128)} custom-call(f32[2,32,20,40,384]{4,3,2,1,0:T(8,128)} %get-tuple-element.23.refs_0_, bf16[2,3,20,256,384]{4,3,2,1,0:T(8,128)(2,1)} %bitcast.49, bf16[8,96,192]{2,1,0:T(8,128)(2,1)} %constant.70.clone.refs_2_, bf16[8,128,192]{2,1,0:T(8,128)(2,1)} %constant.71.clone.refs_3_, ...), custom_call_target="tpu_custom_call" | custom-call | tf_op jit(solution)/shard_map/layer_last/pallas_call | solution.py:723
  (14 shorter events, 0.2 us)

commit v7 on v6

--- a/solution.py
+++ b/solution.py
@@ -24,7 +24,9 @@
 CLASS_ROWS = (0, 64, 160, 256)
 LANES = 128
 ADDENDS = 3
-CHUNKS = ((0, 2), (2, 6), (6, 8))
+REDUCE_CHUNKS = ((0, 2), (2, 6), (6, 8))
+GATHER_CHUNKS = ((0, 4), (4, 6), (6, 8))
+MIX_CHUNKS = ((0, 4), (4, 8))
 FORWARD_UNIT = (2, 10)
 FIRST_UNIT = (2, 10)
 LAST_UNIT = (1, 10)
@@ -202,9 +204,8 @@
     width, lanes = x_ref.shape[2], f_ref.shape[-1]
     pair, per_step = unit
     tables = (t0[0], t1[0], t2[0])
-    start = pl.program_id(2) * width
-
-    @pl.when((pl.program_id(1) == 0) & (start == 0))
+
+    @pl.when(pl.program_id(1) == 0)
     def _():
         zero_spectrum(f_ref)
 
@@ -222,7 +223,7 @@
             if n < count:
                 load(c + n * pair, n)
             if n:
-                forward_stage(u_ref.at[n - 1], tables, f_ref, start + c + (n - 1) * pair, pair)
+                forward_stage(u_ref.at[n - 1], tables, f_ref, c + (n - 1) * pair, pair)
         return 0
     lax.fori_loop(0, width // per_step, body, 0)
 
@@ -230,8 +231,8 @@
 def channel_product(first, x_ref, w_ref, p_ref, d_ref):
     blocks, width, depth, lanes = p_ref.shape
     rows = width * SUB
-    ones = jnp.ones((w_ref.shape[2] - rows, blocks * lanes), BF16)
-    full, (a, b, c) = w_ref[0], (w_ref[i, :, :rows] for i in range(ADDENDS))
+    ones = jnp.ones((w_ref.shape[-1] - rows, blocks * lanes), BF16)
+    full, (a, b, c) = w_ref[0, 0], (w_ref[0, i, :, :rows] for i in range(ADDENDS))
 
     def load(j):
         z = slice(j * SUB, (j + 1) * SUB)
@@ -385,7 +386,7 @@
         lax.fori_loop(0, width, lay, 0)
     for p, out in enumerate((re_s, im_s)):
         out[:, modes] = jnp.concatenate([s_ref[k, pick, p].reshape(part_modes, lanes) for k in range(own)], 0).T
-    pair = 2
+    pair = 1
 
     def outputs(i, _):
         d = i * pair
@@ -400,7 +401,7 @@
                 new += [acc[2 * u] + (a * p - b * q), acc[2 * u + 1] + (a * q + b * p)]
             return tuple(new)
         zero = jnp.zeros((batch, own * part_modes), F32)
-        acc = lax.fori_loop(0, width, inner, (zero,) * (2 * pair))
+        acc = lax.fori_loop(0, width, inner, (zero,) * (2 * pair), unroll=True)
         for u in range(pair):
             at = pl.ds(pl.multiple_of((d + u) * batch, SUB), batch)
             re_t[at, modes] = acc[2 * u]
@@ -423,6 +424,7 @@
         self.y_chip = (data, 1 - ys, xs)
         p, q = lambda a, b: 2 * a + b, lambda a, b: 4 + 2 * a + b
         self.mine = SUB * c
+        self.table = 2 * xs + ys
         self.order = (p(1 - x, 1 - y), q(1 - y, 1 - x), p(1 - x, y), q(1 - y, x),
                       p(x, 1 - y), q(y, 1 - x), p(x, y), q(y, x))
 
@@ -438,26 +440,30 @@
                                         device_id_type=pl.DeviceIdType.MESH)
 
 
-def chunk_of(ref, k, n):
-    low, high = CHUNKS[n]
+def step_and_last():
+    return pl.program_id(0), pl.num_programs(0) - 1
+
+
+def chunk_of(ref, k, chunk):
+    low, high = chunk
     return ref.at[k, pl.ds(low, high - low)]
 
 
-def reduce_kernel(first, m_ref, f_ref, x_ref, w_ref, out_ref, p_ref, d_ref, s_ref, r1, r2, r3,
+def reduce_kernel(first, m_hbm, f_ref, x_ref, w_ref, out_ref, p_ref, m_ref, m_sem, d_ref, s_ref, r1, r2, r3,
                   send1, recv1, send2, recv2, send3, recv3):
     me = Place()
-    step, last = pl.program_id(0), pl.num_programs(0) - 1
+    step, last = step_and_last()
     slots = s_ref.shape[1]
     two, three = [], []
 
     def to_core(slot):
         return [remote(s_ref.at[SUB + me.order[t], slot], r1.at[t, slot], send1.at[slot, t], recv1.at[slot, t], me.core)
                 for t in range(SUB)]
-    for h in range(len(CHUNKS)):
-        mine = [chunk_of(s_ref, k, h) for k in me.order]
-        two.append([remote(mine[t], chunk_of(r2, t, h), send2.at[h, t], recv2.at[h, t], (me.x_chip, me.y_chip)[t % 2])
+    for h, chunk in enumerate(REDUCE_CHUNKS):
+        mine = [chunk_of(s_ref, k, chunk) for k in me.order]
+        two.append([remote(mine[t], chunk_of(r2, t, chunk), send2.at[h, t], recv2.at[h, t], (me.x_chip, me.y_chip)[t % 2])
                     for t in range(4)])
-        three.append([remote(mine[4 + t], chunk_of(r3, t, h), send3.at[h, t], recv3.at[h, t], (me.y_chip, me.x_chip)[t])
+        three.append([remote(mine[4 + t], chunk_of(r3, t, chunk), send3.at[h, t], recv3.at[h, t], (me.y_chip, me.x_chip)[t])
                       for t in range(2)])
 
     def add(dst, a, b):
@@ -467,20 +473,20 @@
         lax.fori_loop(0, dst.shape[0], row, 0)
 
     def from_core(h):
-        arriving = [to_core(slot) for slot in range(*CHUNKS[h])]
+        arriving = [to_core(slot) for slot in range(*REDUCE_CHUNKS[h])]
         for t in range(SUB):
             for copies in arriving:
                 copies[t].wait_recv()
-            to = chunk_of(s_ref, me.order[t], h)
-            add(to, to, chunk_of(r1, t, h))
+            to = chunk_of(s_ref, me.order[t], REDUCE_CHUNKS[h])
+            add(to, to, chunk_of(r1, t, REDUCE_CHUNKS[h]))
             if t < 4:
                 two[h][t].start()
 
-    def from_chip(h, these):
+    def from_chip(h, these=(0, 1)):
         for t in these:
             two[h][t].wait_recv()
-            to = chunk_of(s_ref, me.order[4 + t], h)
-            add(to, to, chunk_of(r2, t, h))
+            to = chunk_of(s_ref, me.order[4 + t], REDUCE_CHUNKS[h])
+            add(to, to, chunk_of(r2, t, REDUCE_CHUNKS[h]))
             if t < 2:
                 three[h][t].start()
 
@@ -488,11 +494,17 @@
         from_chip(h, (2, 3))
         for t in range(2):
             three[h][t].wait_recv()
-            add(chunk_of(out_ref, t, h), chunk_of(s_ref, me.order[6 + t], h), chunk_of(r3, t, h))
-
-    events = ((0, me.enter), (2, lambda: from_core(0)), (slots - 3, lambda: from_chip(0, (0, 1))), (slots - 2, lambda: from_core(1)),
-              (slots, lambda: from_core(2)), (slots + 3, lambda: finish(0)), (slots + 5, lambda: from_chip(1, (0, 1))),
-              (slots + 12, lambda: from_chip(2, (0, 1))))
+            add(*(chunk_of(ref, k, REDUCE_CHUNKS[h]) for ref, k in ((out_ref, t), (s_ref, me.order[6 + t]), (r3, t))))
+
+    def begin():
+        table = pltpu.make_async_copy(m_hbm.at[me.table], m_ref, m_sem)
+        table.start()
+        me.enter()
+        table.wait()
+
+    events = ((0, begin), (2, lambda: from_core(0)), (slots - 3, lambda: from_chip(0)), (slots - 2, lambda: from_core(1)),
+              (slots, lambda: from_core(2)), (slots + 3, lambda: finish(0)), (slots + 5, lambda: from_chip(1)),
+              (slots + 12, lambda: from_chip(2)))
     for at, event in events:
         pl.when(step == at)(event)
 
@@ -515,24 +527,21 @@
                 copy.wait_send()
 
 
-def inverse_slot(step):
-    return jnp.where(step < SUB, jnp.clip(step - 6, 0, 1), jnp.clip(step - 14, 1, SUB - 1))
-
-
-def gather_kernel(first, layer, m_ref, s_ref, re_hbm, im_hbm, x_ref, w_ref, p_in, parts_ref, p_ref, d_ref, t_ref,
+def gather_kernel(first, layer, m_hbm, s_ref, re_hbm, im_hbm, x_ref, w_ref, p_in, parts_ref, p_ref, m_ref, m_sem, d_ref, t_ref,
                   re_w, im_w, rows, re_rows, im_rows, re_s, im_s, re_t, im_t, w_sem, send_sem, recv_sem):
     me = Place()
-    step, last = pl.program_id(0), pl.num_programs(0) - 1
+    step, last = step_and_last()
     p3, q3, p2, q2, p1, q1, p0, q0 = me.order
     plan = [(p0, me.y_chip, 0), (q0, me.x_chip, 0), (p0, me.x_chip, 0), (q0, me.y_chip, 0), (p0, me.core, SUB), (q0, me.core, SUB),
             (p1, me.x_chip, 0), (q1, me.y_chip, 0)] + [(k, me.core, SUB) for k in (p1, q1, p2, q2, p3, q3)]
-    copies = [[remote(chunk_of(t_ref, k, h), chunk_of(t_ref, k + up, h), send_sem.at[h, n], recv_sem.at[h, n], device)
-               for n, (k, device, up) in enumerate(plan)] for h in range(len(CHUNKS))]
+    copies = [[remote(chunk_of(t_ref, k, chunk), chunk_of(t_ref, k + up, chunk), send_sem.at[h, n], recv_sem.at[h, n], device)
+               for n, (k, device, up) in enumerate(plan)] for h, chunk in enumerate(GATHER_CHUNKS)]
     weights = [pltpu.make_async_copy(hbm.at[layer, me.mine + k], to.at[i], w_sem.at[n, i])
                for n, (hbm, to) in enumerate(((re_hbm, re_w), (im_hbm, im_w))) for i, k in enumerate((p0, q0))]
+    weights.append(pltpu.make_async_copy(m_hbm.at[me.table], m_ref, m_sem))
 
     def mixed(h):
-        mix(s_ref, re_w, im_w, t_ref, (p0, q0), CHUNKS[h], rows, re_rows, im_rows, re_s, im_s, re_t, im_t)
+        mix(s_ref, re_w, im_w, t_ref, (p0, q0), MIX_CHUNKS[h], rows, re_rows, im_rows, re_s, im_s, re_t, im_t)
 
     def send(h):
         for copy in copies[h][:6]:
@@ -555,7 +564,6 @@
         for n in range(2):
             copies[h][n].wait_recv()
             copies[h][6 + n].start()
-        for n in range(2):
             copies[h][SUB + n].start()
 
     def finish(h):
@@ -565,21 +573,19 @@
         for n in (4, 5, *range(SUB, len(plan))):
             copies[h][n].wait_recv()
 
-    def second():
-        mixed(1)
-        follow(0)
-
-    for at, event in ((0, begin), (1, second), (2, lambda: mixed(2)), (6, lambda: finish(0)), (SUB, lambda: follow(1)),
-                      (16, lambda: finish(1)), (18, lambda: pass_on(2)), (20, lambda: finish(2))):
+    x_from = last + 1 - t_ref.shape[1]
+    for at, event in ((0, begin), (1, lambda: mixed(1)), (5, lambda: follow(0)), (x_from, lambda: finish(0)),
+                      (x_from + 1, lambda: follow(1)), (x_from + 4, lambda: finish(1)), (x_from + 5, lambda: pass_on(2)),
+                      (x_from + 6, lambda: finish(2))):
         pl.when(step == at)(event)
 
-    @pl.when((step >= 3) & (step <= last - 3))
+    @pl.when((step >= 2) & (step < x_from + 4))
     def _():
         channel_product(first, x_ref, w_ref, p_ref.at[0], d_ref)
 
-    @pl.when((step == 6) | (step == 7) | (step >= 16))
+    @pl.when(step >= x_from)
     def _():
-        x_inverse(m_ref, t_ref, inverse_slot(step), parts_ref)
+        x_inverse(m_ref, t_ref, step - x_from, parts_ref)
 
     @pl.when(step == last)
     def _():
@@ -594,12 +600,24 @@
     return pl.BlockSpec(shape, index_map, **kwargs)
 
 
-def bf16_addends(table):
-    out = []
-    for _ in range(ADDENDS):
-        out.append(lax.reduce_precision(table, exponent_bits=SUB, mantissa_bits=7))
-        table = table - out[-1]
-    return jnp.stack(out).astype(BF16)
+def point_table_kernel(w_ref, b_ref, out_ref):
+    layers, width = b_ref.shape
+    rows = width * SUB
+
+    def spread(shape, axis):
+        at = [lax.broadcasted_iota(jnp.int32, shape, k) for k in range(2)]
+        return jnp.where(at[axis] // SUB == at[1 - axis], 1.0, 0.0).astype(BF16)
+    down, across = spread((rows, width), 0), spread((width, rows), 1)
+    at = [lax.broadcasted_iota(jnp.int32, (rows, rows), k) % SUB for k in range(2)]
+    column = lax.broadcasted_iota(jnp.int32, (rows, 2 * SUB), 1)
+    for layer in range(layers):
+        weights, biases = split3(0.5 * w_ref[layer].T), split3(0.5 * b_ref[layer:layer + 1])
+        shift = sum(jnp.where(column == i, jnp.sum(down.astype(F32) * b.astype(F32), 1, keepdims=True), 0.0)
+                    for i, b in enumerate(biases))
+        for i, w in enumerate(weights):
+            wide = dot(dot(down, w).astype(BF16), across)
+            wide = jnp.where(at[0] == at[1], wide, 0.0)
+            out_ref[layer, i] = jnp.concatenate([wide, shift if i == 0 else jnp.zeros_like(shift)], 1).astype(BF16)
 
 
 def solution(mesh):
@@ -613,7 +631,6 @@
         lanes = X_GROUP * batch
         kx, ky = kept(modes, grid_x), kept(modes, grid_y)
         n_kx, n_ky = len(kx), len(ky)
-        x_index, y_index = lax.axis_index('xs'), lax.axis_index('ys')
         fwd_np, inv_np = all_tables(blocks, ky, grid_y, grid_z, grid_x * grid_y * grid_z)
         fwd, inv = [jnp.asarray(t) for t in fwd_np], [jnp.asarray(t) for t in inv_np]
 
@@ -623,29 +640,24 @@
         inv_x = np.transpose(fwd_x, (2, 3, 0, 1))
         fwd_x = fwd_x.reshape(n_kx, 2, col_devs, x_loc, 2).transpose(2, 0, 1, 3, 4).reshape(col_devs, 2 * n_kx, 2 * x_loc)
         inv_x = inv_x.reshape(col_devs, 2 * x_loc, 2 * n_kx)
-        odd = (jnp.arange(16 * x_loc) % 2 * y_index)[:, None]
-
-        core, x_chip = x_index % 2, x_index // 2
-
-        def x_table(tables, axis):
-            wide = np.kron(tables, np.eye(SUB)).astype(np.float32)
-            t = lax.dynamic_index_in_dim(jnp.asarray(wide), x_index, 0, keepdims=False)
-            t = jnp.where(core == 1, jnp.roll(t, SUB * n_kx, axis), t)
-            return bf16_addends(jnp.where(odd == 1, -t, t))
-        fwd_x, inv_x = x_table(fwd_x, 0), x_table(inv_x, 1)
-        eye = jnp.eye(Z_BLOCK, dtype=F32)
-        def point_table(layer):
-            w = bf16_addends((0.5 * mix_weight[layer].T[:, None, :, None] * eye[None, :, None, :]).reshape(width * SUB, width * SUB))
-            b = bf16_addends(jnp.broadcast_to(0.5 * bias[layer][:, None], (width, SUB)).reshape(width * SUB))
-            b = jnp.pad(jnp.stack([b.T, 0 * b.T, 0 * b.T]), ((0, 0), (0, 0), (0, 2 * SUB - 3)))
-            return jnp.concatenate([w, b], -1)
-        point_w = [point_table(layer) for layer in range(2)]
+        odd_rows = np.where(np.arange(2 * SUB * x_loc) % 2, -1.0, 1.0)[:, None]
+
+        def x_tables(tables, axis):
+            out = []
+            for xs in range(col_devs):
+                t = np.roll(np.kron(tables[xs], np.eye(SUB)), SUB * n_kx * (xs % 2), axis)
+                out += [np.stack(pieces(t * sign)) for sign in (1.0, odd_rows)]
+            return jnp.asarray(np.stack(out))
+        fwd_x, inv_x = x_tables(fwd_x, 0), x_tables(inv_x, 1)
+        params = pltpu.CompilerParams(vmem_limit_bytes=VMEM_LIMIT)
+        point_w = pl.pallas_call(
+            point_table_kernel, out_shape=jax.ShapeDtypeStruct((2, ADDENDS, width * SUB, width * SUB + 2 * SUB), BF16),
+            compiler_params=params, name='point_table')(mix_weight, bias)
 
         real_w, imag_w = (jnp.swapaxes(w, 3, 4) for w in (spec_real, spec_imag))
         v = jnp.swapaxes(jnp.moveaxis(field, 0, -1), 2, 3)
         grid = (groups, blocks, 2)
         part_width = width // 2
-        params = pltpu.CompilerParams(vmem_limit_bytes=VMEM_LIMIT)
         spec_shape = jax.ShapeDtypeStruct((groups, width, 256, lanes), F32)
         in_block = block((X_GROUP, Y_BLOCK, part_width, grid_z, batch), 'ijkoo')
         mid_block = block((1, Y_BLOCK, part_width, grid_z, lanes), 'ijkoo')
@@ -655,7 +667,6 @@
 
         def stage(unit):
             return pltpu.VMEM((unit[1] // unit[0], 5, Y_BLOCK * SUB, unit[0] * lanes), F32)
-        w_block = block((ADDENDS, width * SUB, width * SUB + 2 * SUB), 'ooo')
 
         units = y_loc // HALF_BLOCK
 
@@ -668,16 +679,19 @@
             return [block((1,) + t.shape[1:], 'joo') for t in tables]
 
         f = pl.pallas_call(
-            functools.partial(forward_kernel, FORWARD_UNIT), grid=grid, out_shape=spec_shape,
-            in_specs=[in_block] + table_specs(fwd),
+            functools.partial(forward_kernel, FORWARD_UNIT), grid=grid[:2], out_shape=spec_shape,
+            in_specs=[block((X_GROUP, Y_BLOCK, width, grid_z, batch), 'ijooo')] + table_specs(fwd),
             out_specs=block((1, width, 256, lanes), 'iooo'),
             scratch_shapes=[stage(FORWARD_UNIT)], compiler_params=params, name='forward')(v, *fwd)
 
         own, slots, halves = 2, SUB, n_ky // SUB
         unit = (slots, 2, n_ky, width * batch)
         own_block = block((own,) + unit, 'ooooo')
-        x_block = block((ADDENDS, 16 * x_loc, 16 * x_loc), 'ooo')
+
+        def w_block(layer):
+            return block((1,) + point_w.shape[1:], 'sooo', lambda j: layer)
         dma = pltpu.SemaphoreType.DMA
+        x_scratch = [pltpu.VMEM(fwd_x.shape[1:], BF16), dma]
         half_rows = pltpu.VMEM((2, width * SUB, HALF_BLOCK * lanes), F32)
 
         def exchange(number):
@@ -688,28 +702,28 @@
             s, p = pl.pallas_call(
                 functools.partial(reduce_kernel, first), grid=(slots + units,),
                 out_shape=(jax.ShapeDtypeStruct((own,) + unit, F32), mid_shape),
-                in_specs=[x_block,
+                in_specs=[anywhere,
                           block((groups, width, 1, 2, halves, SUB, lanes), 'oosoooo', lambda j: jnp.minimum(j, slots - 1)),
-                          half_block(first, 0, slots), w_block],
+                          half_block(first, 0, slots), w_block(layer)],
                 out_specs=(own_block, half_block(False, 0, slots)),
-                scratch_shapes=[half_rows] + [pltpu.VMEM((n,) + unit, F32) for n in (n_kx, SUB, 4, 2)]
-                + [dma((slots, SUB))] * 2 + [dma((len(CHUNKS), n)) for n in (4, 4, 2, 2)],
+                scratch_shapes=x_scratch + [half_rows] + [pltpu.VMEM((n,) + unit, F32) for n in (n_kx, SUB, 4, 2)]
+                + [dma((slots, SUB))] * 2 + [dma((len(REDUCE_CHUNKS), n)) for n in (4, 4, 2, 2)],
                 compiler_params=exchange(2 * layer), name='reduce')(
-                    fwd_x, f.reshape(groups, width, slots, 2, halves, SUB, lanes), source, point_w[layer])
+                    fwd_x, f.reshape(groups, width, slots, 2, halves, SUB, lanes), source, point_w)
             parts, p = pl.pallas_call(
                 functools.partial(gather_kernel, first, layer), grid=(units + 6,),
                 out_shape=(jax.ShapeDtypeStruct((groups, ADDENDS, width, slots, 2, halves, SUB, lanes), BF16), mid_shape),
-                in_specs=[x_block, own_block, anywhere, anywhere, half_block(first, 1, 3), w_block, anywhere],
-                out_specs=(block((groups, ADDENDS, width, 1, 2, halves, SUB, lanes), 'ooosoooo', inverse_slot),
-                           half_block(False, 1, 3)),
+                in_specs=[anywhere, own_block, anywhere, anywhere, half_block(first, 1, 2), w_block(layer), anywhere],
+                out_specs=(block((groups, ADDENDS, width, 1, 2, halves, SUB, lanes), 'ooosoooo', lambda j: jnp.maximum(j - units + 2, 0)),
+                           half_block(False, 1, 2)),
                 input_output_aliases={6: 1},
-                scratch_shapes=[half_rows, pltpu.VMEM((n_kx,) + unit, F32)]
+                scratch_shapes=x_scratch + [half_rows, pltpu.VMEM((n_kx,) + unit, F32)]
                 + [pltpu.VMEM((own, n_ky, width, SUB, width), F32)] * 2
                 + [pltpu.VMEM((own * n_ky * SUB, LANES), F32)] + [pltpu.VMEM((width, 24, LANES), F32)] * 2
                 + [pltpu.VMEM((width * batch, LANES), F32)] * 4
-                + [dma((2, 2))] + [dma((len(CHUNKS), 14))] * 2,
+                + [dma((2, 2))] + [dma((len(GATHER_CHUNKS), 14))] * 2,
                 compiler_params=exchange(2 * layer + 1), name='gather')(
-                    inv_x, s, real_w, imag_w, source, point_w[layer], p)
+                    inv_x, s, real_w, imag_w, source, point_w, p)
             return parts.reshape(groups, ADDENDS, width, CLASS_ROWS[-1], lanes), p
 
         parts, p = across(f, 0, v)

time: 733 us -> 702 us (0.958)
  Pallas kernels: 716 us -> 697 us
    pallas_call x2, Pallas kernels: 222 us -> 206 us  [across(): pl.pallas_call(functools.partial(gather_kernel, first, layer), grid=(unit...]
where the time goes in v7:
time: 702 us; the launch traced here: 698 us
  Pallas kernels  697 us (99%)
    pallas_call x2, Pallas kernels, across(): pl.pallas_call(functools.partial(gather_kernel, first, layer), grid=(unit...  206 us
    pallas_call x2, Pallas kernels, across(): pl.pallas_call(functools.partial(reduce_kernel, first), grid=(slots + uni...  174 us
    pallas_call x1, Pallas kernels, local_layers(): pl.pallas_call(functools.partial(layer_kernel, FIRST_UNIT, True), grid=gr...  118 us
    pallas_call x1, Pallas kernels, local_layers(): pl.pallas_call(functools.partial(layer_kernel, LAST_UNIT, False), grid=gr...  112 us
    pallas_call x1, Pallas kernels, local_layers(): pl.pallas_call(functools.partial(forward_kernel, FORWARD_UNIT), grid=grid...  83.8 us

profile of v7, /device:TPU:0, one launch (start us, length us, event | category | flops | bytes accessed | tf_op | source)
XLA Modules:
  0.0 698.4 jit_solution(13797723655692448733)
XLA Ops:
  0.0 1.3 copy.18.w_ref
  1.3 2.3 point_table.1.w_ref
  3.6 83.8 %forward.1 = f32[2,20,256,384]{3,2,1,0:T(8,128)} custom-call(f32[16,32,20,40,48]{4,3,2,1,0:T(8,128)} %bitcast.x_ref, bf16[8,64,192]{2,1,0:T(8,128)(2,1)} %constant.20.clone.t0.refs_7_, bf16[8,192,256]{2,1,0:T(8,128)(2,1)} %constant.21.clone.t1.refs_8_, bf16[8,192,256]{2,1,0:T(8,128)(2,1)} %constant.22.clone.t2.refs_9_), custom_call_target="tpu_custom_call" | custom-call | tf_op jit(solution)/shard_map/forward/pallas_call | solution.py:681
  87.4 90.2 %reduce.2 = (f32[2,8,2,16,960]{4,3,2,1,0:T(8,128)}, f32[2,32,20,40,384]{4,3,2,1,0:T(8,128)}) custom-call(bf16[8,3,256,256]{3,2,1,0:T(8,128)(2,1)} %constant.28.clone.m_hbm, f32[2,20,8,2,2,8,384]{6,5,4,3,2,1,0:T(8,128)} %bitcast.12, f32[16,32,20,40,48]{4,3,2,1,0:T(8,128)} %bitcast.x_ref, bf16[2,3,160,176]{3,2,1,0:T(8,128)(2,1)} %point_table.1.w_ref), custom_call_target="tpu_custom_call" | custom-call | tf_op jit(solution)/shard_map/reduce/pallas_call | solution.py:702
  177.6 110.8 %gather.2 = (bf16[2,3,20,8,2,2,8,384]{7,6,5,4,3,2,1,0:T(8,128)(2,1)}, f32[2,32,20,40,384]{4,3,2,1,0:T(8,128)}) custom-call(bf16[8,3,256,256]{3,2,1,0:T(8,128)(2,1)} %constant.29.clone.m_hbm, f32[2,8,2,16,960]{4,3,2,1,0:T(8,128)} %get-tuple-element.15.s_ref, f32[2,16,16,20,8,20]{5,4,3,2,1,0:T(8,128)} %bitcast.8, ...), custom_call_target="tpu_custom_call", output_to_operand_aliasing={{1}: (6, {})} | custom-call | tf_op jit(solution)/shard_map/gather/pallas_call | solution.py:713
  288.4 118.3 %layer_first.1 = (f32[2,32,20,40,384]{4,3,2,1,0:T(8,128)}, f32[2,20,256,384]{3,2,1,0:T(8,128)}) custom-call(f32[2,32,20,40,384]{4,3,2,1,0:T(8,128)} %get-tuple-element.17.refs_0_, bf16[2,3,20,256,384]{4,3,2,1,0:T(8,128)(2,1)} %bitcast.14, bf16[8,96,192]{2,1,0:T(8,128)(2,1)} %constant.23.clone.refs_2_, bf16[8,128,192]{2,1,0:T(8,128)(2,1)} %constant.24.clone.refs_3_, ...), custom_call_target="tpu_custom_call" | custom-call | tf_op jit(solution)/shard_map/layer_first/pallas_call | solution.py:730
  406.7 84.1 %reduce.3 = (f32[2,8,2,16,960]{4,3,2,1,0:T(8,128)}, f32[2,32,20,40,384]{4,3,2,1,0:T(8,128)}) custom-call(bf16[8,3,256,256]{3,2,1,0:T(8,128)(2,1)} %constant.28.clone.m_hbm, f32[2,20,8,2,2,8,384]{6,5,4,3,2,1,0:T(8,128)} %bitcast.15, f32[2,32,20,40,384]{4,3,2,1,0:T(8,128)} %get-tuple-element.20.x_ref, bf16[2,3,160,176]{3,2,1,0:T(8,128)(2,1)} %point_table.1.w_ref), custom_call_target="tpu_custom_call" | custom-call | tf_op jit(solution)/shard_map/reduce/pallas_call | solution.py:702
  490.8 95.6 %gather.3 = (bf16[2,3,20,8,2,2,8,384]{7,6,5,4,3,2,1,0:T(8,128)(2,1)}, f32[2,32,20,40,384]{4,3,2,1,0:T(8,128)}) custom-call(bf16[8,3,256,256]{3,2,1,0:T(8,128)(2,1)} %constant.29.clone.m_hbm, f32[2,8,2,16,960]{4,3,2,1,0:T(8,128)} %get-tuple-element.21.s_ref, f32[2,16,16,20,8,20]{5,4,3,2,1,0:T(8,128)} %bitcast.9, ...), custom_call_target="tpu_custom_call", output_to_operand_aliasing={{1}: (6, {})} | custom-call | tf_op jit(solution)/shard_map/gather/pallas_call | solution.py:713
  586.3 112.1 %layer_last.1 = f32[16,32,20,40,48]{4,3,2,1,0:T(8,128)} custom-call(f32[2,32,20,40,384]{4,3,2,1,0:T(8,128)} %get-tuple-element.23.refs_0_, bf16[2,3,20,256,384]{4,3,2,1,0:T(8,128)(2,1)} %bitcast.13, bf16[8,96,192]{2,1,0:T(8,128)(2,1)} %constant.23.clone.refs_2_, bf16[8,128,192]{2,1,0:T(8,128)(2,1)} %constant.24.clone.refs_3_, ...), custom_call_target="tpu_custom_call" | custom-call | tf_op jit(solution)/shard_map/layer_last/pallas_call | solution.py:737

commit v8 on v7

--- a/solution.py
+++ b/solution.py
@@ -24,6 +24,9 @@
 CLASS_ROWS = (0, 64, 160, 256)
 LANES = 128
 ADDENDS = 3
+CUT = 96
+HALF = 0.5
+REDUCE_UNITS = (20, 22)
 REDUCE_CHUNKS = ((0, 2), (2, 6), (6, 8))
 GATHER_CHUNKS = ((0, 4), (4, 6), (6, 8))
 MIX_CHUNKS = ((0, 4), (4, 8))
@@ -74,7 +77,7 @@
     cols = []
     for kz in group:
         t, s = yz_angles(kz, y_pos, ky, grid_y, grid_z).transpose(1, 2, 0), kz_sign(kz)
-        w = (0.5 if kz == 0 else 1.0) / points
+        w = (HALF if kz == 0 else 1.0) / points
         real, imag = [w * np.cos(t)], [-w * np.sin(t)]
         if s:
             real.append(s * SIN_1 * w * np.sin(t))
@@ -231,8 +234,8 @@
 def channel_product(first, x_ref, w_ref, p_ref, d_ref):
     blocks, width, depth, lanes = p_ref.shape
     rows = width * SUB
-    ones = jnp.ones((w_ref.shape[-1] - rows, blocks * lanes), BF16)
-    full, (a, b, c) = w_ref[0, 0], (w_ref[0, i, :, :rows] for i in range(ADDENDS))
+    ones = jnp.ones((w_ref.shape[-1] + CUT - 2 * rows, blocks * lanes), BF16)
+    left = [w_ref[0, i] for i in range(w_ref.shape[1])]
 
     def load(j):
         z = slice(j * SUB, (j + 1) * SUB)
@@ -244,7 +247,8 @@
 
     def product(j):
         d1, d2, d3 = split3(d_ref[j % 2])
-        p = dot(full, jnp.concatenate([d1, ones], 0)) + dot(a, d2) + dot(a, d3) + dot(b, d1) + dot(b, d2) + dot(c, d1)
+        low, high = jnp.concatenate([d1, d2[:CUT]], 0), jnp.concatenate([d2[CUT:], d3, ones], 0)
+        p = functools.reduce(jnp.add, [dot(w, low if i < ADDENDS else high) for i, w in enumerate(left)])
         for y in range(blocks):
             p_ref[y, :, j * SUB:(j + 1) * SUB, :] = p[:, y * lanes:(y + 1) * lanes].reshape(width, SUB, lanes)
     count = depth // SUB
@@ -262,8 +266,10 @@
     batch = lanes // X_GROUP
     start = pl.program_id(2) * width
     if first:
-        *tabs, v_ref, f_hbm, a_ref, u_ref, f_ref, sem = tabs
+        *tabs, v_ref, f_hbm, a_ref, u_ref, f_all, f_sem = tabs
         v_ref = v_ref.at[0]
+        group = pl.program_id(0)
+        f_ref = f_all.at[group]
 
         @pl.when((pl.program_id(1) == 0) & (start == 0))
         def _():
@@ -308,9 +314,14 @@
     if first:
         @pl.when((pl.program_id(1) == pl.num_programs(1) - 1) & (start > 0))
         def _():
-            copy = pltpu.make_async_copy(f_ref, f_hbm.at[pl.program_id(0)], sem)
-            copy.start()
-            copy.wait()
+            copies = [pltpu.make_async_copy(f_all.at[g], f_hbm.at[g], f_sem.at[g]) for g in range(f_all.shape[0])]
+            for g, copy in enumerate(copies):
+                pl.when(group == g)(copy.start)
+
+            @pl.when(group == len(copies) - 1)
+            def _():
+                for copy in copies:
+                    copy.wait()
 
 
 def store_field(o_ref, y, c, z, row, batch):
@@ -609,15 +620,16 @@
         return jnp.where(at[axis] // SUB == at[1 - axis], 1.0, 0.0).astype(BF16)
     down, across = spread((rows, width), 0), spread((width, rows), 1)
     at = [lax.broadcasted_iota(jnp.int32, (rows, rows), k) % SUB for k in range(2)]
-    column = lax.broadcasted_iota(jnp.int32, (rows, 2 * SUB), 1)
+    column = lax.broadcasted_iota(jnp.int32, (rows, out_ref.shape[-1] + CUT - 2 * rows), 1)
     for layer in range(layers):
-        weights, biases = split3(0.5 * w_ref[layer].T), split3(0.5 * b_ref[layer:layer + 1])
+        weights, biases = split3(HALF * w_ref[layer].T), split3(HALF * b_ref[layer:layer + 1])
         shift = sum(jnp.where(column == i, jnp.sum(down.astype(F32) * b.astype(F32), 1, keepdims=True), 0.0)
                     for i, b in enumerate(biases))
-        for i, w in enumerate(weights):
-            wide = dot(dot(down, w).astype(BF16), across)
-            wide = jnp.where(at[0] == at[1], wide, 0.0)
-            out_ref[layer, i] = jnp.concatenate([wide, shift if i == 0 else jnp.zeros_like(shift)], 1).astype(BF16)
+        a, b, c = (jnp.where(at[0] == at[1], dot(dot(down, w).astype(BF16), across), 0.0) for w in weights)
+        none = jnp.zeros_like(a)
+        for i, parts in enumerate(((a, a[:, :CUT]), (b, b[:, :CUT]), (c, none[:, :CUT]),
+                                   (a[:, CUT:], a, shift), (b[:, CUT:], none, jnp.zeros_like(shift)))):
+            out_ref[layer, i] = jnp.concatenate(parts, 1).astype(BF16)
 
 
 def solution(mesh):
@@ -651,7 +663,7 @@
         fwd_x, inv_x = x_tables(fwd_x, 0), x_tables(inv_x, 1)
         params = pltpu.CompilerParams(vmem_limit_bytes=VMEM_LIMIT)
         point_w = pl.pallas_call(
-            point_table_kernel, out_shape=jax.ShapeDtypeStruct((2, ADDENDS, width * SUB, width * SUB + 2 * SUB), BF16),
+            point_table_kernel, out_shape=jax.ShapeDtypeStruct((2, 5, width * SUB, width * SUB + CUT), BF16),
             compiler_params=params, name='point_table')(mix_weight, bias)
 
         real_w, imag_w = (jnp.swapaxes(w, 3, 4) for w in (spec_real, spec_imag))
@@ -670,10 +682,13 @@
 
         units = y_loc // HALF_BLOCK
 
-        def half_block(first, half, start):
+        def unit_block(first, steps, base, count):
             shape = (HALF_BLOCK, width, grid_z) + ((batch,) if first else (lanes,))
-            return pl.BlockSpec((X_GROUP if first else 1,) + shape,
-                                lambda j: (half, jnp.clip(j - start, 0, units - 1), 0, 0, 0))
+
+            def index_map(j):
+                n = jnp.clip(j - steps, 0, count - 1) + base
+                return n // units, n % units, 0, 0, 0
+            return pl.BlockSpec((X_GROUP if first else 1,) + shape, index_map)
 
         def table_specs(tables):
             return [block((1,) + t.shape[1:], 'joo') for t in tables]
@@ -698,24 +713,25 @@
             return pltpu.CompilerParams(vmem_limit_bytes=VMEM_LIMIT, collective_id=number, has_side_effects=True)
 
         def across(f, layer, source):
-            first = layer == 0
+            first, early = layer == 0, REDUCE_UNITS[layer]
+            late = groups * units - early
             s, p = pl.pallas_call(
-                functools.partial(reduce_kernel, first), grid=(slots + units,),
+                functools.partial(reduce_kernel, first), grid=(slots + early,),
                 out_shape=(jax.ShapeDtypeStruct((own,) + unit, F32), mid_shape),
                 in_specs=[anywhere,
                           block((groups, width, 1, 2, halves, SUB, lanes), 'oosoooo', lambda j: jnp.minimum(j, slots - 1)),
-                          half_block(first, 0, slots), w_block(layer)],
-                out_specs=(own_block, half_block(False, 0, slots)),
+                          unit_block(first, slots, 0, early), w_block(layer)],
+                out_specs=(own_block, unit_block(False, slots, 0, early)),
                 scratch_shapes=x_scratch + [half_rows] + [pltpu.VMEM((n,) + unit, F32) for n in (n_kx, SUB, 4, 2)]
                 + [dma((slots, SUB))] * 2 + [dma((len(REDUCE_CHUNKS), n)) for n in (4, 4, 2, 2)],
                 compiler_params=exchange(2 * layer), name='reduce')(
                     fwd_x, f.reshape(groups, width, slots, 2, halves, SUB, lanes), source, point_w)
             parts, p = pl.pallas_call(
-                functools.partial(gather_kernel, first, layer), grid=(units + 6,),
+                functools.partial(gather_kernel, first, layer), grid=(late + 6,),
                 out_shape=(jax.ShapeDtypeStruct((groups, ADDENDS, width, slots, 2, halves, SUB, lanes), BF16), mid_shape),
-                in_specs=[anywhere, own_block, anywhere, anywhere, half_block(first, 1, 2), w_block(layer), anywhere],
-                out_specs=(block((groups, ADDENDS, width, 1, 2, halves, SUB, lanes), 'ooosoooo', lambda j: jnp.maximum(j - units + 2, 0)),
-                           half_block(False, 1, 2)),
+                in_specs=[anywhere, own_block, anywhere, anywhere, unit_block(first, 2, early, late), w_block(layer), anywhere],
+                out_specs=(block((groups, ADDENDS, width, 1, 2, halves, SUB, lanes), 'ooosoooo', lambda j: jnp.maximum(j - late + 2, 0)),
+                           unit_block(False, 2, early, late)),
                 input_output_aliases={6: 1},
                 scratch_shapes=x_scratch + [half_rows, pltpu.VMEM((n_kx,) + unit, F32)]
                 + [pltpu.VMEM((own, n_ky, width, SUB, width), F32)] * 2
@@ -731,7 +747,7 @@
             functools.partial(layer_kernel, FIRST_UNIT, True), grid=grid, out_shape=(mid_shape, spec_shape),
             in_specs=[mid_block, part_block] + table_specs(inv) + table_specs(fwd),
             out_specs=(mid_block, anywhere),
-            scratch_shapes=[stage(FIRST_UNIT)] * 2 + [pltpu.VMEM((width, 256, lanes), F32), pltpu.SemaphoreType.DMA],
+            scratch_shapes=[stage(FIRST_UNIT)] * 2 + [pltpu.VMEM(spec_shape.shape, F32), pltpu.SemaphoreType.DMA((groups,))],
             compiler_params=params, name='layer_first')(p, parts, *inv, *fwd)
         parts, p = across(f, 1, v1)
         out = pl.pallas_call(

time: 702 us -> 699 us (level)
  no operation moved by 1% of the time
where the time goes in v8:
time: 699 us; the launch traced here: 695 us
  Pallas kernels  693 us (99%)
    pallas_call x2, Pallas kernels, across(): pl.pallas_call(functools.partial(reduce_kernel, first), grid=(slots + ear...  188 us
    pallas_call x2, Pallas kernels, across(): pl.pallas_call(functools.partial(gather_kernel, first, layer), grid=(late...  188 us
    pallas_call x1, Pallas kernels, local_layers(): pl.pallas_call(functools.partial(layer_kernel, FIRST_UNIT, True), grid=gr...  119 us
    pallas_call x1, Pallas kernels, local_layers(): pl.pallas_call(functools.partial(layer_kernel, LAST_UNIT, False), grid=gr...  112 us
    pallas_call x1, Pallas kernels, local_layers(): pl.pallas_call(functools.partial(forward_kernel, FORWARD_UNIT), grid=grid...  83.8 us

profile of v8, /device:TPU:0, one launch (start us, length us, event | category | flops | bytes accessed | tf_op | source)
XLA Modules:
  0.0 694.7 jit_solution(1642240822644994352)
XLA Ops:
  0.0 1.3 copy.18.w_ref
  1.3 2.5 point_table.1.w_ref
  3.8 83.8 %forward.1 = f32[2,20,256,384]{3,2,1,0:T(8,128)} custom-call(f32[16,32,20,40,48]{4,3,2,1,0:T(8,128)} %bitcast.x_ref, bf16[8,64,192]{2,1,0:T(8,128)(2,1)} %constant.20.clone.t0.refs_7_, bf16[8,192,256]{2,1,0:T(8,128)(2,1)} %constant.21.clone.t1.refs_8_, bf16[8,192,256]{2,1,0:T(8,128)(2,1)} %constant.22.clone.t2.refs_9_), custom_call_target="tpu_custom_call" | custom-call | tf_op jit(solution)/shard_map/forward/pallas_call | solution.py:696
  87.6 101.5 %reduce.2 = (f32[2,8,2,16,960]{4,3,2,1,0:T(8,128)}, f32[2,32,20,40,384]{4,3,2,1,0:T(8,128)}) custom-call(bf16[8,3,256,256]{3,2,1,0:T(8,128)(2,1)} %constant.28.clone.m_hbm, f32[2,20,8,2,2,8,384]{6,5,4,3,2,1,0:T(8,128)} %bitcast.12, f32[16,32,20,40,48]{4,3,2,1,0:T(8,128)} %bitcast.x_ref, bf16[2,5,160,256]{3,2,1,0:T(8,128)(2,1)} %point_table.1.w_ref), custom_call_target="tpu_custom_call" | custom-call | tf_op jit(solution)/shard_map/reduce/pallas_call | solution.py:718
  189.1 96.5 %gather.2 = (bf16[2,3,20,8,2,2,8,384]{7,6,5,4,3,2,1,0:T(8,128)(2,1)}, f32[2,32,20,40,384]{4,3,2,1,0:T(8,128)}) custom-call(bf16[8,3,256,256]{3,2,1,0:T(8,128)(2,1)} %constant.29.clone.m_hbm, f32[2,8,2,16,960]{4,3,2,1,0:T(8,128)} %get-tuple-element.15.s_ref, f32[2,16,16,20,8,20]{5,4,3,2,1,0:T(8,128)} %bitcast.8, ...), custom_call_target="tpu_custom_call", output_to_operand_aliasing={{1}: (6, {})} | custom-call | tf_op jit(solution)/shard_map/gather/pallas_call | solution.py:729
  285.7 119.3 %layer_first.1 = (f32[2,32,20,40,384]{4,3,2,1,0:T(8,128)}, f32[2,20,256,384]{3,2,1,0:T(8,128)}) custom-call(f32[2,32,20,40,384]{4,3,2,1,0:T(8,128)} %get-tuple-element.17.refs_0_, bf16[2,3,20,256,384]{4,3,2,1,0:T(8,128)(2,1)} %bitcast.14, bf16[8,96,192]{2,1,0:T(8,128)(2,1)} %constant.23.clone.refs_2_, bf16[8,128,192]{2,1,0:T(8,128)(2,1)} %constant.24.clone.refs_3_, ...), custom_call_target="tpu_custom_call" | custom-call | tf_op jit(solution)/shard_map/layer_first/pallas_call | solution.py:746
  405.0 86.5 %reduce.3 = (f32[2,8,2,16,960]{4,3,2,1,0:T(8,128)}, f32[2,32,20,40,384]{4,3,2,1,0:T(8,128)}) custom-call(bf16[8,3,256,256]{3,2,1,0:T(8,128)(2,1)} %constant.28.clone.m_hbm, f32[2,20,8,2,2,8,384]{6,5,4,3,2,1,0:T(8,128)} %bitcast.15, f32[2,32,20,40,384]{4,3,2,1,0:T(8,128)} %get-tuple-element.20.x_ref, bf16[2,5,160,256]{3,2,1,0:T(8,128)(2,1)} %point_table.1.w_ref), custom_call_target="tpu_custom_call" | custom-call | tf_op jit(solution)/shard_map/reduce/pallas_call | solution.py:718
  491.6 91.1 %gather.3 = (bf16[2,3,20,8,2,2,8,384]{7,6,5,4,3,2,1,0:T(8,128)(2,1)}, f32[2,32,20,40,384]{4,3,2,1,0:T(8,128)}) custom-call(bf16[8,3,256,256]{3,2,1,0:T(8,128)(2,1)} %constant.29.clone.m_hbm, f32[2,8,2,16,960]{4,3,2,1,0:T(8,128)} %get-tuple-element.21.s_ref, f32[2,16,16,20,8,20]{5,4,3,2,1,0:T(8,128)} %bitcast.9, ...), custom_call_target="tpu_custom_call", output_to_operand_aliasing={{1}: (6, {})} | custom-call | tf_op jit(solution)/shard_map/gather/pallas_call | solution.py:729
  582.6 112.1 %layer_last.1 = f32[16,32,20,40,48]{4,3,2,1,0:T(8,128)} custom-call(f32[2,32,20,40,384]{4,3,2,1,0:T(8,128)} %get-tuple-element.23.refs_0_, bf16[2,3,20,256,384]{4,3,2,1,0:T(8,128)(2,1)} %bitcast.13, bf16[8,96,192]{2,1,0:T(8,128)(2,1)} %constant.23.clone.refs_2_, bf16[8,128,192]{2,1,0:T(8,128)(2,1)} %constant.24.clone.refs_3_, ...), custom_call_target="tpu_custom_call" | custom-call | tf_op jit(solution)/shard_map/layer_last/pallas_call | solution.py:753

commit v9 on v8

--- a/solution.py
+++ b/solution.py
@@ -27,7 +27,7 @@
 CUT = 96
 HALF = 0.5
 REDUCE_UNITS = (20, 22)
-REDUCE_CHUNKS = ((0, 2), (2, 6), (6, 8))
+REDUCE_CHUNKS = ((0, 1), (1, 3), (3, 8))
 GATHER_CHUNKS = ((0, 4), (4, 6), (6, 8))
 MIX_CHUNKS = ((0, 4), (4, 8))
 FORWARD_UNIT = (2, 10)
@@ -264,14 +264,14 @@
     p_ref = p_ref.at[0]
     width, lanes = p_ref.shape[1], p_ref.shape[-1]
     batch = lanes // X_GROUP
-    start = pl.program_id(2) * width
+    start = pl.program_id(1) * width
     if first:
         *tabs, v_ref, f_hbm, a_ref, u_ref, f_all, f_sem = tabs
         v_ref = v_ref.at[0]
         group = pl.program_id(0)
-        f_ref = f_all.at[group]
-
-        @pl.when((pl.program_id(1) == 0) & (start == 0))
+        f_ref = f_all.at[group, pl.ds(start, width)]
+
+        @pl.when(pl.program_id(2) == 0)
         def _():
             zero_spectrum(f_ref)
     else:
@@ -303,16 +303,16 @@
         count = per_step // pair
         for n in range(count + 2):
             if n < count:
-                inverse_stage(s_ref, start + c + n * pair, pair, inv, a_ref.at[n])
+                inverse_stage(s_ref, c + n * pair, pair, inv, a_ref.at[n])
             if 0 < n <= count:
                 activate(c + (n - 1) * pair, n - 1)
             if first and n > 1:
-                forward_stage(u_ref.at[n - 2], fwd, f_ref, start + c + (n - 2) * pair, pair)
+                forward_stage(u_ref.at[n - 2], fwd, f_ref, c + (n - 2) * pair, pair)
         return 0
     lax.fori_loop(0, width // per_step, body, 0)
 
     if first:
-        @pl.when((pl.program_id(1) == pl.num_programs(1) - 1) & (start > 0))
+        @pl.when((pl.program_id(2) == pl.num_programs(2) - 1) & (start > 0))
         def _():
             copies = [pltpu.make_async_copy(f_all.at[g], f_hbm.at[g], f_sem.at[g]) for g in range(f_all.shape[0])]
             for g, copy in enumerate(copies):
@@ -451,6 +451,10 @@
                                         device_id_type=pl.DeviceIdType.MESH)
 
 
+def run(event):
+    event()
+
+
 def step_and_last():
     return pl.program_id(0), pl.num_programs(0) - 1
 
@@ -513,11 +517,11 @@
         me.enter()
         table.wait()
 
-    events = ((0, begin), (2, lambda: from_core(0)), (slots - 3, lambda: from_chip(0)), (slots - 2, lambda: from_core(1)),
-              (slots, lambda: from_core(2)), (slots + 3, lambda: finish(0)), (slots + 5, lambda: from_chip(1)),
-              (slots + 12, lambda: from_chip(2)))
+    events = ((0, begin), (1, lambda: from_core(0)), (3, lambda: (from_chip(0), from_core(1))),
+              (slots, lambda: (from_chip(1), from_core(2))), (slots + 2, lambda: finish(0)), (slots + 6, lambda: finish(1)),
+              (slots + 10, lambda: from_chip(2)))
     for at, event in events:
-        pl.when(step == at)(event)
+        pl.when(step == at)(functools.partial(run, event))
 
     @pl.when(step < slots)
     def _():
@@ -531,7 +535,6 @@
 
     @pl.when(step == last)
     def _():
-        finish(1)
         finish(2)
         for copies in [to_core(slot) for slot in range(slots)] + two + three:
             for copy in copies:
@@ -668,12 +671,12 @@
 
         real_w, imag_w = (jnp.swapaxes(w, 3, 4) for w in (spec_real, spec_imag))
         v = jnp.swapaxes(jnp.moveaxis(field, 0, -1), 2, 3)
-        grid = (groups, blocks, 2)
+        grid = (groups, 2, blocks)
         part_width = width // 2
         spec_shape = jax.ShapeDtypeStruct((groups, width, 256, lanes), F32)
-        in_block = block((X_GROUP, Y_BLOCK, part_width, grid_z, batch), 'ijkoo')
-        mid_block = block((1, Y_BLOCK, part_width, grid_z, lanes), 'ijkoo')
-        part_block = block((1, ADDENDS, width, CLASS_ROWS[-1], lanes), 'ioooo')
+        in_block = block((X_GROUP, Y_BLOCK, part_width, grid_z, batch), 'ikjoo')
+        mid_block = block((1, Y_BLOCK, part_width, grid_z, lanes), 'ikjoo')
+        part_block = block((1, ADDENDS, part_width, CLASS_ROWS[-1], lanes), 'iojoo')
         mid_shape = jax.ShapeDtypeStruct((groups, y_loc, width, grid_z, lanes), F32)
         anywhere = pl.BlockSpec(memory_space=pl.ANY)
 
@@ -690,12 +693,12 @@
                 return n // units, n % units, 0, 0, 0
             return pl.BlockSpec((X_GROUP if first else 1,) + shape, index_map)
 
-        def table_specs(tables):
-            return [block((1,) + t.shape[1:], 'joo') for t in tables]
+        def table_specs(tables, index):
+            return [block((1,) + t.shape[1:], index) for t in tables]
 
         f = pl.pallas_call(
-            functools.partial(forward_kernel, FORWARD_UNIT), grid=grid[:2], out_shape=spec_shape,
-            in_specs=[block((X_GROUP, Y_BLOCK, width, grid_z, batch), 'ijooo')] + table_specs(fwd),
+            functools.partial(forward_kernel, FORWARD_UNIT), grid=(groups, blocks), out_shape=spec_shape,
+            in_specs=[block((X_GROUP, Y_BLOCK, width, grid_z, batch), 'ijooo')] + table_specs(fwd, 'joo'),
             out_specs=block((1, width, 256, lanes), 'iooo'),
             scratch_shapes=[stage(FORWARD_UNIT)], compiler_params=params, name='forward')(v, *fwd)
 
@@ -745,7 +748,7 @@
         parts, p = across(f, 0, v)
         v1, f = pl.pallas_call(
             functools.partial(layer_kernel, FIRST_UNIT, True), grid=grid, out_shape=(mid_shape, spec_shape),
-            in_specs=[mid_block, part_block] + table_specs(inv) + table_specs(fwd),
+            in_specs=[mid_block, part_block] + table_specs(inv + fwd, 'koo'),
             out_specs=(mid_block, anywhere),
             scratch_shapes=[stage(FIRST_UNIT)] * 2 + [pltpu.VMEM(spec_shape.shape, F32), pltpu.SemaphoreType.DMA((groups,))],
             compiler_params=params, name='layer_first')(p, parts, *inv, *fwd)
@@ -753,7 +756,7 @@
         out = pl.pallas_call(
             functools.partial(layer_kernel, LAST_UNIT, False), grid=grid,
             out_shape=jax.ShapeDtypeStruct((x_loc, y_loc, width, grid_z, batch), F32),
-            in_specs=[mid_block, part_block] + table_specs(inv), out_specs=in_block, scratch_shapes=[stage(LAST_UNIT)],
+            in_specs=[mid_block, part_block] + table_specs(inv, 'koo'), out_specs=in_block, scratch_shapes=[stage(LAST_UNIT)],
             compiler_params=params, name='layer_last')(p, parts, *inv)
         return jnp.moveaxis(jnp.swapaxes(out, 2, 3), -1, 0)
 

time: 699 us -> 706 us (1.010)
  Pallas kernels: 693 us -> 701 us
where the time goes in v9:
time: 706 us; the launch traced here: 702 us
  Pallas kernels  701 us (99%)
    pallas_call x2, Pallas kernels, across(): pl.pallas_call(functools.partial(reduce_kernel, first), grid=(slots + ear...  192 us
    pallas_call x2, Pallas kernels, across(): pl.pallas_call(functools.partial(gather_kernel, first, layer), grid=(late...  188 us
    pallas_call x1, Pallas kernels, local_layers(): pl.pallas_call(functools.partial(layer_kernel, LAST_UNIT, False), grid=gr...  118 us
    pallas_call x1, Pallas kernels, local_layers(): pl.pallas_call(functools.partial(layer_kernel, FIRST_UNIT, True), grid=gr...  116 us
    pallas_call x1, Pallas kernels, local_layers(): pl.pallas_call(functools.partial(forward_kernel, FORWARD_UNIT), grid=(gro...  83.8 us

profile of v9, /device:TPU:0, one launch (start us, length us, event | category | flops | bytes accessed | tf_op | source)
XLA Modules:
  0.0 702.3 jit_solution(3079561318634275036)
XLA Ops:
  0.0 1.3 copy.18.w_ref
  1.3 2.5 point_table.1.w_ref
  3.8 83.8 %forward.1 = f32[2,20,256,384]{3,2,1,0:T(8,128)} custom-call(f32[16,32,20,40,48]{4,3,2,1,0:T(8,128)} %bitcast.x_ref, bf16[8,64,192]{2,1,0:T(8,128)(2,1)} %constant.20.clone.t0.refs_7_, bf16[8,192,256]{2,1,0:T(8,128)(2,1)} %constant.21.clone.t1.refs_8_, bf16[8,192,256]{2,1,0:T(8,128)(2,1)} %constant.22.clone.t2.refs_9_), custom_call_target="tpu_custom_call" | custom-call | tf_op jit(solution)/shard_map/forward/pallas_call | solution.py:699
  87.6 105.8 %reduce.2 = (f32[2,8,2,16,960]{4,3,2,1,0:T(8,128)}, f32[2,32,20,40,384]{4,3,2,1,0:T(8,128)}) custom-call(bf16[8,3,256,256]{3,2,1,0:T(8,128)(2,1)} %constant.28.clone.m_hbm, f32[2,20,8,2,2,8,384]{6,5,4,3,2,1,0:T(8,128)} %bitcast.12, f32[16,32,20,40,48]{4,3,2,1,0:T(8,128)} %bitcast.x_ref, bf16[2,5,160,256]{3,2,1,0:T(8,128)(2,1)} %point_table.1.w_ref), custom_call_target="tpu_custom_call" | custom-call | tf_op jit(solution)/shard_map/reduce/pallas_call | solution.py:721
  193.4 96.4 %gather.2 = (bf16[2,3,20,8,2,2,8,384]{7,6,5,4,3,2,1,0:T(8,128)(2,1)}, f32[2,32,20,40,384]{4,3,2,1,0:T(8,128)}) custom-call(bf16[8,3,256,256]{3,2,1,0:T(8,128)(2,1)} %constant.29.clone.m_hbm, f32[2,8,2,16,960]{4,3,2,1,0:T(8,128)} %get-tuple-element.15.s_ref, f32[2,16,16,20,8,20]{5,4,3,2,1,0:T(8,128)} %bitcast.8, ...), custom_call_target="tpu_custom_call", output_to_operand_aliasing={{1}: (6, {})} | custom-call | tf_op jit(solution)/shard_map/gather/pallas_call | solution.py:732
  289.8 116.5 %layer_first.1 = (f32[2,32,20,40,384]{4,3,2,1,0:T(8,128)}, f32[2,20,256,384]{3,2,1,0:T(8,128)}) custom-call(f32[2,32,20,40,384]{4,3,2,1,0:T(8,128)} %get-tuple-element.17.refs_0_, bf16[2,3,20,256,384]{4,3,2,1,0:T(8,128)(2,1)} %bitcast.14, bf16[8,96,192]{2,1,0:T(8,128)(2,1)} %constant.23.clone.refs_2_, bf16[8,128,192]{2,1,0:T(8,128)(2,1)} %constant.24.clone.refs_3_, ...), custom_call_target="tpu_custom_call" | custom-call | tf_op jit(solution)/shard_map/layer_first/pallas_call | solution.py:749
  406.3 86.4 %reduce.3 = (f32[2,8,2,16,960]{4,3,2,1,0:T(8,128)}, f32[2,32,20,40,384]{4,3,2,1,0:T(8,128)}) custom-call(bf16[8,3,256,256]{3,2,1,0:T(8,128)(2,1)} %constant.28.clone.m_hbm, f32[2,20,8,2,2,8,384]{6,5,4,3,2,1,0:T(8,128)} %bitcast.15, f32[2,32,20,40,384]{4,3,2,1,0:T(8,128)} %get-tuple-element.20.x_ref, bf16[2,5,160,256]{3,2,1,0:T(8,128)(2,1)} %point_table.1.w_ref), custom_call_target="tpu_custom_call" | custom-call | tf_op jit(solution)/shard_map/reduce/pallas_call | solution.py:721
  492.8 91.2 %gather.3 = (bf16[2,3,20,8,2,2,8,384]{7,6,5,4,3,2,1,0:T(8,128)(2,1)}, f32[2,32,20,40,384]{4,3,2,1,0:T(8,128)}) custom-call(bf16[8,3,256,256]{3,2,1,0:T(8,128)(2,1)} %constant.29.clone.m_hbm, f32[2,8,2,16,960]{4,3,2,1,0:T(8,128)} %get-tuple-element.21.s_ref, f32[2,16,16,20,8,20]{5,4,3,2,1,0:T(8,128)} %bitcast.9, ...), custom_call_target="tpu_custom_call", output_to_operand_aliasing={{1}: (6, {})} | custom-call | tf_op jit(solution)/shard_map/gather/pallas_call | solution.py:732
  583.9 118.3 %layer_last.1 = f32[16,32,20,40,48]{4,3,2,1,0:T(8,128)} custom-call(f32[2,32,20,40,384]{4,3,2,1,0:T(8,128)} %get-tuple-element.23.refs_0_, bf16[2,3,20,256,384]{4,3,2,1,0:T(8,128)(2,1)} %bitcast.13, bf16[8,96,192]{2,1,0:T(8,128)(2,1)} %constant.23.clone.refs_2_, bf16[8,128,192]{2,1,0:T(8,128)(2,1)} %constant.24.clone.refs_3_, ...), custom_call_target="tpu_custom_call" | custom-call | tf_op jit(solution)/shard_map/layer_last/pallas_call | solution.py:756

commit v10 on v9

--- a/solution.py
+++ b/solution.py
@@ -26,11 +26,11 @@
 ADDENDS = 3
 CUT = 96
 HALF = 0.5
-REDUCE_UNITS = (20, 22)
-REDUCE_CHUNKS = ((0, 1), (1, 3), (3, 8))
+REDUCE_UNITS = 22
+REDUCE_CHUNKS = ((0, 2), (2, 6), (6, 8))
 GATHER_CHUNKS = ((0, 4), (4, 6), (6, 8))
 MIX_CHUNKS = ((0, 4), (4, 8))
-FORWARD_UNIT = (2, 10)
+FORWARD_UNIT = (2, 20)
 FIRST_UNIT = (2, 10)
 LAST_UNIT = (1, 10)
 ROOT5_4 = math.sqrt(5.0) / 4.0
@@ -264,8 +264,8 @@
     p_ref = p_ref.at[0]
     width, lanes = p_ref.shape[1], p_ref.shape[-1]
     batch = lanes // X_GROUP
-    start = pl.program_id(1) * width
     if first:
+        start = pl.program_id(1) * width
         *tabs, v_ref, f_hbm, a_ref, u_ref, f_all, f_sem = tabs
         v_ref = v_ref.at[0]
         group = pl.program_id(0)
@@ -275,6 +275,7 @@
         def _():
             zero_spectrum(f_ref)
     else:
+        start = pl.program_id(2) * width
         *tabs, o_ref, a_ref = tabs
     inv, fwd = [t[0] for t in tabs[:5]], [t[0] for t in tabs[5:]]
     pair, per_step = unit
@@ -303,7 +304,7 @@
         count = per_step // pair
         for n in range(count + 2):
             if n < count:
-                inverse_stage(s_ref, c + n * pair, pair, inv, a_ref.at[n])
+                inverse_stage(s_ref, (0 if first else start) + c + n * pair, pair, inv, a_ref.at[n])
             if 0 < n <= count:
                 activate(c + (n - 1) * pair, n - 1)
             if first and n > 1:
@@ -451,10 +452,6 @@
                                         device_id_type=pl.DeviceIdType.MESH)
 
 
-def run(event):
-    event()
-
-
 def step_and_last():
     return pl.program_id(0), pl.num_programs(0) - 1
 
@@ -494,7 +491,7 @@
                 copies[t].wait_recv()
             to = chunk_of(s_ref, me.order[t], REDUCE_CHUNKS[h])
             add(to, to, chunk_of(r1, t, REDUCE_CHUNKS[h]))
-            if t < 4:
+            if t < len(two[h]):
                 two[h][t].start()
 
     def from_chip(h, these=(0, 1)):
@@ -502,7 +499,7 @@
             two[h][t].wait_recv()
             to = chunk_of(s_ref, me.order[4 + t], REDUCE_CHUNKS[h])
             add(to, to, chunk_of(r2, t, REDUCE_CHUNKS[h]))
-            if t < 2:
+            if t < len(three[h]):
                 three[h][t].start()
 
     def finish(h):
@@ -517,11 +514,11 @@
         me.enter()
         table.wait()
 
-    events = ((0, begin), (1, lambda: from_core(0)), (3, lambda: (from_chip(0), from_core(1))),
-              (slots, lambda: (from_chip(1), from_core(2))), (slots + 2, lambda: finish(0)), (slots + 6, lambda: finish(1)),
-              (slots + 10, lambda: from_chip(2)))
+    events = ((0, begin), (2, lambda: from_core(0)), (slots - 3, lambda: from_chip(0)), (slots - 2, lambda: from_core(1)),
+              (slots, lambda: from_core(2)), (slots + 3, lambda: finish(0)), (slots + 5, lambda: from_chip(1)),
+              (slots + 12, lambda: from_chip(2)))
     for at, event in events:
-        pl.when(step == at)(functools.partial(run, event))
+        pl.when(step == at)(event)
 
     @pl.when(step < slots)
     def _():
@@ -535,6 +532,7 @@
 
     @pl.when(step == last)
     def _():
+        finish(1)
         finish(2)
         for copies in [to_core(slot) for slot in range(slots)] + two + three:
             for copy in copies:
@@ -674,7 +672,6 @@
         grid = (groups, 2, blocks)
         part_width = width // 2
         spec_shape = jax.ShapeDtypeStruct((groups, width, 256, lanes), F32)
-        in_block = block((X_GROUP, Y_BLOCK, part_width, grid_z, batch), 'ikjoo')
         mid_block = block((1, Y_BLOCK, part_width, grid_z, lanes), 'ikjoo')
         part_block = block((1, ADDENDS, part_width, CLASS_ROWS[-1], lanes), 'iojoo')
         mid_shape = jax.ShapeDtypeStruct((groups, y_loc, width, grid_z, lanes), F32)
@@ -690,7 +687,7 @@
 
             def index_map(j):
                 n = jnp.clip(j - steps, 0, count - 1) + base
-                return n // units, n % units, 0, 0, 0
+                return n // units, n % units, *(0,) * len(shape[1:])
             return pl.BlockSpec((X_GROUP if first else 1,) + shape, index_map)
 
         def table_specs(tables, index):
@@ -716,7 +713,7 @@
             return pltpu.CompilerParams(vmem_limit_bytes=VMEM_LIMIT, collective_id=number, has_side_effects=True)
 
         def across(f, layer, source):
-            first, early = layer == 0, REDUCE_UNITS[layer]
+            first, early = layer == 0, REDUCE_UNITS
             late = groups * units - early
             s, p = pl.pallas_call(
                 functools.partial(reduce_kernel, first), grid=(slots + early,),
@@ -754,9 +751,11 @@
             compiler_params=params, name='layer_first')(p, parts, *inv, *fwd)
         parts, p = across(f, 1, v1)
         out = pl.pallas_call(
-            functools.partial(layer_kernel, LAST_UNIT, False), grid=grid,
+            functools.partial(layer_kernel, LAST_UNIT, False), grid=(groups, blocks, 2),
             out_shape=jax.ShapeDtypeStruct((x_loc, y_loc, width, grid_z, batch), F32),
-            in_specs=[mid_block, part_block] + table_specs(inv, 'koo'), out_specs=in_block, scratch_shapes=[stage(LAST_UNIT)],
+            in_specs=[block((1, Y_BLOCK, part_width, grid_z, lanes), 'ijkoo'),
+                      block((1, ADDENDS, width, CLASS_ROWS[-1], lanes), 'ioooo')] + table_specs(inv, 'joo'),
+            out_specs=block((X_GROUP, Y_BLOCK, part_width, grid_z, batch), 'ijkoo'), scratch_shapes=[stage(LAST_UNIT)],
             compiler_params=params, name='layer_last')(p, parts, *inv)
         return jnp.moveaxis(jnp.swapaxes(out, 2, 3), -1, 0)
 

time: 706 us -> 698 us (0.989)
  Pallas kernels: 701 us -> 693 us
where the time goes in v10:
time: 698 us; the launch traced here: 694 us
  Pallas kernels  693 us (99%)
    pallas_call x2, Pallas kernels, across(): pl.pallas_call(functools.partial(reduce_kernel, first), grid=(slots + ear...  194 us
    pallas_call x2, Pallas kernels, across(): pl.pallas_call(functools.partial(gather_kernel, first, layer), grid=(late...  188 us
    pallas_call x1, Pallas kernels, local_layers(): pl.pallas_call(functools.partial(layer_kernel, FIRST_UNIT, True), grid=gr...  116 us
    pallas_call x1, Pallas kernels, local_layers(): pl.pallas_call(functools.partial(layer_kernel, LAST_UNIT, False), grid=(g...  112 us
    pallas_call x1, Pallas kernels, local_layers(): pl.pallas_call(functools.partial(forward_kernel, FORWARD_UNIT), grid=(gro...  79.5 us

profile of v10, /device:TPU:0, one launch (start us, length us, event | category | flops | bytes accessed | tf_op | source)
XLA Modules:
  0.0 693.9 jit_solution(6377348136012239919)
XLA Ops:
  0.0 1.3 copy.18.w_ref
  1.3 2.5 point_table.1.w_ref
  3.8 79.5 %forward.1 = f32[2,20,256,384]{3,2,1,0:T(8,128)} custom-call(f32[16,32,20,40,48]{4,3,2,1,0:T(8,128)} %bitcast.x_ref, bf16[8,64,192]{2,1,0:T(8,128)(2,1)} %constant.20.clone.t0.refs_7_, bf16[8,192,256]{2,1,0:T(8,128)(2,1)} %constant.21.clone.t1.refs_8_, bf16[8,192,256]{2,1,0:T(8,128)(2,1)} %constant.22.clone.t2.refs_9_), custom_call_target="tpu_custom_call" | custom-call | tf_op jit(solution)/shard_map/forward/pallas_call | solution.py:696
  83.3 107.9 %reduce.2 = (f32[2,8,2,16,960]{4,3,2,1,0:T(8,128)}, f32[2,32,20,40,384]{4,3,2,1,0:T(8,128)}) custom-call(bf16[8,3,256,256]{3,2,1,0:T(8,128)(2,1)} %constant.28.clone.m_hbm, f32[2,20,8,2,2,8,384]{6,5,4,3,2,1,0:T(8,128)} %bitcast.12, f32[16,32,20,40,48]{4,3,2,1,0:T(8,128)} %bitcast.x_ref, bf16[2,5,160,256]{3,2,1,0:T(8,128)(2,1)} %point_table.1.w_ref), custom_call_target="tpu_custom_call" | custom-call | tf_op jit(solution)/shard_map/reduce/pallas_call | solution.py:718
  191.2 96.5 %gather.2 = (bf16[2,3,20,8,2,2,8,384]{7,6,5,4,3,2,1,0:T(8,128)(2,1)}, f32[2,32,20,40,384]{4,3,2,1,0:T(8,128)}) custom-call(bf16[8,3,256,256]{3,2,1,0:T(8,128)(2,1)} %constant.29.clone.m_hbm, f32[2,8,2,16,960]{4,3,2,1,0:T(8,128)} %get-tuple-element.15.s_ref, f32[2,16,16,20,8,20]{5,4,3,2,1,0:T(8,128)} %bitcast.8, ...), custom_call_target="tpu_custom_call", output_to_operand_aliasing={{1}: (6, {})} | custom-call | tf_op jit(solution)/shard_map/gather/pallas_call | solution.py:729
  287.7 116.5 %layer_first.1 = (f32[2,32,20,40,384]{4,3,2,1,0:T(8,128)}, f32[2,20,256,384]{3,2,1,0:T(8,128)}) custom-call(f32[2,32,20,40,384]{4,3,2,1,0:T(8,128)} %get-tuple-element.17.refs_0_, bf16[2,3,20,256,384]{4,3,2,1,0:T(8,128)(2,1)} %bitcast.14, bf16[8,96,192]{2,1,0:T(8,128)(2,1)} %constant.23.clone.refs_2_, bf16[8,128,192]{2,1,0:T(8,128)(2,1)} %constant.24.clone.refs_3_, ...), custom_call_target="tpu_custom_call" | custom-call | tf_op jit(solution)/shard_map/layer_first/pallas_call | solution.py:746
  404.2 86.6 %reduce.3 = (f32[2,8,2,16,960]{4,3,2,1,0:T(8,128)}, f32[2,32,20,40,384]{4,3,2,1,0:T(8,128)}) custom-call(bf16[8,3,256,256]{3,2,1,0:T(8,128)(2,1)} %constant.28.clone.m_hbm, f32[2,20,8,2,2,8,384]{6,5,4,3,2,1,0:T(8,128)} %bitcast.15, f32[2,32,20,40,384]{4,3,2,1,0:T(8,128)} %get-tuple-element.20.x_ref, bf16[2,5,160,256]{3,2,1,0:T(8,128)(2,1)} %point_table.1.w_ref), custom_call_target="tpu_custom_call" | custom-call | tf_op jit(solution)/shard_map/reduce/pallas_call | solution.py:718
  490.8 91.0 %gather.3 = (bf16[2,3,20,8,2,2,8,384]{7,6,5,4,3,2,1,0:T(8,128)(2,1)}, f32[2,32,20,40,384]{4,3,2,1,0:T(8,128)}) custom-call(bf16[8,3,256,256]{3,2,1,0:T(8,128)(2,1)} %constant.29.clone.m_hbm, f32[2,8,2,16,960]{4,3,2,1,0:T(8,128)} %get-tuple-element.21.s_ref, f32[2,16,16,20,8,20]{5,4,3,2,1,0:T(8,128)} %bitcast.9, ...), custom_call_target="tpu_custom_call", output_to_operand_aliasing={{1}: (6, {})} | custom-call | tf_op jit(solution)/shard_map/gather/pallas_call | solution.py:729
  581.8 112.1 %layer_last.1 = f32[16,32,20,40,48]{4,3,2,1,0:T(8,128)} custom-call(f32[2,32,20,40,384]{4,3,2,1,0:T(8,128)} %get-tuple-element.23.refs_0_, bf16[2,3,20,256,384]{4,3,2,1,0:T(8,128)(2,1)} %bitcast.13, bf16[8,96,192]{2,1,0:T(8,128)(2,1)} %constant.23.clone.refs_2_, bf16[8,128,192]{2,1,0:T(8,128)(2,1)} %constant.24.clone.refs_3_, ...), custom_call_target="tpu_custom_call" | custom-call | tf_op jit(solution)/shard_map/layer_last/pallas_call | solution.py:753

commit v11 on v10

--- a/solution.py
+++ b/solution.py
@@ -26,7 +26,7 @@
 ADDENDS = 3
 CUT = 96
 HALF = 0.5
-REDUCE_UNITS = 22
+REDUCE_UNITS = (20, 22)
 REDUCE_CHUNKS = ((0, 2), (2, 6), (6, 8))
 GATHER_CHUNKS = ((0, 4), (4, 6), (6, 8))
 MIX_CHUNKS = ((0, 4), (4, 8))
@@ -713,7 +713,7 @@
             return pltpu.CompilerParams(vmem_limit_bytes=VMEM_LIMIT, collective_id=number, has_side_effects=True)
 
         def across(f, layer, source):
-            first, early = layer == 0, REDUCE_UNITS
+            first, early = layer == 0, REDUCE_UNITS[layer]
             late = groups * units - early
             s, p = pl.pallas_call(
                 functools.partial(reduce_kernel, first), grid=(slots + early,),

time: 698 us -> 691 us (0.990)
  Pallas kernels: 693 us -> 686 us
where the time goes in v11:
time: 691 us; the launch traced here: 688 us
  Pallas kernels  686 us (99%)
    pallas_call x2, Pallas kernels, across(): pl.pallas_call(functools.partial(reduce_kernel, first), grid=(slots + ear...  188 us
    pallas_call x2, Pallas kernels, across(): pl.pallas_call(functools.partial(gather_kernel, first, layer), grid=(late...  188 us
    pallas_call x1, Pallas kernels, local_layers(): pl.pallas_call(functools.partial(layer_kernel, FIRST_UNIT, True), grid=gr...  116 us
    pallas_call x1, Pallas kernels, local_layers(): pl.pallas_call(functools.partial(layer_kernel, LAST_UNIT, False), grid=(g...  112 us
    pallas_call x1, Pallas kernels, local_layers(): pl.pallas_call(functools.partial(forward_kernel, FORWARD_UNIT), grid=(gro...  79.5 us

profile of v11, /device:TPU:0, one launch (start us, length us, event | category | flops | bytes accessed | tf_op | source)
XLA Modules:
  0.0 687.5 jit_solution(3597875781720135906)
XLA Ops:
  0.0 1.3 copy.18.w_ref
  1.3 2.5 point_table.1.w_ref
  3.8 79.5 %forward.1 = f32[2,20,256,384]{3,2,1,0:T(8,128)} custom-call(f32[16,32,20,40,48]{4,3,2,1,0:T(8,128)} %bitcast.x_ref, bf16[8,64,192]{2,1,0:T(8,128)(2,1)} %constant.20.clone.t0.refs_7_, bf16[8,192,256]{2,1,0:T(8,128)(2,1)} %constant.21.clone.t1.refs_8_, bf16[8,192,256]{2,1,0:T(8,128)(2,1)} %constant.22.clone.t2.refs_9_), custom_call_target="tpu_custom_call" | custom-call | tf_op jit(solution)/shard_map/forward/pallas_call | solution.py:696
  83.3 101.5 %reduce.2 = (f32[2,8,2,16,960]{4,3,2,1,0:T(8,128)}, f32[2,32,20,40,384]{4,3,2,1,0:T(8,128)}) custom-call(bf16[8,3,256,256]{3,2,1,0:T(8,128)(2,1)} %constant.28.clone.m_hbm, f32[2,20,8,2,2,8,384]{6,5,4,3,2,1,0:T(8,128)} %bitcast.12, f32[16,32,20,40,48]{4,3,2,1,0:T(8,128)} %bitcast.x_ref, bf16[2,5,160,256]{3,2,1,0:T(8,128)(2,1)} %point_table.1.w_ref), custom_call_target="tpu_custom_call" | custom-call | tf_op jit(solution)/shard_map/reduce/pallas_call | solution.py:718
  184.8 96.6 %gather.2 = (bf16[2,3,20,8,2,2,8,384]{7,6,5,4,3,2,1,0:T(8,128)(2,1)}, f32[2,32,20,40,384]{4,3,2,1,0:T(8,128)}) custom-call(bf16[8,3,256,256]{3,2,1,0:T(8,128)(2,1)} %constant.29.clone.m_hbm, f32[2,8,2,16,960]{4,3,2,1,0:T(8,128)} %get-tuple-element.15.s_ref, f32[2,16,16,20,8,20]{5,4,3,2,1,0:T(8,128)} %bitcast.8, ...), custom_call_target="tpu_custom_call", output_to_operand_aliasing={{1}: (6, {})} | custom-call | tf_op jit(solution)/shard_map/gather/pallas_call | solution.py:729
  281.4 116.5 %layer_first.1 = (f32[2,32,20,40,384]{4,3,2,1,0:T(8,128)}, f32[2,20,256,384]{3,2,1,0:T(8,128)}) custom-call(f32[2,32,20,40,384]{4,3,2,1,0:T(8,128)} %get-tuple-element.17.refs_0_, bf16[2,3,20,256,384]{4,3,2,1,0:T(8,128)(2,1)} %bitcast.14, bf16[8,96,192]{2,1,0:T(8,128)(2,1)} %constant.23.clone.refs_2_, bf16[8,128,192]{2,1,0:T(8,128)(2,1)} %constant.24.clone.refs_3_, ...), custom_call_target="tpu_custom_call" | custom-call | tf_op jit(solution)/shard_map/layer_first/pallas_call | solution.py:746
  397.9 86.5 %reduce.3 = (f32[2,8,2,16,960]{4,3,2,1,0:T(8,128)}, f32[2,32,20,40,384]{4,3,2,1,0:T(8,128)}) custom-call(bf16[8,3,256,256]{3,2,1,0:T(8,128)(2,1)} %constant.28.clone.m_hbm, f32[2,20,8,2,2,8,384]{6,5,4,3,2,1,0:T(8,128)} %bitcast.15, f32[2,32,20,40,384]{4,3,2,1,0:T(8,128)} %get-tuple-element.20.x_ref, bf16[2,5,160,256]{3,2,1,0:T(8,128)(2,1)} %point_table.1.w_ref), custom_call_target="tpu_custom_call" | custom-call | tf_op jit(solution)/shard_map/reduce/pallas_call | solution.py:718
  484.4 91.0 %gather.3 = (bf16[2,3,20,8,2,2,8,384]{7,6,5,4,3,2,1,0:T(8,128)(2,1)}, f32[2,32,20,40,384]{4,3,2,1,0:T(8,128)}) custom-call(bf16[8,3,256,256]{3,2,1,0:T(8,128)(2,1)} %constant.29.clone.m_hbm, f32[2,8,2,16,960]{4,3,2,1,0:T(8,128)} %get-tuple-element.21.s_ref, f32[2,16,16,20,8,20]{5,4,3,2,1,0:T(8,128)} %bitcast.9, ...), custom_call_target="tpu_custom_call", output_to_operand_aliasing={{1}: (6, {})} | custom-call | tf_op jit(solution)/shard_map/gather/pallas_call | solution.py:729
  575.4 112.1 %layer_last.1 = f32[16,32,20,40,48]{4,3,2,1,0:T(8,128)} custom-call(f32[2,32,20,40,384]{4,3,2,1,0:T(8,128)} %get-tuple-element.23.refs_0_, bf16[2,3,20,256,384]{4,3,2,1,0:T(8,128)(2,1)} %bitcast.13, bf16[8,96,192]{2,1,0:T(8,128)(2,1)} %constant.23.clone.refs_2_, bf16[8,128,192]{2,1,0:T(8,128)(2,1)} %constant.24.clone.refs_3_, ...), custom_call_target="tpu_custom_call" | custom-call | tf_op jit(solution)/shard_map/layer_last/pallas_call | solution.py:753
